TPU v7x, 32 devices: a whole 2x2x4 slice. The times are simulated.
32 devices in a mesh: seg: 4 (over z), cp: 8 (over y, x, core).
Axes of the slice: x: 2, y: 2, z: 4, core: 2. Of those that a mesh axis runs over, the one named last changes fastest.
Arguments:
- mixed_qkv: bfloat16 [4096, 8192], P(('seg', 'cp')), may hold values from -6 to 6
- gate_z: bfloat16 [4096, 4096], P(('seg', 'cp')), may hold values from -6 to 6
- gate_logits: bfloat16 [4096, 64], P(('seg', 'cp')), may hold values from -16 to 4
- block_table: int32 [4, 16], P('seg'), may hold values from 0 to 15, as said below
- conv_weight: float32 [4, 8192], replicated, may hold values from -3 to 3
- a_log: float32 [32], replicated, may hold values from -0.7 to 0.7
- dt_bias: float32 [32], replicated, may hold values from -0.5 to 0.5
- norm_gain: float32 [128], replicated, may hold values from 0.25 to 1.75
Outputs:
- mixed_out: bfloat16 [4096, 4096], P(('seg', 'cp'))
Inputs may be any that keep to these rules, and one draw needn't show every extreme that they name: Each row of block_table is a permutation of the numbers 0 to 15; its entries at even positions are below 8, those at odd positions are 8 or more.
All inputs are finite; a program needn't handle non-finite values.
Results may differ from a plain program's by a relative error of at most 0.001.
Values may be sent and summed in bfloat16 or wider, within the bound.
No kernel may reach another device: no remote copies, remote signals or barrier semaphores. Data moves between devices by JAX's collectives and lax.ppermute only.
A program may use at most 128 MiB of HBM per device.

v0:
```python
import functools

import jax
import jax.numpy as jnp
from jax import lax
from jax.experimental import pallas as pl
from jax.experimental.pallas import tpu as pltpu
from jax.sharding import PartitionSpec as P

VALUE_HEADS = 32
KEY_HEADS = 16
HEAD_DIM = 128
CONV = 4
BLOCK = 128
GROUP = VALUE_HEADS // KEY_HEADS
LEVELS = (2, 4, 8, 16, 32, 64)

F32 = jnp.float32
BF16 = jnp.bfloat16
highest = lax.Precision.HIGHEST


def dot(a, b):
    return jnp.dot(a, b, preferred_element_type=F32)


def split(x):
    high = x.astype(BF16)
    low = (x - high.astype(F32)).astype(BF16)
    return high, low


def beside(*parts):
    return jnp.concatenate(parts, axis=1)


def below(*parts):
    return jnp.concatenate(parts, axis=0)


def narrow_product(a, b):
    row = beside(b[0], b[1])
    both = dot(beside(a[0], a[1]), below(row, row))
    half = row.shape[1] // 2
    return both[:, :half] + both[:, half:]


def wide_product(a, b):
    return dot(beside(a[0], a[1]), below(b[0], b[0])) + dot(a[0], b[1])


def silu(v):
    return v / (1.0 + jnp.exp(-v))


def softplus(v):
    e = jnp.exp(-jnp.abs(v))
    s = e / (2.0 + e)
    t = s * s
    series = 1.0 / 19.0
    for odd in (17, 15, 13, 11, 9, 7, 5, 3, 1):
        series = series * t + 1.0 / odd
    return jnp.maximum(v, 0.0) + 2.0 * s * series


def local_kernel(
    dims,
    order_ref,
    recv_ref,
    tail_ref,
    weight_ref,
    rate_ref,
    out_ref,
    reach_ref,
    final_ref,
    rows_ref,
    mask_ref,
    state_ref,
):
    key_heads, heads, count, per_step = dims
    tiles = 2 * key_heads + heads
    share = heads // key_heads
    piece_rows = BLOCK // 2
    gate_row = tiles * BLOCK

    row_index = lax.broadcasted_iota(jnp.int32, (BLOCK, BLOCK), 0)
    col_index = lax.broadcasted_iota(jnp.int32, (BLOCK, BLOCK), 1)
    differ = row_index ^ col_index
    for place, size in enumerate(LEVELS):
        inside = (differ >= size) & (differ < 2 * size)
        mask_ref[place] = jnp.where(inside, 1.0, 0.0).astype(BF16)
    eye = jnp.where(row_index == col_index, 1.0, 0.0).astype(F32)
    for h in range(heads):
        state_ref[h] = beside(jnp.zeros((HEAD_DIM, HEAD_DIM), F32), eye)

    def step(index, carry):
        blocks = [index * per_step + b for b in range(per_step)]
        keys, queries, values = {}, {}, {}
        for b, n in enumerate(blocks):
            for tile in range(tiles):
                slot = b * tiles + tile
                before = jnp.maximum(2 * n - 1, 0)
                place = order_ref[before]
                start = tile * BLOCK + (place % 2) * piece_rows + piece_rows - 16
                start = pl.multiple_of(start, 16)
                old = recv_ref[place // 2, pl.ds(start, 16), :]
                old = jnp.where(n == 0, tail_ref[tile].astype(F32), old.astype(F32))
                rows_ref[slot, 0:8, :] = old[8:16]
                for half in range(2):
                    place = order_ref[2 * n + half]
                    start = tile * BLOCK + (place % 2) * piece_rows
                    start = pl.multiple_of(start, piece_rows)
                    fresh = recv_ref[place // 2, pl.ds(start, piece_rows), :]
                    rows_ref[slot, 8 + half * piece_rows : 8 + (half + 1) * piece_rows, :] = (
                        fresh.astype(F32)
                    )
                summed = None
                for offset in range(CONV):
                    tap = weight_ref[tile, offset : offset + 1, :]
                    shifted = rows_ref[slot, 8 - CONV + 1 + offset : 8 - CONV + 1 + offset + BLOCK, :]
                    term = tap * shifted
                    summed = term if summed is None else summed + term
                active = silu(summed)
                if tile < 2 * key_heads:
                    norm = lax.rsqrt(jnp.sum(active * active, axis=-1, keepdims=True) + 1e-06)
                    if tile < key_heads:
                        queries[b, tile] = active * (norm * HEAD_DIM ** (-0.5))
                    else:
                        keys[b, tile - key_heads] = active * norm
                else:
                    values[b, tile - 2 * key_heads] = active

        lane = lax.broadcasted_iota(jnp.int32, (16, BLOCK), 1)
        upper = jnp.where(row_index <= col_index, 1.0, 0.0).astype(BF16)
        cum_rows, beta_rows, end_rows, cum_cols = {}, {}, {}, {}
        for b, n in enumerate(blocks):
            picked = []
            for half in range(2):
                place = order_ref[2 * n + half]
                start = pl.multiple_of(gate_row + (place % 2) * 16, 16)
                picked.append(recv_ref[place // 2, pl.ds(start, 16), :].astype(F32))
            logits = jnp.where(lane < piece_rows, picked[0], picked[1])
            beta_rows[b] = 1.0 / (1.0 + jnp.exp(-logits[0:8]))
            decay = -jnp.exp(rate_ref[0]) * softplus(logits[8:16] + rate_ref[1])
            high, rest = split(decay)
            middle_full = decay - high.astype(F32)
            middle = middle_full.astype(BF16)
            low = (middle_full - middle.astype(F32)).astype(BF16)
            stacked = below(high.astype(F32), middle.astype(F32), low.astype(F32))
            stacked = below(stacked, jnp.zeros((8, BLOCK), F32)).astype(BF16)
            sums = dot(stacked, upper)
            cum = sums[0:8] + sums[8:16] + sums[16:24]
            cum_rows[b] = cum
            end_rows[b] = jnp.broadcast_to(cum[:, BLOCK - 1 :], (8, BLOCK))
            padded = below(cum, jnp.zeros((BLOCK - 8, BLOCK), F32))
            cum_cols[b] = padded.T

        strict = row_index > col_index
        inclusive = row_index >= col_index
        flipped, grams = {}, {}
        for b in range(per_step):
            for g in range(key_heads):
                turned = keys[b, g].T
                flipped[b, g] = turned
                k_high, k_low = split(keys[b, g])
                q_high, q_low = split(queries[b, g])
                t_high, t_low = split(turned)
                row = beside(t_high, t_low)
                left = below(beside(k_high, k_low), beside(q_high, q_low))
                both = dot(left, below(row, row))
                gram = both[:, :BLOCK] + both[:, BLOCK:]
                grams[b, g] = (gram[:BLOCK], gram[BLOCK:])

        units = [(b, h) for b in range(per_step) for h in range(heads)]
        system, inverse, attend, grow = {}, {}, {}, {}
        for b, h in units:
            g = h // share
            column = jnp.broadcast_to(cum_cols[b][:, h : h + 1], (BLOCK, BLOCK))
            line = cum_rows[b][h : h + 1]
            decay = jnp.exp(jnp.where(inclusive, column - line, 0.0))
            grow[b, h] = jnp.exp(column)
            scaled = decay * beta_rows[b][h : h + 1]
            gram_key, gram_query = grams[b, g]
            attend[b, h] = split(jnp.where(inclusive, gram_query * scaled, 0.0))
            lower = jnp.where(strict, gram_key * scaled, 0.0)
            system[b, h] = split(lower)
            inverse[b, h] = eye - jnp.where(differ == 1, lower, 0.0)

        for place, size in enumerate(LEVELS):
            mask = mask_ref[place]
            halves, cross = {}, {}
            for u in units:
                halves[u] = split(inverse[u])
                parts = (system[u][0] * mask, system[u][1] * mask)
                cross[u] = split(narrow_product(parts, halves[u]))
            for u in units:
                inverse[u] = inverse[u] - narrow_product(halves[u], cross[u])

        solved = {}
        for b, h in units:
            g = h // share
            right = split(beside(values[b, h], keys[b, g] * grow[b, h]))
            solved[b, h] = wide_product(split(inverse[b, h]), right)

        for b, n in enumerate(blocks):
            for h in range(heads):
                g = h // share
                ux = solved[b, h][:, :HEAD_DIM]
                px = split(solved[b, h][:, HEAD_DIM:])
                state = state_ref[h]
                state_parts = split(state)
                fresh = beside(ux, jnp.zeros((BLOCK, HEAD_DIM), F32)) - wide_product(px, state_parts)
                fresh_parts = split(fresh)
                end = end_rows[b][h : h + 1]
                line = cum_rows[b][h : h + 1]
                weight = jnp.exp(end - line) * beta_rows[b][h : h + 1]
                key_parts = split(flipped[b, g] * weight)
                keep = jnp.exp(end)
                state_ref[h] = state * beside(keep, keep) + wide_product(key_parts, fresh_parts)
                q_high, q_low = split(queries[b, g] * grow[b, h])
                a_high, a_low = attend[b, h]
                right_high = below(state_parts[0], fresh_parts[0])
                right_low = below(state_parts[1], fresh_parts[1])
                left_high = beside(q_high, a_high)
                left_low = beside(q_low, a_low)
                both = dot(left_high, right_high) + dot(left_low, right_high) + dot(left_high, right_low)
                at = pl.multiple_of(n * BLOCK, BLOCK)
                out_ref[h, pl.ds(at, BLOCK), :] = both[:, :HEAD_DIM]
                r_high, r_low = split(both[:, HEAD_DIM:])
                reach_ref[h, pl.ds(at, BLOCK), :] = beside(r_high, r_low)
        return carry

    lax.fori_loop(0, count // per_step, step, 0)
    for h in range(heads):
        final_ref[h] = state_ref[h]


def finish_kernel(dims, order_ref, core_ref, reach_ref, incoming_ref, gate_ref, gain_ref, out_ref):
    heads, count = dims
    piece_rows = BLOCK // 2

    def step(n, carry):
        at = pl.multiple_of(n * BLOCK, BLOCK)
        for h in range(heads):
            high, low = split(incoming_ref[h])
            row = beside(high, low)
            both = dot(reach_ref[h, pl.ds(at, BLOCK), :], below(row, row))
            core = core_ref[h, pl.ds(at, BLOCK), :] + both[:, :HEAD_DIM] + both[:, HEAD_DIM:]
            scale = lax.rsqrt(jnp.mean(core * core, axis=-1, keepdims=True) + 1e-06)
            gates = []
            for half in range(2):
                place = order_ref[2 * n + half]
                start = pl.multiple_of(h * BLOCK + (place % 2) * piece_rows, piece_rows)
                gates.append(gate_ref[place // 2, pl.ds(start, piece_rows), :].astype(F32))
            gate = below(*gates)
            result = core * scale * gain_ref[...] * silu(gate)
            out_ref[n, h * BLOCK : (h + 1) * BLOCK, :] = result.astype(BF16)
        return carry

    lax.fori_loop(0, count, step, 0)


def passed_along(value, axis, by):
    length = lax.axis_size(axis)
    pairs = [(i, i + by) for i in range(length) if 0 <= i + by < length]
    return lax.ppermute(value, axis, pairs)


def per_device(mixed_qkv, gate_z, gate_logits, block_table, conv_weight, a_log, dt_bias, norm_gain):
    cp_count = lax.axis_size("cp")
    seg_count = lax.axis_size("seg")
    cp_place = lax.axis_index("cp")
    rows = mixed_qkv.shape[0]
    heads = VALUE_HEADS // cp_count
    key_heads = max(1, heads // GROUP)
    copies = cp_count * key_heads // KEY_HEADS
    tiles = 2 * key_heads + heads
    key_width = KEY_HEADS * HEAD_DIM
    count = cp_count * rows // BLOCK
    per_step = 2 if count % 2 == 0 else 1
    order = jnp.argsort(block_table[0]).astype(jnp.int32)

    def key_tiles(array, lead):
        shaped = array.reshape(lead, KEY_HEADS, HEAD_DIM)
        if copies > 1:
            shaped = jnp.repeat(shaped, copies, axis=1)
        return shaped.reshape(lead, cp_count, key_heads, HEAD_DIM)

    def value_tiles(array, lead):
        return array.reshape(lead, cp_count, heads, HEAD_DIM)

    def by_tiles(array):
        lead = array.shape[0]
        return (
            key_tiles(array[:, :key_width], lead),
            key_tiles(array[:, key_width : 2 * key_width], lead),
            value_tiles(array[:, 2 * key_width :], lead),
        )

    def to_send(shaped):
        return shaped.transpose(1, 2, 0, 3).reshape(cp_count, -1, HEAD_DIM)

    half_rows = rows // 2
    gates = gate_logits.T.reshape(2, cp_count, heads, 2, half_rows).transpose(1, 3, 0, 2, 4)
    gates = jnp.pad(gates, ((0, 0), (0, 0), (0, 0), (0, 8 - heads), (0, 0)))
    gates = jnp.concatenate([gates, gates], axis=-1).reshape(cp_count, 32, 2 * half_rows)
    sent = jnp.concatenate([to_send(part) for part in by_tiles(mixed_qkv)] + [gates], axis=1)
    received = lax.all_to_all(sent, "cp", split_axis=0, concat_axis=0, tiled=True)
    gate_seq = lax.all_to_all(
        to_send(value_tiles(gate_z, rows)), "cp", split_axis=0, concat_axis=0, tiled=True
    )

    last = order[2 * cp_count - 1]
    last_rows = lax.dynamic_index_in_dim(received, last // 2, 0, keepdims=False)
    tail = last_rows[: tiles * BLOCK].reshape(tiles, BLOCK, HEAD_DIM)
    tail = lax.dynamic_slice_in_dim(tail, (last % 2) * half_rows + half_rows - 16, 16, 1)
    tail = passed_along(tail, "seg", 1)

    weights = jnp.concatenate(
        [
            lax.dynamic_index_in_dim(part, cp_place, 1, keepdims=False)
            for part in by_tiles(conv_weight)
        ],
        axis=1,
    ).transpose(1, 0, 2)
    head_log = lax.dynamic_slice_in_dim(a_log, cp_place * heads, heads, 0)
    head_bias = lax.dynamic_slice_in_dim(dt_bias, cp_place * heads, heads, 0)
    rates = jnp.pad(jnp.stack([head_log, head_bias]), ((0, 0), (0, 8 - heads)))
    rates = jnp.broadcast_to(rates[:, :, None], (2, 8, BLOCK))

    vmem = pl.BlockSpec(memory_space=pltpu.VMEM)
    smem = pl.BlockSpec(memory_space=pltpu.SMEM)
    core, reach, final = pl.pallas_call(
        functools.partial(local_kernel, (key_heads, heads, count, per_step)),
        out_shape=(
            jax.ShapeDtypeStruct((heads, count * BLOCK, HEAD_DIM), F32),
            jax.ShapeDtypeStruct((heads, count * BLOCK, 2 * HEAD_DIM), BF16),
            jax.ShapeDtypeStruct((heads, HEAD_DIM, 2 * HEAD_DIM), F32),
        ),
        in_specs=[smem, vmem, vmem, vmem, vmem],
        out_specs=(vmem, vmem, vmem),
        scratch_shapes=[
            pltpu.VMEM((per_step * tiles, 8 + BLOCK, HEAD_DIM), F32),
            pltpu.VMEM((len(LEVELS), BLOCK, BLOCK), BF16),
            pltpu.VMEM((heads, HEAD_DIM, 2 * HEAD_DIM), F32),
        ],
        cost_estimate=pl.CostEstimate(
            flops=int(2e10), bytes_accessed=int(8e6), transcendentals=int(1e6)
        ),
        name="local",
    )(order, received, tail, weights, rates)

    shift = final[:, :, :HEAD_DIM]
    reach_map = final[:, :, HEAD_DIM:]
    incoming = jnp.zeros((heads, HEAD_DIM, HEAD_DIM), F32)
    for rounds in range(seg_count - 1):
        advanced = shift
        if rounds:
            advanced = shift + jnp.einsum("hij,hjk->hik", reach_map, incoming, precision=highest)
        incoming = passed_along(advanced, "seg", 1)

    blocks = pl.pallas_call(
        functools.partial(finish_kernel, (heads, count)),
        out_shape=jax.ShapeDtypeStruct((count, heads * BLOCK, HEAD_DIM), BF16),
        in_specs=[smem, vmem, vmem, vmem, vmem, vmem],
        out_specs=vmem,
        cost_estimate=pl.CostEstimate(
            flops=int(2e9), bytes_accessed=int(6e6), transcendentals=int(1e6)
        ),
        name="finish",
    )(order, core, reach, incoming, gate_seq, norm_gain.reshape(1, HEAD_DIM))
    swapped = lax.all_to_all(blocks, "cp", split_axis=0, concat_axis=0, tiled=True)
    swapped = swapped.reshape(cp_count, heads, rows, HEAD_DIM)
    return swapped.transpose(2, 0, 1, 3).reshape(rows, VALUE_HEADS * HEAD_DIM)


def solution(mesh):
    return jax.shard_map(
        per_device,
        mesh=mesh,
        in_specs=(
            P(("seg", "cp"), None),
            P(("seg", "cp"), None),
            P(("seg", "cp"), None),
            P("seg", None),
            P(),
            P(),
            P(),
            P(),
        ),
        out_specs=P(("seg", "cp"), None),
        check_vma=False,
    )
```

profile of v0, /device:TPU:0, one launch (start us, length us, event | category | flops | bytes accessed | tf_op | source)
XLA Modules:
  0.0 130.0 jit_solution(8418673926092601781)
XLA Ops:
  0.0 1.3 fusion.2
  1.3 0.0 slice-start
  1.3 0.4 reshape_reshape.12
  1.7 0.1 copy.9
  1.8 0.4 reshape_reshape.13
  2.2 0.1 copy.10
  2.3 0.2 slice-done
  2.5 0.0 copy-start.5
  2.5 0.7 reshape.44
  3.3 0.4 copy.11
  3.7 0.0 copy-done.5
  3.7 0.1 reshape.46
  3.8 0.1 pad_maximum_fusion.1
  3.9 1.5 %pad_maximum_fusion = bf16[8,1056,128]{2,1,0:T(8,128)(2,1)} fusion(bf16[8,32,128]{2,1,0:T(8,128)(2,1)S(1)} %bitcast.46, bf16[8,512,128]{2,1,0:T(8,128)(2,1)S(1)} %bitcast.42, bf16[8,256,128]{2,1,0:T(8,128)(2,1)S(1)} %bitcast.44, bf16[8,256,128]{2,1,0:T(8,128)(2,1)S(1)} %bitcast.43), kind=kLoop, calls=%fused_computation | loop fusion | flops 8650752 | bytes 4325376 | tf_op jit(solution)/shard_map/concatenate | solution.py:307
  5.4 0.0 copy-start.10
  5.4 0.0 copy-start.6
  5.4 0.0 copy-start.7
  5.4 0.0 slice-start.1
  5.4 0.0 copy-start.4
  5.4 5.3 %all-to-all-start = ((bf16[8,1056,128]{2,1,0:T(8,128)(2,1)}), bf16[8,1056,128]{2,1,0:T(8,128)(2,1)S(1)}, u32[]{:S(2)}, u32[]{:S(2)}) async-start(bf16[8,1056,128]{2,1,0:T(8,128)(2,1)} %pad_maximum_fusion), calls=%async_computation | async-start | bytes 4325376 | tf_op jit(solution)/shard_map/all_to_all | solution.py:308
  10.8 0.0 copy-done.10
  10.8 1.2 sort.17
  12.0 0.0 copy-start.11
  12.0 0.6 slice.34
  15.2 0.0 copy-done.6
  15.3 0.0 copy-done.7
  15.3 0.1 dynamic-slice_bitcast_fusion.3
  15.3 0.0 slice-done.1
  15.3 0.0 copy-done.4
  15.4 0.6 maximum_bitcast_fusion.weight_ref
  16.0 22.1 %all-to-all-done.recv_ref = bf16[8,1056,128]{2,1,0:T(8,128)(2,1)S(1)} async-done(((bf16[8,1056,128]{2,1,0:T(8,128)(2,1)}), bf16[8,1056,128]{2,1,0:T(8,128)(2,1)S(1)}, u32[]{:S(2)}, u32[]{:S(2)}) %all-to-all-start) | async-done | bytes 2162720 | tf_op jit(solution)/shard_map/all_to_all | solution.py:308
  38.1 0.0 copy-start
  38.1 3.5 %collective-permute-start = (bf16[8,16,128]{2,1,0:T(8,128)(2,1)S(1)}, bf16[8,16,128]{2,1,0:T(8,128)(2,1)S(1)}, u32[]{:S(2)}, u32[]{:S(2)}) collective-permute-start(bf16[8,16,128]{2,1,0:T(8,128)(2,1)S(1)} %constant_dynamic-slice_fusion), channel_id=1, source_target_pairs={{0,8},{8,16},{16,24},{1,9},{9,17},{17,25},{2,10},{10,18},{18,26},{... | collective-permute-start | bytes 98312 | tf_op jit(solution)/shard_map/ppermute | solution.py:266
  41.6 1.6 %collective-permute-done.tail_ref = bf16[8,16,128]{2,1,0:T(8,128)(2,1)S(1)} collective-permute-done((bf16[8,16,128]{2,1,0:T(8,128)(2,1)S(1)}, bf16[8,16,128]{2,1,0:T(8,128)(2,1)S(1)}, u32[]{:S(2)}, u32[]{:S(2)}) %collective-permute-start) | collective-permute-done | bytes 32800 | tf_op jit(solution)/shard_map/ppermute | solution.py:266
  43.2 0.0 copy-start.9
  43.2 0.7 broadcast_in_dim.2.rate_ref
  43.9 0.0 copy-done.11
  43.9 0.0 copy-done
  43.9 0.0 copy-done.9
  43.9 26.9 %local.1 = (f32[4,1024,128]{2,1,0:T(8,128)}, bf16[4,1024,256]{2,1,0:T(8,128)(2,1)}, f32[4,128,256]{2,1,0:T(8,128)}) custom-call(s32[16]{0:T(128)} %copy-done.11, bf16[8,1056,128]{2,1,0:T(8,128)(2,1)} %copy-done, bf16[8,16,128]{2,1,0:T(8,128)(2,1)} %copy-done.9, f32[8,4,128]{2,1,0:T(4,128)} %maximum_bitcast_fusion.weight_ref, ...), custom_call_target="tpu_custom_call" | custom-call | flops 20000000000 | bytes 8000000 | tf_op jit(solution)/shard_map/local/pallas_call | solution.py:333
  70.8 1.0 slice.39
  71.7 4.2 %collective-permute-start.1 = (f32[4,128,128]{2,1,0:T(8,128)S(1)}, f32[4,128,128]{2,1,0:T(8,128)S(1)}, u32[]{:S(2)}, u32[]{:S(2)}) collective-permute-start(f32[4,128,128]{2,1,0:T(8,128)S(1)} %slice.39), channel_id=1, source_target_pairs={{0,8},{8,16},{16,24},{1,9},{9,17},{17,25},{2,10},{10,18},{18,26},{... | collective-permute-start | bytes 786440 | tf_op jit(solution)/shard_map/ppermute | solution.py:266
  76.0 0.0 copy-done.2
  76.0 0.8 reshape.50
  76.7 0.0 copy-start.1
  76.7 1.4 %copy.16 = bf16[128,8,4,128]{3,0,2,1:T(8,128)(2,1)} copy(bf16[128,8,4,128]{3,2,1,0:T(4,128)(2,1)S(1)} %reshape.50) | data formatting | bytes 2097152 | tf_op jit(solution)/shard_map/reshape | solution.py:290
  78.1 3.6 %all-to-all-start.1 = ((bf16[8,512,128]{2,1,0:T(8,128)(2,1)}), bf16[8,512,128]{2,1,0:T(8,128)(2,1)S(1)}, u32[]{:S(2)}, u32[]{:S(2)}) async-start(bf16[8,512,128]{2,1,0:T(8,128)(2,1)} %bitcast.22), calls=%async_computation.1 | async-start | bytes 2097152 | tf_op jit(solution)/shard_map/all_to_all | solution.py:309
  81.7 0.0 collective-permute-done.1
  81.7 0.0 copy-done.1
  81.7 0.4 convolution_add_fusion.1
  82.1 3.5 %collective-permute-start.2 = (f32[4,128,128]{2,1,0:T(8,128)S(1)}, f32[4,128,128]{2,1,0:T(8,128)S(1)}, u32[]{:S(2)}, u32[]{:S(2)}) collective-permute-start(f32[4,128,128]{2,1,0:T(8,128)S(1)} %convolution_add_fusion.1), channel_id=1, source_target_pairs={{0,8},{8,16},{16,24},{1,9},{9,17},{17,25},{2,10},{10,18},{18,26},{... | collective-permute-start | bytes 786440 | tf_op jit(solution)/shard_map/ppermute | solution.py:266
  85.6 6.1 %collective-permute-done.2 = f32[4,128,128]{2,1,0:T(8,128)S(1)} collective-permute-done((f32[4,128,128]{2,1,0:T(8,128)S(1)}, f32[4,128,128]{2,1,0:T(8,128)S(1)}, u32[]{:S(2)}, u32[]{:S(2)}) %collective-permute-start.2) | collective-permute-done | bytes 262176 | tf_op jit(solution)/shard_map/ppermute | solution.py:266
  91.7 0.4 convolution_add_fusion
  92.1 4.4 %collective-permute-start.3 = (f32[4,128,128]{2,1,0:T(8,128)S(1)}, f32[4,128,128]{2,1,0:T(8,128)S(1)}, u32[]{:S(2)}, u32[]{:S(2)}) collective-permute-start(f32[4,128,128]{2,1,0:T(8,128)S(1)} %convolution_add_fusion), channel_id=1, source_target_pairs={{0,8},{8,16},{16,24},{1,9},{9,17},{17,25},{2,10},{10,18},{18,26},{... | collective-permute-start | bytes 786440 | tf_op jit(solution)/shard_map/ppermute | solution.py:266
  96.5 0.5 all-to-all-done.1.gate_ref
  97.0 0.0 copy-start.3
  97.0 4.7 %collective-permute-done.3.incoming_ref = f32[4,128,128]{2,1,0:T(8,128)S(1)} collective-permute-done((f32[4,128,128]{2,1,0:T(8,128)S(1)}, f32[4,128,128]{2,1,0:T(8,128)S(1)}, u32[]{:S(2)}, u32[]{:S(2)}) %collective-permute-start.3) | collective-permute-done | bytes 262176 | tf_op jit(solution)/shard_map/ppermute | solution.py:266
  101.8 0.0 copy-start.8
  101.8 0.0 copy-done.3
  101.8 0.7 copy-done.8
  102.5 6.2 %finish.1 = bf16[8,512,128]{2,1,0:T(8,128)(2,1)} custom-call(s32[16]{0:T(128)} %copy-done.11, f32[4,1024,128]{2,1,0:T(8,128)} %get-tuple-element.10.core_ref, bf16[4,1024,256]{2,1,0:T(8,128)(2,1)} %get-tuple-element.11.reach_ref, f32[4,128,128]{2,1,0:T(8,128)} %copy-done.8, bf16[8,512,128]{2,1,0:T(8,128)(2,1)} %copy-done.3, f32[1,128]{1,0:T(1,128)} %bitcast.53), custom_call_target="tpu_custom_call" | custom-call | flops 2000000000 | bytes 6000000 | tf_op jit(solution)/shard_map/finish/pallas_call | solution.py:362
  108.7 18.9 %all_to_all.15 = bf16[8,512,128]{2,1,0:T(8,128)(2,1)S(1)} all-to-all(bf16[8,512,128]{2,1,0:T(8,128)(2,1)} %finish.1), channel_id=1, replica_groups=mesh['seg'=4,'cp'=8] {'cp'}, dimensions={0} | all-to-all | bytes 2097152 | tf_op jit(solution)/shard_map/all_to_all | solution.py:372
  127.6 0.8 copy.17
  128.4 1.6 %reshape.54 = bf16[128,4096]{1,0:T(8,128)(2,1)} reshape(bf16[128,8,4,128]{3,2,1,0:T(4,128)(2,1)S(1)} %copy.17) | data formatting | bytes 2097152 | tf_op jit(solution)/shard_map/reshape | solution.py:374
  (10 shorter events, 0.1 us)
Async XLA Ops:
  1.3 1.2 slice-start
  2.5 1.2 copy-start.5
  5.4 5.4 %copy-start.10 = (s32[1,16]{1,0:T(1,128)S(1)}, s32[1,16]{1,0:T(1,128)}, u32[]{:S(2)}) copy-start(s32[1,16]{1,0:T(1,128)} %param.11) | copy-start | bytes 196
  5.4 9.8 %copy-start.6 = (f32[32]{0:T(128)S(1)}, f32[32]{0:T(128)}, u32[]{:S(2)}) copy-start(f32[32]{0:T(128)} %param.14) | copy-start | bytes 388
  5.4 9.8 %copy-start.7 = (f32[32]{0:T(128)S(1)}, f32[32]{0:T(128)}, u32[]{:S(2)}) copy-start(f32[32]{0:T(128)} %param.13) | copy-start | bytes 388
  5.4 9.9 %slice-start.1 = ((f32[4,8192]{1,0:T(4,128)}), f32[4,4096]{1,0:T(4,128)S(1)}, s32[]{:S(2)}) async-start(f32[4,8192]{1,0:T(4,128)} %param.12), calls=%async_computation.4 | async-start | bytes 131072 | tf_op jit(solution)/shard_map/slice | solution.py:297
  5.4 9.9 %copy-start.4 = (f32[4,8192]{1,0:T(4,128)S(1)}, f32[4,8192]{1,0:T(4,128)}, u32[]{:S(2)}) copy-start(f32[4,8192]{1,0:T(4,128)} %param.12) | copy-start | bytes 393220
  5.4 32.7 %all-to-all-start = ((bf16[8,1056,128]{2,1,0:T(8,128)(2,1)}), bf16[8,1056,128]{2,1,0:T(8,128)(2,1)S(1)}, u32[]{:S(2)}, u32[]{:S(2)}) async-start(bf16[8,1056,128]{2,1,0:T(8,128)(2,1)} %pad_maximum_fusion), calls=%async_computation | async-start | bytes 4325376 | tf_op jit(solution)/shard_map/all_to_all | solution.py:308
  12.0 31.8 %copy-start.11 = (s32[16]{0:T(128)}, s32[16]{0:T(128)S(1)}, u32[]{:S(2)}) copy-start(s32[16]{0:T(128)S(1)} %get-tuple-element.9.order_ref) | copy-start | bytes 196
  38.1 5.8 %copy-start = (bf16[8,1056,128]{2,1,0:T(8,128)(2,1)}, bf16[8,1056,128]{2,1,0:T(8,128)(2,1)S(1)}, u32[]{:S(2)}) copy-start(bf16[8,1056,128]{2,1,0:T(8,128)(2,1)S(1)} %all-to-all-done.recv_ref) | copy-start | bytes 6488068
  38.1 5.1 %collective-permute-start = (bf16[8,16,128]{2,1,0:T(8,128)(2,1)S(1)}, bf16[8,16,128]{2,1,0:T(8,128)(2,1)S(1)}, u32[]{:S(2)}, u32[]{:S(2)}) collective-permute-start(bf16[8,16,128]{2,1,0:T(8,128)(2,1)S(1)} %constant_dynamic-slice_fusion), channel_id=1, source_target_pairs={{0,8},{8,16},{16,24},{1,9},{9,17},{17,25},{2,10},{10,18},{18,26},{... | collective-permute-start | bytes 98312 | tf_op jit(solution)/shard_map/ppermute | solution.py:266
  43.2 0.7 copy-start.9
  43.9 32.1 %copy-start.2 = (bf16[128,4096]{1,0:T(8,128)(2,1)S(1)}, bf16[128,4096]{1,0:T(8,128)(2,1)}, u32[]{:S(2)}) copy-start(bf16[128,4096]{1,0:T(8,128)(2,1)} %param.9) | copy-start | bytes 3145732
  71.7 10.0 %collective-permute-start.1 = (f32[4,128,128]{2,1,0:T(8,128)S(1)}, f32[4,128,128]{2,1,0:T(8,128)S(1)}, u32[]{:S(2)}, u32[]{:S(2)}) collective-permute-start(f32[4,128,128]{2,1,0:T(8,128)S(1)} %slice.39), channel_id=1, source_target_pairs={{0,8},{8,16},{16,24},{1,9},{9,17},{17,25},{2,10},{10,18},{18,26},{... | collective-permute-start | bytes 786440 | tf_op jit(solution)/shard_map/ppermute | solution.py:266
  76.7 5.0 %copy-start.1 = (f32[4,128,256]{2,1,0:T(8,128)S(1)}, f32[4,128,256]{2,1,0:T(8,128)}, u32[]{:S(2)}) copy-start(f32[4,128,256]{2,1,0:T(8,128)} %get-tuple-element.12) | copy-start | bytes 1572868
  78.1 18.9 %all-to-all-start.1 = ((bf16[8,512,128]{2,1,0:T(8,128)(2,1)}), bf16[8,512,128]{2,1,0:T(8,128)(2,1)S(1)}, u32[]{:S(2)}, u32[]{:S(2)}) async-start(bf16[8,512,128]{2,1,0:T(8,128)(2,1)} %bitcast.22), calls=%async_computation.1 | async-start | bytes 2097152 | tf_op jit(solution)/shard_map/all_to_all | solution.py:309
  82.1 9.6 %collective-permute-start.2 = (f32[4,128,128]{2,1,0:T(8,128)S(1)}, f32[4,128,128]{2,1,0:T(8,128)S(1)}, u32[]{:S(2)}, u32[]{:S(2)}) collective-permute-start(f32[4,128,128]{2,1,0:T(8,128)S(1)} %convolution_add_fusion.1), channel_id=1, source_target_pairs={{0,8},{8,16},{16,24},{1,9},{9,17},{17,25},{2,10},{10,18},{18,26},{... | collective-permute-start | bytes 786440 | tf_op jit(solution)/shard_map/ppermute | solution.py:266
  92.1 9.6 %collective-permute-start.3 = (f32[4,128,128]{2,1,0:T(8,128)S(1)}, f32[4,128,128]{2,1,0:T(8,128)S(1)}, u32[]{:S(2)}, u32[]{:S(2)}) collective-permute-start(f32[4,128,128]{2,1,0:T(8,128)S(1)} %convolution_add_fusion), channel_id=1, source_target_pairs={{0,8},{8,16},{16,24},{1,9},{9,17},{17,25},{2,10},{10,18},{18,26},{... | collective-permute-start | bytes 786440 | tf_op jit(solution)/shard_map/ppermute | solution.py:266
  97.0 4.8 %copy-start.3 = (bf16[8,512,128]{2,1,0:T(8,128)(2,1)}, bf16[8,512,128]{2,1,0:T(8,128)(2,1)S(1)}, u32[]{:S(2)}) copy-start(bf16[8,512,128]{2,1,0:T(8,128)(2,1)S(1)} %all-to-all-done.1.gate_ref) | copy-start | bytes 3145732
  101.8 0.7 copy-start.8
where the time goes:
time: 131 us; the launch traced here: 130 us
  waiting for transfers between devices  35 us (27%)
  Pallas kernels  33.1 us (25%)
  starting transfers between devices  24.5 us (19%)
  blocking collectives  18.9 us (14%)
  local copies, waits for them, and re-layouts  11.4 us (9%)
  other arithmetic  3.45 us (3%)
  between operations  2.89 us (2%)
    pallas_call x1, Pallas kernels, per_device(): pl.pallas_call(functools.partial(local_kernel, (key_heads, heads, count,...  26.9 us
    all_to_all x1, waiting for transfers between devices, per_device(): lax.all_to_all(sent, 'cp', split_axis=0, concat_axis=0, tiled=True)  22.1 us
    all_to_all x1, blocking collectives, per_device(): lax.all_to_all(blocks, 'cp', split_axis=0, concat_axis=0, tiled=True)  18.9 us
    ppermute x4, starting transfers between devices, passed_along(): return lax.ppermute(value, axis, pairs)  15.6 us
    ppermute x4, waiting for transfers between devices, passed_along(): return lax.ppermute(value, axis, pairs)  12.4 us
    pallas_call x1, Pallas kernels, per_device(): pl.pallas_call(functools.partial(finish_kernel, (heads, count)), out_shap...  6.25 us
    all_to_all x1, starting transfers between devices, per_device(): lax.all_to_all(sent, 'cp', split_axis=0, concat_axis=0, tiled=True)  5.34 us
    all_to_all x1, starting transfers between devices, per_device(): lax.all_to_all(to_send(value_tiles(gate_z, rows)), 'cp', split_axis=0, co...  3.56 us
  transfers between devices with their start and end apart: 6, of which 5 were waited for; matrix products, arithmetic and copies ran while one was open for 4% of the time, Pallas kernels for 0%

commit v1 on v0

v1 whole, which is shorter than its diff:
```python
import functools

import jax
import jax.numpy as jnp
from jax import lax
from jax.experimental import pallas as pl
from jax.experimental.pallas import tpu as pltpu
from jax.sharding import PartitionSpec as P

VALUE_HEADS = 32
KEY_HEADS = 16
HEAD_DIM = 128
CONV = 4
BLOCK = 128
GROUP = VALUE_HEADS // KEY_HEADS
LEVELS = (2, 4, 8, 16, 32, 64)

F32 = jnp.float32
BF16 = jnp.bfloat16
highest = lax.Precision.HIGHEST


def dot(a, b):
    return jnp.dot(a, b, preferred_element_type=F32)


def split(x):
    high = x.astype(BF16)
    low = (x - high.astype(F32)).astype(BF16)
    return high, low


def beside(*parts):
    return jnp.concatenate(parts, axis=1)


def below(*parts):
    return jnp.concatenate(parts, axis=0)


def narrow_product(a, b):
    row = beside(b[0], b[1])
    both = dot(beside(a[0], a[1]), below(row, row))
    half = row.shape[1] // 2
    return both[:, :half] + both[:, half:]


def wide_product(a, b):
    return dot(beside(a[0], a[1]), below(b[0], b[0])) + dot(a[0], b[1])


def silu(v):
    return v / (1.0 + jnp.exp(-v))


def softplus(v):
    e = jnp.exp(-jnp.abs(v))
    s = e / (2.0 + e)
    t = s * s
    series = 1.0 / 19.0
    for odd in (17, 15, 13, 11, 9, 7, 5, 3, 1):
        series = series * t + 1.0 / odd
    return jnp.maximum(v, 0.0) + 2.0 * s * series


def local_kernel(
    dims,
    meta_ref,
    recv_ref,
    logit_ref,
    tail_ref,
    weight_ref,
    rate_ref,
    *refs,
):
    group, share, first_block, count, per_step, gate_row, carried = dims
    if carried:
        given_ref, refs = refs[0], refs[1:]
    out_ref, reach_ref, final_ref, rows_ref, mask_ref, state_ref = refs
    tiles = 2 + share
    piece_rows = BLOCK // 2
    is_first = meta_ref[meta_ref.shape[0] - 1]

    row_index = lax.broadcasted_iota(jnp.int32, (BLOCK, BLOCK), 0)
    col_index = lax.broadcasted_iota(jnp.int32, (BLOCK, BLOCK), 1)
    differ = row_index ^ col_index
    for place, size in enumerate(LEVELS):
        inside = (differ >= size) & (differ < 2 * size)
        mask_ref[place] = jnp.where(inside, 1.0, 0.0).astype(BF16)
    eye = jnp.where(row_index == col_index, 1.0, 0.0).astype(F32)
    for h in range(share):
        if carried:
            state_ref[h] = given_ref[h]
        else:
            state_ref[h] = beside(jnp.zeros((HEAD_DIM, HEAD_DIM), F32), eye)

    def step(index, carry):
        spots = [index * per_step + b for b in range(per_step)]
        blocks = [first_block + spot for spot in spots]
        keys, queries, values = {}, {}, {}
        for b, n in enumerate(blocks):
            for tile in range(tiles):
                slot = b * tiles + tile
                before = jnp.maximum(2 * n - 1, 0)
                place = meta_ref[before]
                start = tile * BLOCK + (place % 2) * piece_rows + piece_rows - 16
                start = pl.multiple_of(start, 16)
                old = recv_ref[place // 2, pl.ds(start, 16), :].astype(F32)
                if first_block == 0:
                    lead = tail_ref[tile].astype(F32)
                    lead = jnp.where(is_first == 1, 0.0, lead)
                    old = jnp.where(n == 0, lead, old)
                rows_ref[slot, 0:8, :] = old[8:16]
                for half in range(2):
                    place = meta_ref[2 * n + half]
                    start = tile * BLOCK + (place % 2) * piece_rows
                    start = pl.multiple_of(start, piece_rows)
                    fresh = recv_ref[place // 2, pl.ds(start, piece_rows), :]
                    rows_ref[slot, 8 + half * piece_rows : 8 + (half + 1) * piece_rows, :] = (
                        fresh.astype(F32)
                    )
                summed = None
                for offset in range(CONV):
                    tap = weight_ref[tile, offset : offset + 1, :]
                    begin = 8 - CONV + 1 + offset
                    term = tap * rows_ref[slot, begin : begin + BLOCK, :]
                    summed = term if summed is None else summed + term
                active = silu(summed)
                if tile < 2:
                    norm = lax.rsqrt(jnp.sum(active * active, axis=-1, keepdims=True) + 1e-06)
                    if tile == 0:
                        queries[b] = active * (norm * HEAD_DIM ** (-0.5))
                    else:
                        keys[b] = active * norm
                else:
                    values[b, tile - 2] = active

        lane = lax.broadcasted_iota(jnp.int32, (16, BLOCK), 1)
        upper = jnp.where(row_index <= col_index, 1.0, 0.0).astype(BF16)
        cum_rows, beta_rows, end_rows, cum_cols = {}, {}, {}, {}
        for b, n in enumerate(blocks):
            picked = []
            for half in range(2):
                place = meta_ref[2 * n + half]
                start = pl.multiple_of(gate_row + (place % 2) * 16, 16)
                picked.append(logit_ref[place // 2, pl.ds(start, 16), :].astype(F32))
            logits = jnp.where(lane < piece_rows, picked[0], picked[1])
            beta_rows[b] = 1.0 / (1.0 + jnp.exp(-logits[0:8]))
            decay = -jnp.exp(rate_ref[0]) * softplus(logits[8:16] + rate_ref[1])
            high, rest = split(decay)
            middle_full = decay - high.astype(F32)
            middle = middle_full.astype(BF16)
            low = (middle_full - middle.astype(F32)).astype(BF16)
            stacked = below(high.astype(F32), middle.astype(F32), low.astype(F32))
            stacked = below(stacked, jnp.zeros((8, BLOCK), F32)).astype(BF16)
            sums = dot(stacked, upper)
            cum = sums[0:8] + sums[8:16] + sums[16:24]
            cum_rows[b] = cum
            end_rows[b] = jnp.broadcast_to(cum[:, BLOCK - 1 :], (8, BLOCK))
            padded = below(cum, jnp.zeros((BLOCK - 8, BLOCK), F32))
            cum_cols[b] = padded.T

        strict = row_index > col_index
        inclusive = row_index >= col_index
        flipped, grams = {}, {}
        for b in range(per_step):
            turned = keys[b].T
            flipped[b] = turned
            k_high, k_low = split(keys[b])
            q_high, q_low = split(queries[b])
            t_high, t_low = split(turned)
            row = beside(t_high, t_low)
            left = below(beside(k_high, k_low), beside(q_high, q_low))
            both = dot(left, below(row, row))
            gram = both[:, :BLOCK] + both[:, BLOCK:]
            grams[b] = (gram[:BLOCK], gram[BLOCK:])

        units = [(b, h) for b in range(per_step) for h in range(share)]
        system, inverse, attend, grow = {}, {}, {}, {}
        for b, h in units:
            at = group * share + h
            column = jnp.broadcast_to(cum_cols[b][:, at : at + 1], (BLOCK, BLOCK))
            line = cum_rows[b][at : at + 1]
            decay = jnp.exp(jnp.where(inclusive, column - line, 0.0))
            grow[b, h] = jnp.exp(column)
            scaled = decay * beta_rows[b][at : at + 1]
            gram_key, gram_query = grams[b]
            attend[b, h] = split(jnp.where(inclusive, gram_query * scaled, 0.0))
            lower = jnp.where(strict, gram_key * scaled, 0.0)
            system[b, h] = split(lower)
            inverse[b, h] = eye - jnp.where(differ == 1, lower, 0.0)

        for place, size in enumerate(LEVELS):
            mask = mask_ref[place]
            halves, cross = {}, {}
            for u in units:
                halves[u] = split(inverse[u])
                parts = (system[u][0] * mask, system[u][1] * mask)
                cross[u] = split(narrow_product(parts, halves[u]))
            for u in units:
                inverse[u] = inverse[u] - narrow_product(halves[u], cross[u])

        solved = {}
        for b, h in units:
            right = split(beside(values[b, h], keys[b] * grow[b, h]))
            solved[b, h] = wide_product(split(inverse[b, h]), right)

        for b, spot in enumerate(spots):
            for h in range(share):
                row = group * share + h
                ux = solved[b, h][:, :HEAD_DIM]
                px = split(solved[b, h][:, HEAD_DIM:])
                state = state_ref[h]
                state_parts = split(state)
                fresh = beside(ux, jnp.zeros((BLOCK, HEAD_DIM), F32)) - wide_product(px, state_parts)
                fresh_parts = split(fresh)
                end = end_rows[b][row : row + 1]
                line = cum_rows[b][row : row + 1]
                weight = jnp.exp(end - line) * beta_rows[b][row : row + 1]
                key_parts = split(flipped[b] * weight)
                keep = jnp.exp(end)
                state_ref[h] = state * beside(keep, keep) + wide_product(key_parts, fresh_parts)
                q_high, q_low = split(queries[b] * grow[b, h])
                a_high, a_low = attend[b, h]
                right_high = below(state_parts[0], fresh_parts[0])
                right_low = below(state_parts[1], fresh_parts[1])
                left_high = beside(q_high, a_high)
                left_low = beside(q_low, a_low)
                both = dot(left_high, right_high) + dot(left_low, right_high) + dot(left_high, right_low)
                at = pl.multiple_of(spot * BLOCK, BLOCK)
                out_ref[h, pl.ds(at, BLOCK), :] = both[:, :HEAD_DIM]
                r_high, r_low = split(both[:, HEAD_DIM:])
                reach_ref[h, pl.ds(at, BLOCK), :] = beside(r_high, r_low)
        return carry

    lax.fori_loop(0, count // per_step, step, 0)
    for h in range(share):
        final_ref[h] = state_ref[h]


def finish_kernel(dims, meta_ref, incoming_ref, gate_ref, gain_ref, *refs):
    share, gate_row, counts = dims
    out_ref, pieces = refs[-1], refs[:-1]
    piece_rows = BLOCK // 2
    is_first = meta_ref[meta_ref.shape[0] - 1]
    first_block = 0
    for number, count in enumerate(counts):
        core_ref, reach_ref = pieces[2 * number], pieces[2 * number + 1]

        def step(spot, carry, core_ref=core_ref, reach_ref=reach_ref, first_block=first_block):
            n = first_block + spot
            at = pl.multiple_of(spot * BLOCK, BLOCK)
            for h in range(share):
                high, low = split(jnp.where(is_first == 1, 0.0, incoming_ref[h]))
                row = beside(high, low)
                both = dot(reach_ref[h, pl.ds(at, BLOCK), :], below(row, row))
                core = core_ref[h, pl.ds(at, BLOCK), :] + both[:, :HEAD_DIM] + both[:, HEAD_DIM:]
                scale = lax.rsqrt(jnp.mean(core * core, axis=-1, keepdims=True) + 1e-06)
                gates = []
                for half in range(2):
                    place = meta_ref[2 * n + half]
                    start = gate_row + h * BLOCK + (place % 2) * piece_rows
                    start = pl.multiple_of(start, piece_rows)
                    gates.append(gate_ref[place // 2, pl.ds(start, piece_rows), :].astype(F32))
                gate = below(*gates)
                result = core * scale * gain_ref[...] * silu(gate)
                out_ref[n, h * BLOCK : (h + 1) * BLOCK, :] = result.astype(BF16)
            return carry

        lax.fori_loop(0, count, step, 0)
        first_block = first_block + count


def gather_kernel(moves, logit_place, *refs):
    sources = refs[: len(refs) - 2 - (1 if logit_place else 0)]
    if logit_place:
        first_row, heads = logit_place
        sources, logit_ref = sources[:-1], sources[-1]
        out_ref, sems, wide_ref = refs[-3], refs[-2], refs[-1]
    else:
        out_ref, sems = refs[-2], refs[-1]
    copies = []
    for number, (begin, length, column, place, row) in enumerate(moves):
        copies.append(
            pltpu.make_async_copy(
                sources[0].at[pl.ds(begin, length), pl.ds(column, HEAD_DIM)],
                out_ref.at[place, pl.ds(row, length), :],
                sems.at[number],
            )
        )
    for copy in copies:
        copy.start()
    if logit_place:
        tokens = logit_ref.shape[0]
        half = tokens // 2
        turned = logit_ref[...].astype(F32).T
        wide_ref[...] = jnp.zeros(wide_ref.shape, F32)
        wide_ref[0 : 2 * VALUE_HEADS, :] = turned
        lane = lax.broadcasted_iota(jnp.int32, (8, tokens), 1)
        for place in range(out_ref.shape[0]):
            early, late = [], []
            for kind in range(2):
                begin = kind * VALUE_HEADS + place * heads
                part = wide_ref[begin : begin + 8, :]
                rolled = pltpu.roll(part, half, 1)
                early.append(jnp.where(lane < half, part, rolled))
                late.append(jnp.where(lane < half, rolled, part))
            joined = below(*(early + late)).astype(BF16)
            out_ref[place, first_row : first_row + 32, :] = joined
    for copy in copies:
        copy.wait()


def scatter_kernel(moves, aliased, *refs):
    source_ref, out_ref, sems = refs[0], refs[-2], refs[-1]
    copies = []
    for number, (place, row, length, column) in enumerate(moves):
        copies.append(
            pltpu.make_async_copy(
                source_ref.at[place, pl.ds(row, length), :],
                out_ref.at[:, pl.ds(column, HEAD_DIM)],
                sems.at[number],
            )
        )
    for copy in copies:
        copy.start()
    for copy in copies:
        copy.wait()


MIB = 2**20


def limits(mib):
    return pltpu.CompilerParams(vmem_limit_bytes=mib * MIB)


def cost(flops):
    return pl.CostEstimate(flops=int(flops), bytes_accessed=2**20, transcendentals=0)


vmem = pl.BlockSpec(memory_space=pltpu.VMEM)
smem = pl.BlockSpec(memory_space=pltpu.SMEM)
anywhere = pl.BlockSpec(memory_space=pl.ANY)


def gather(name, source, moves, places, rows, logits=None, first_row=0, heads=0):
    operands, in_specs = [source], [anywhere]
    scratch = [pltpu.SemaphoreType.DMA((len(moves),))]
    logit_place = None
    if logits is not None:
        operands.append(logits)
        in_specs.append(vmem)
        scratch.append(pltpu.VMEM((2 * VALUE_HEADS + 8, logits.shape[0]), F32))
        logit_place = (first_row, heads)
    return pl.pallas_call(
        functools.partial(gather_kernel, tuple(moves), logit_place),
        out_shape=jax.ShapeDtypeStruct((places, rows, HEAD_DIM), BF16),
        in_specs=in_specs,
        out_specs=vmem,
        scratch_shapes=scratch,
        compiler_params=limits(6),
        cost_estimate=cost(8e8),
        name=name,
    )(*operands)


def scatter(name, source, moves, out_shape, base=None):
    operands, in_specs, aliases = [source], [vmem], {}
    if base is not None:
        operands.append(base)
        in_specs.append(anywhere)
        aliases = {1: 0}
    return pl.pallas_call(
        functools.partial(scatter_kernel, tuple(moves), base is not None),
        out_shape=jax.ShapeDtypeStruct(out_shape, BF16),
        in_specs=in_specs,
        out_specs=anywhere,
        scratch_shapes=[pltpu.SemaphoreType.DMA((len(moves),))],
        input_output_aliases=aliases,
        compiler_params=limits(4),
        cost_estimate=cost(8e8),
        name=name,
    )(*operands)


def passed_round(value, axis):
    length = lax.axis_size(axis)
    return lax.ppermute(value, axis, [(i, (i + 1) % length) for i in range(length)])


def exchanged(value):
    return lax.all_to_all(value, "cp", split_axis=0, concat_axis=0, tiled=True)


def per_device(mixed_qkv, gate_z, gate_logits, block_table, conv_weight, a_log, dt_bias, norm_gain):
    cp_count = lax.axis_size("cp")
    seg_count = lax.axis_size("seg")
    cp_place = lax.axis_index("cp")
    rows = mixed_qkv.shape[0]
    heads = VALUE_HEADS // cp_count
    groups = max(1, heads // GROUP)
    share = heads // groups
    tiles = 2 + share
    key_width = KEY_HEADS * HEAD_DIM
    count = cp_count * rows // BLOCK
    gate_row = tiles * BLOCK

    order = jnp.argsort(block_table[0]).astype(jnp.int32)
    is_first = (lax.axis_index("seg") == 0).astype(jnp.int32).reshape(1)
    meta = jnp.concatenate([order, is_first])

    def columns(place, group):
        value_head = place * heads + group * share
        key_head = value_head // GROUP
        found = [key_head * HEAD_DIM, key_width + key_head * HEAD_DIM]
        return found + [2 * key_width + (value_head + h) * HEAD_DIM for h in range(share)]

    def group_moves(group):
        return [
            (0, rows, column, place, tile * rows)
            for place in range(cp_count)
            for tile, column in enumerate(columns(place, group))
        ]

    received = []
    for group in range(groups):
        with_logits = dict(logits=gate_logits, first_row=gate_row, heads=heads) if group == 0 else {}
        sent = gather(
            "pack%d" % group,
            mixed_qkv,
            group_moves(group),
            cp_count,
            gate_row + (32 if group == 0 else 0),
            **with_logits,
        )
        received.append(exchanged(sent))
    tail_moves = [
        (rows - 16, 16, column, place, (group * tiles + tile) * 16)
        for place in range(cp_count)
        for group in range(groups)
        for tile, column in enumerate(columns(place, group))
    ]
    tails = gather("packtail", mixed_qkv, tail_moves, cp_count, groups * tiles * 16)
    tails = exchanged(tails)
    last = order[2 * cp_count - 1]
    tail = lax.dynamic_index_in_dim(tails, last // 2, 0, keepdims=False)
    tail = passed_round(tail, "seg").reshape(groups, tiles, 16, HEAD_DIM)

    gate_moves = [
        (0, rows, (place * heads + h) * HEAD_DIM, place, h * rows)
        for place in range(cp_count)
        for h in range(heads)
    ]
    gate_seq = exchanged(gather("packz", gate_z, gate_moves, cp_count, heads * rows))

    def group_weights(group):
        value_head = cp_place * heads + group * share
        key_head = value_head // GROUP
        shaped = conv_weight.reshape(CONV, -1, HEAD_DIM)
        picked = [
            lax.dynamic_slice_in_dim(shaped, key_head, 1, 1),
            lax.dynamic_slice_in_dim(shaped, KEY_HEADS + key_head, 1, 1),
            lax.dynamic_slice_in_dim(shaped, 2 * KEY_HEADS + value_head, share, 1),
        ]
        return jnp.concatenate(picked, axis=1).transpose(1, 0, 2)

    head_log = lax.dynamic_slice_in_dim(a_log, cp_place * heads, heads, 0)
    head_bias = lax.dynamic_slice_in_dim(dt_bias, cp_place * heads, heads, 0)
    rates = jnp.pad(jnp.stack([head_log, head_bias]), ((0, 0), (0, 8 - heads)))
    rates = jnp.broadcast_to(rates[:, :, None], (2, 8, BLOCK))

    def local(group, part, first_block, blocks, state):
        per_step = min(4, blocks)
        operands = [meta, received[group], received[0], tail[group], group_weights(group), rates]
        if state is not None:
            operands.append(state)
        in_specs = [smem] + [vmem] * (len(operands) - 1)
        dims = (group, share, first_block, blocks, per_step, gate_row, state is not None)
        return pl.pallas_call(
            functools.partial(local_kernel, dims),
            out_shape=(
                jax.ShapeDtypeStruct((share, blocks * BLOCK, HEAD_DIM), F32),
                jax.ShapeDtypeStruct((share, blocks * BLOCK, 2 * HEAD_DIM), BF16),
                jax.ShapeDtypeStruct((share, HEAD_DIM, 2 * HEAD_DIM), F32),
            ),
            in_specs=in_specs,
            out_specs=(vmem, vmem, vmem),
            scratch_shapes=[
                pltpu.VMEM((per_step * tiles, 8 + BLOCK, HEAD_DIM), F32),
                pltpu.VMEM((len(LEVELS), BLOCK, BLOCK), BF16),
                pltpu.VMEM((share, HEAD_DIM, 2 * HEAD_DIM), F32),
            ],
            compiler_params=limits(20),
            cost_estimate=cost(6e8 * blocks * share),
            name="local%d_%d" % (group, part),
        )(*operands)

    def chain(final):
        shift = final[:, :, :HEAD_DIM]
        reach_map = final[:, :, HEAD_DIM:]
        reach_map = jnp.where(lax.axis_index("seg") == 0, 0.0, reach_map)
        incoming = jnp.zeros((share, HEAD_DIM, HEAD_DIM), F32)
        for rounds in range(seg_count - 1):
            advanced = shift
            if rounds:
                advanced = shift + jnp.einsum(
                    "hij,hjk->hik", reach_map, incoming, precision=highest
                )
            incoming = passed_round(advanced, "seg")
        return incoming

    def finish(group, incoming, pieces, counts):
        flat = [array for piece in pieces for array in piece]
        return pl.pallas_call(
            functools.partial(finish_kernel, (share, group * share * rows, counts)),
            out_shape=jax.ShapeDtypeStruct((count, share * BLOCK, HEAD_DIM), BF16),
            in_specs=[smem] + [vmem] * (3 + len(flat)),
            out_specs=vmem,
            compiler_params=limits(8),
            cost_estimate=cost(1e9),
            name="finish%d" % group,
        )(meta, incoming, gate_seq, norm_gain.reshape(1, HEAD_DIM), *flat)

    result = None
    for group in range(groups):
        parts = 2 if group == 1 and count % 8 == 0 else 1
        state, pieces = None, []
        for part in range(parts):
            blocks = count // parts
            core, reach, state = local(group, part, part * blocks, blocks, state)
            pieces.append((core, reach))
        incoming = chain(state)
        done = finish(group, incoming, pieces, [count // parts] * parts)
        swapped = exchanged(done)
        moves = [
            (place, h * rows, rows, (place * heads + group * share + h) * HEAD_DIM)
            for place in range(cp_count)
            for h in range(share)
        ]
        result = scatter(
            "unpack%d" % group, swapped, moves, (rows, VALUE_HEADS * HEAD_DIM), result
        )
    return result


def solution(mesh):
    return jax.shard_map(
        per_device,
        mesh=mesh,
        in_specs=(
            P(("seg", "cp"), None),
            P(("seg", "cp"), None),
            P(("seg", "cp"), None),
            P("seg", None),
            P(),
            P(),
            P(),
            P(),
        ),
        out_specs=P(("seg", "cp"), None),
        check_vma=False,
    )
```

time: 131 us -> 126 us (0.962)
  blocking collectives: 18.9 us -> 0 us
  starting transfers between devices: 24.5 us -> 31.8 us
  Pallas kernels: 33.1 us -> 40.4 us
  matrix products: 0.79 us -> 3.56 us
  other arithmetic: 3.45 us -> 1.34 us
    all_to_all x1 -> x0, blocking collectives: 18.9 us -> none  [per_device(): lax.all_to_all(blocks, 'cp', split_axis=0, concat_axis=0, tiled=True)]
    all_to_all x2 -> x6, starting transfers between devices: 8.9 us -> 25 us  [exchanged(): return lax.all_to_all(value, 'cp', split_axis=0, concat_axis=0, tiled=True)]
    ppermute x4 -> x7, starting transfers between devices: 15.6 us -> 6.79 us  [passed_round(): lax.ppermute(value, axis, [(i, (i + 1) % length) for i in range(length)])]
    pallas_call x2 -> x11, Pallas kernels: 33.1 us -> 40.4 us  [the longest x3 24.7 us: local(): pl.pallas_call(functools.partial(local_kernel, dims), out_shape=(jax.Shap...]
    unnamed x24 -> x45, local copies, waits for them, and re-layouts: 0.74 us -> 7.57 us
    reshape x7 -> x0, local copies, waits for them, and re-layouts: 5 us -> none  [the longest x4 3.3 us: value_tiles(): return array.reshape(lead, cp_count, heads, HEAD_DIM)]
    dot_general x2 -> x4, matrix products: 0.79 us -> 3.56 us  [chain(): jnp.einsum('hij,hjk->hik', reach_map, incoming, precision=highest)]
    all_to_all x2 -> x6, waiting for transfers between devices: 22.6 us -> 20 us  [exchanged(): return lax.all_to_all(value, 'cp', split_axis=0, concat_axis=0, tiled=True)]
  transfers between devices with their start and end apart: 6 -> 13, of which waited for: 5 -> 5; matrix products, arithmetic and copies ran while one was open for 4% -> 6% of each run, Pallas kernels for 0% -> 30%
where the time goes in v1:
time: 126 us; the launch traced here: 125 us
  Pallas kernels  40.4 us (32%)
  waiting for transfers between devices  34.8 us (28%)
  starting transfers between devices  31.8 us (25%)
  local copies, waits for them, and re-layouts  10.5 us (8%)
  matrix products  3.56 us (3%)
  between operations  3.08 us (2%)
  other arithmetic  1.34 us (1%)
    all_to_all x6, starting transfers between devices, exchanged(): return lax.all_to_all(value, 'cp', split_axis=0, concat_axis=0, tiled=True)  25 us
    pallas_call x3, Pallas kernels, local(): pl.pallas_call(functools.partial(local_kernel, dims), out_shape=(jax.Shap...  24.7 us
    all_to_all x6, waiting for transfers between devices, exchanged(): return lax.all_to_all(value, 'cp', split_axis=0, concat_axis=0, tiled=True)  20 us
    ppermute x7, waiting for transfers between devices, passed_round(): lax.ppermute(value, axis, [(i, (i + 1) % length) for i in range(length)])  14.8 us
    unnamed x45, local copies, waits for them, and re-layouts  7.57 us
    pallas_call x2, Pallas kernels, finish(): pl.pallas_call(functools.partial(finish_kernel, (share, group * share * r...  7.4 us
    ppermute x7, starting transfers between devices, passed_round(): lax.ppermute(value, axis, [(i, (i + 1) % length) for i in range(length)])  6.79 us
    pallas_call x4, Pallas kernels, gather(): pl.pallas_call(functools.partial(gather_kernel, tuple(moves), logit_place...  6.48 us
  transfers between devices with their start and end apart: 13, of which 5 were waited for; matrix products, arithmetic and copies ran while one was open for 6% of the time, Pallas kernels for 30%

profile of v1, /device:TPU:0, one launch (start us, length us, event | category | flops | bytes accessed | tf_op | source)
XLA Modules:
  0.0 125.4 jit_solution(16872168929594446403)
XLA Ops:
  0.0 1.6 %copy-done = bf16[128,8192]{1,0:T(8,128)(2,1)S(1)} copy-done((bf16[128,8192]{1,0:T(8,128)(2,1)S(1)}, bf16[128,8192]{1,0:T(8,128)(2,1)}, u32[]{:S(2)}) %copy-start) | copy-done | bytes 2097176
  1.6 1.5 %packtail.1 = bf16[8,128,128]{2,1,0:T(8,128)(2,1)} custom-call(bf16[128,8192]{1,0:T(8,128)(2,1)S(1)} %copy-done), custom_call_target="tpu_custom_call" | custom-call | flops 800000000 | bytes 1048576 | tf_op jit(solution)/shard_map/packtail/pallas_call | solution.py:356
  3.1 5.2 %all-to-all-start.2 = ((bf16[8,128,128]{2,1,0:T(8,128)(2,1)}), bf16[8,128,128]{2,1,0:T(8,128)(2,1)S(1)}, u32[]{:S(2)}, u32[]{:S(2)}) async-start(bf16[8,128,128]{2,1,0:T(8,128)(2,1)} %packtail.1), calls=%async_computation.2 | async-start | bytes 524288 | tf_op jit(solution)/shard_map/all_to_all | solution.py:393
  8.3 1.2 sort.17
  9.6 0.6 slice.24
  12.8 0.1 copy.10.refs_1_
  12.9 0.0 copy-done.1
  12.9 1.6 %pack1.1 = bf16[8,512,128]{2,1,0:T(8,128)(2,1)} custom-call(bf16[128,8192]{1,0:T(8,128)(2,1)S(1)} %copy-done.1), custom_call_target="tpu_custom_call" | custom-call | flops 800000000 | bytes 1048576 | tf_op jit(solution)/shard_map/pack1/pallas_call | solution.py:356
  14.5 1.8 %pack0.1 = bf16[8,544,128]{2,1,0:T(8,128)(2,1)} custom-call(bf16[128,8192]{1,0:T(8,128)(2,1)S(1)} %copy-done.1, bf16[128,64]{1,0:T(8,128)(2,1)S(1)} %copy.10.refs_1_), custom_call_target="tpu_custom_call" | custom-call | flops 800000000 | bytes 1048576 | tf_op jit(solution)/shard_map/pack0/pallas_call | solution.py:356
  16.3 0.0 copy-start.19
  16.3 0.0 copy-start.20
  16.3 0.0 copy-start.17
  16.4 0.0 all-to-all-done.2
  16.4 4.3 %all-to-all-start.1 = ((bf16[8,544,128]{2,1,0:T(8,128)(2,1)}), bf16[8,544,128]{2,1,0:T(8,128)(2,1)S(1)}, u32[]{:S(2)}, u32[]{:S(2)}) async-start(bf16[8,544,128]{2,1,0:T(8,128)(2,1)} %pack0.1), calls=%async_computation.1 | async-start | bytes 2228224 | tf_op jit(solution)/shard_map/all_to_all | solution.py:393
  20.7 0.1 pad_add_fusion.meta_ref
  20.8 0.0 copy-done.20
  20.8 0.1 dynamic-slice_bitcast_fusion.1
  20.9 0.7 constant_dynamic-slice_fusion
  21.6 0.7 constant_dynamic-slice_fusion.2
  22.3 1.6 %collective-permute-start = (bf16[128,128]{1,0:T(8,128)(2,1)S(1)}, bf16[128,128]{1,0:T(8,128)(2,1)S(1)}, u32[]{:S(2)}, u32[]{:S(2)}) collective-permute-start(bf16[128,128]{1,0:T(8,128)(2,1)S(1)} %dynamic-slice_bitcast_fusion), channel_id=1, source_target_pairs={{0,8},{8,16},{16,24},{24,0},{1,9},{9,17},{17,25},{25,1},{2,10},{10... | collective-permute-start | bytes 98312 | tf_op jit(solution)/shard_map/ppermute | solution.py:389
  24.0 1.6 %packz.1 = bf16[8,512,128]{2,1,0:T(8,128)(2,1)} custom-call(bf16[128,4096]{1,0:T(8,128)(2,1)S(1)} %copy-done.17), custom_call_target="tpu_custom_call" | custom-call | flops 800000000 | bytes 1048576 | tf_op jit(solution)/shard_map/packz/pallas_call | solution.py:356
  25.6 11.2 %all-to-all-done.1.logit_ref.recv_ref = bf16[8,544,128]{2,1,0:T(8,128)(2,1)S(1)} async-done(((bf16[8,544,128]{2,1,0:T(8,128)(2,1)}), bf16[8,544,128]{2,1,0:T(8,128)(2,1)S(1)}, u32[]{:S(2)}, u32[]{:S(2)}) %all-to-all-start.1) | async-done | bytes 1114144 | tf_op jit(solution)/shard_map/all_to_all | solution.py:393
  36.8 3.6 %all-to-all-start = ((bf16[8,512,128]{2,1,0:T(8,128)(2,1)}), bf16[8,512,128]{2,1,0:T(8,128)(2,1)S(1)}, u32[]{:S(2)}, u32[]{:S(2)}) async-start(bf16[8,512,128]{2,1,0:T(8,128)(2,1)} %pack1.1), calls=%async_computation | async-start | bytes 2097152 | tf_op jit(solution)/shard_map/all_to_all | solution.py:393
  40.3 0.0 collective-permute-done
  40.4 0.1 broadcast_in_dim.11.rate_ref
  40.4 12.1 %local0_0.1 = (f32[2,1024,128]{2,1,0:T(8,128)S(1)}, bf16[2,1024,256]{2,1,0:T(8,128)(2,1)S(1)}, f32[2,128,256]{2,1,0:T(8,128)S(1)}) custom-call(s32[17]{0:T(128)S(1)} %pad_add_fusion.meta_ref, bf16[8,544,128]{2,1,0:T(8,128)(2,1)S(1)} %all-to-all-done.1.logit_ref.recv_ref, bf16[8,544,128]{2,1,0:T(8,128)(2,1)S(1)} %all-to-all-done.1.logit_ref.recv_ref, ...), custom_call_target="tpu_custom_call" | custom-call | flops 9600000000 | bytes 1048576 | tf_op jit(solution)/shard_map/local0_0/pallas_call | solution.py:480
  52.5 1.0 copy-done.2
  53.5 1.0 copy-done.4
  54.5 0.7 slice.29
  55.2 1.6 %collective-permute-start.4 = (f32[2,128,128]{2,1,0:T(8,128)}, f32[2,128,128]{2,1,0:T(8,128)}, u32[]{:S(2)}, u32[]{:S(2)}) collective-permute-start(f32[2,128,128]{2,1,0:T(8,128)} %slice.29), channel_id=1, source_target_pairs={{0,8},{8,16},{16,24},{24,0},{1,9},{9,17},{17,25},{25,1},{2,10},{10... | collective-permute-start | bytes 393224 | tf_op jit(solution)/shard_map/ppermute | solution.py:389
  56.8 0.0 all-to-all-done.recv_ref
  56.8 4.1 %all-to-all-start.3 = ((bf16[8,512,128]{2,1,0:T(8,128)(2,1)}), bf16[8,512,128]{2,1,0:T(8,128)(2,1)S(1)}, u32[]{:S(2)}, u32[]{:S(2)}) async-start(bf16[8,512,128]{2,1,0:T(8,128)(2,1)} %packz.1), calls=%async_computation.3 | async-start | bytes 2097152 | tf_op jit(solution)/shard_map/all_to_all | solution.py:393
  60.9 6.3 %local1_0.1 = (f32[2,512,128]{2,1,0:T(8,128)S(1)}, bf16[2,512,256]{2,1,0:T(8,128)(2,1)S(1)}, f32[2,128,256]{2,1,0:T(8,128)S(1)}) custom-call(s32[17]{0:T(128)S(1)} %pad_add_fusion.meta_ref, bf16[8,512,128]{2,1,0:T(8,128)(2,1)S(1)} %all-to-all-done.recv_ref, bf16[8,544,128]{2,1,0:T(8,128)(2,1)S(1)} %all-to-all-done.1.logit_ref.recv_ref, ...), custom_call_target="tpu_custom_call" | custom-call | flops 4800000000 | bytes 1048576 | tf_op jit(solution)/shard_map/local1_0/pallas_call | solution.py:480
  67.2 0.0 copy-start.8
  67.2 0.8 copy-done.8
  68.0 0.8 copy-done.10
  68.8 0.0 collective-permute-done.4
  68.8 1.2 convolution_add_fusion.1
  70.0 1.6 %collective-permute-start.5 = (f32[2,128,128]{2,1,0:T(8,128)S(1)}, f32[2,128,128]{2,1,0:T(8,128)S(1)}, u32[]{:S(2)}, u32[]{:S(2)}) collective-permute-start(f32[2,128,128]{2,1,0:T(8,128)S(1)} %convolution_add_fusion.1), channel_id=1, source_target_pairs={{0,8},{8,16},{16,24},{24,0},{1,9},{9,17},{17,25},{25,1},{2,10},{10... | collective-permute-start | bytes 393224 | tf_op jit(solution)/shard_map/ppermute | solution.py:389
  71.6 6.3 %local1_1.1 = (f32[2,512,128]{2,1,0:T(8,128)S(1)}, bf16[2,512,256]{2,1,0:T(8,128)(2,1)S(1)}, f32[2,128,256]{2,1,0:T(8,128)S(1)}) custom-call(s32[17]{0:T(128)S(1)} %pad_add_fusion.meta_ref, bf16[8,512,128]{2,1,0:T(8,128)(2,1)S(1)} %all-to-all-done.recv_ref, bf16[8,544,128]{2,1,0:T(8,128)(2,1)S(1)} %all-to-all-done.1.logit_ref.recv_ref, ...), custom_call_target="tpu_custom_call" | custom-call | flops 4800000000 | bytes 1048576 | tf_op jit(solution)/shard_map/local1_1/pallas_call | solution.py:480
  78.0 1.7 %collective-permute-start.1 = (f32[2,128,128]{2,1,0:T(8,128)S(1)}, f32[2,128,128]{2,1,0:T(8,128)S(1)}, u32[]{:S(2)}, u32[]{:S(2)}) collective-permute-start(f32[2,128,128]{2,1,0:T(8,128)S(1)} %slice.26), channel_id=1, source_target_pairs={{0,8},{8,16},{16,24},{24,0},{1,9},{9,17},{17,25},{25,1},{2,10},{10... | collective-permute-start | bytes 393224 | tf_op jit(solution)/shard_map/ppermute | solution.py:389
  79.6 0.0 collective-permute-done.5
  79.6 0.0 copy-done.7
  79.6 0.3 convolution_add_fusion
  79.9 0.2 collective-permute-start.6
  80.1 6.0 %collective-permute-done.1 = f32[2,128,128]{2,1,0:T(8,128)S(1)} collective-permute-done((f32[2,128,128]{2,1,0:T(8,128)S(1)}, f32[2,128,128]{2,1,0:T(8,128)S(1)}, u32[]{:S(2)}, u32[]{:S(2)}) %collective-permute-start.1) | collective-permute-done | bytes 131104 | tf_op jit(solution)/shard_map/ppermute | solution.py:389
  86.2 0.9 convolution_add_fusion.3
  87.1 0.0 collective-permute-start.2
  87.1 0.0 all-to-all-done.3.gate_ref
  87.1 1.1 collective-permute-done.6.incoming_ref
  88.2 1.2 copy-done.5
  89.5 3.7 %finish0.1 = bf16[8,256,128]{2,1,0:T(8,128)(2,1)} custom-call(s32[17]{0:T(128)S(1)} %pad_add_fusion.meta_ref, f32[2,128,128]{2,1,0:T(8,128)S(1)} %collective-permute-done.6.incoming_ref, bf16[8,512,128]{2,1,0:T(8,128)(2,1)S(1)} %all-to-all-done.3.gate_ref, f32[1,128]{1,0:T(1,128)S(1)} %bitcast.24, f32[2,1024,128]{2,1,0:T(8,128)S(1)} %copy-done.3, ...), custom_call_target="tpu_custom_call" | custom-call | flops 1000000000 | bytes 1048576 | tf_op jit(solution)/shard_map/finish0/pallas_call | solution.py:515
  93.2 3.9 %all-to-all-start.5 = ((bf16[8,256,128]{2,1,0:T(8,128)(2,1)}), bf16[8,256,128]{2,1,0:T(8,128)(2,1)S(1)}, u32[]{:S(2)}, u32[]{:S(2)}) async-start(bf16[8,256,128]{2,1,0:T(8,128)(2,1)} %finish0.1), calls=%async_computation.5 | async-start | bytes 1048576 | tf_op jit(solution)/shard_map/all_to_all | solution.py:393
  97.1 0.0 collective-permute-done.2
  97.1 1.2 convolution_add_fusion.2
  98.3 0.1 collective-permute-start.3
  98.4 7.7 %collective-permute-done.3.incoming_ref = f32[2,128,128]{2,1,0:T(8,128)S(1)} collective-permute-done((f32[2,128,128]{2,1,0:T(8,128)S(1)}, f32[2,128,128]{2,1,0:T(8,128)S(1)}, u32[]{:S(2)}, u32[]{:S(2)}) %collective-permute-start.3) | collective-permute-done | bytes 131104 | tf_op jit(solution)/shard_map/ppermute | solution.py:389
  106.1 1.0 copy-done.15
  107.1 3.7 %finish1.1 = bf16[8,256,128]{2,1,0:T(8,128)(2,1)} custom-call(s32[17]{0:T(128)S(1)} %pad_add_fusion.meta_ref, f32[2,128,128]{2,1,0:T(8,128)S(1)} %collective-permute-done.3.incoming_ref, bf16[8,512,128]{2,1,0:T(8,128)(2,1)S(1)} %all-to-all-done.3.gate_ref, f32[1,128]{1,0:T(1,128)S(1)} %bitcast.25, f32[2,512,128]{2,1,0:T(8,128)S(1)} %copy-done.9, ...), custom_call_target="tpu_custom_call" | custom-call | flops 1000000000 | bytes 1048576 | tf_op jit(solution)/shard_map/finish1/pallas_call | solution.py:515
  110.8 0.0 all-to-all-done.5.refs_0_
  110.8 3.8 %all-to-all-start.4 = ((bf16[8,256,128]{2,1,0:T(8,128)(2,1)}), bf16[8,256,128]{2,1,0:T(8,128)(2,1)S(1)}, u32[]{:S(2)}, u32[]{:S(2)}) async-start(bf16[8,256,128]{2,1,0:T(8,128)(2,1)} %finish1.1), calls=%async_computation.4 | async-start | bytes 1048576 | tf_op jit(solution)/shard_map/all_to_all | solution.py:393
  114.6 0.9 unpack0.1.refs_1_
  115.5 8.8 %all-to-all-done.4.refs_0_ = bf16[8,256,128]{2,1,0:T(8,128)(2,1)S(1)} async-done(((bf16[8,256,128]{2,1,0:T(8,128)(2,1)}), bf16[8,256,128]{2,1,0:T(8,128)(2,1)S(1)}, u32[]{:S(2)}, u32[]{:S(2)}) %all-to-all-start.4) | async-done | bytes 524320 | tf_op jit(solution)/shard_map/all_to_all | solution.py:393
  124.3 0.9 unpack1.1
  (37 shorter events, 0.1 us)
Async XLA Ops:
  0.0 1.6 %copy-start = (bf16[128,8192]{1,0:T(8,128)(2,1)S(1)}, bf16[128,8192]{1,0:T(8,128)(2,1)}, u32[]{:S(2)}) copy-start(bf16[128,8192]{1,0:T(8,128)(2,1)} %refs_0_.6) | copy-start | bytes 6291460
  1.6 6.7 %copy-start.21 = (s32[1,16]{1,0:T(1,128)S(1)}, s32[1,16]{1,0:T(1,128)}, u32[]{:S(2)}) copy-start(s32[1,16]{1,0:T(1,128)} %param.11) | copy-start | bytes 196
  1.6 11.2 %copy-start.18 = (bf16[128,64]{0,1:T(8,128)(2,1)S(1)}, bf16[128,64]{0,1:T(8,128)(2,1)}, u32[]{:S(2)}) copy-start(bf16[128,64]{0,1:T(8,128)(2,1)} %param.10) | copy-start | bytes 49156
  1.6 11.3 %copy-start.1 = (bf16[128,8192]{1,0:T(8,128)(2,1)S(1)}, bf16[128,8192]{1,0:T(8,128)(2,1)}, u32[]{:S(2)}) copy-start(bf16[128,8192]{1,0:T(8,128)(2,1)} %refs_0_.6) | copy-start | bytes 6291460
  3.1 13.3 %all-to-all-start.2 = ((bf16[8,128,128]{2,1,0:T(8,128)(2,1)}), bf16[8,128,128]{2,1,0:T(8,128)(2,1)S(1)}, u32[]{:S(2)}, u32[]{:S(2)}) async-start(bf16[8,128,128]{2,1,0:T(8,128)(2,1)} %packtail.1), calls=%async_computation.2 | async-start | bytes 524288 | tf_op jit(solution)/shard_map/all_to_all | solution.py:393
  16.3 4.5 %copy-start.19 = (f32[32]{0:T(128)S(1)}, f32[32]{0:T(128)}, u32[]{:S(2)}) copy-start(f32[32]{0:T(128)} %param.14) | copy-start | bytes 388
  16.3 4.4 %copy-start.20 = (f32[32]{0:T(128)S(1)}, f32[32]{0:T(128)}, u32[]{:S(2)}) copy-start(f32[32]{0:T(128)} %param.13) | copy-start | bytes 388
  16.3 7.6 %copy-start.17 = (bf16[128,4096]{1,0:T(8,128)(2,1)S(1)}, bf16[128,4096]{1,0:T(8,128)(2,1)}, u32[]{:S(2)}) copy-start(bf16[128,4096]{1,0:T(8,128)(2,1)} %refs_0_.7) | copy-start | bytes 3145732
  16.4 20.4 %all-to-all-start.1 = ((bf16[8,544,128]{2,1,0:T(8,128)(2,1)}), bf16[8,544,128]{2,1,0:T(8,128)(2,1)S(1)}, u32[]{:S(2)}, u32[]{:S(2)}) async-start(bf16[8,544,128]{2,1,0:T(8,128)(2,1)} %pack0.1), calls=%async_computation.1 | async-start | bytes 2228224 | tf_op jit(solution)/shard_map/all_to_all | solution.py:393
  22.3 18.0 %collective-permute-start = (bf16[128,128]{1,0:T(8,128)(2,1)S(1)}, bf16[128,128]{1,0:T(8,128)(2,1)S(1)}, u32[]{:S(2)}, u32[]{:S(2)}) collective-permute-start(bf16[128,128]{1,0:T(8,128)(2,1)S(1)} %dynamic-slice_bitcast_fusion), channel_id=1, source_target_pairs={{0,8},{8,16},{16,24},{24,0},{1,9},{9,17},{17,25},{25,1},{2,10},{10... | collective-permute-start | bytes 98312 | tf_op jit(solution)/shard_map/ppermute | solution.py:389
  36.8 20.0 %all-to-all-start = ((bf16[8,512,128]{2,1,0:T(8,128)(2,1)}), bf16[8,512,128]{2,1,0:T(8,128)(2,1)S(1)}, u32[]{:S(2)}, u32[]{:S(2)}) async-start(bf16[8,512,128]{2,1,0:T(8,128)(2,1)} %pack1.1), calls=%async_computation | async-start | bytes 2097152 | tf_op jit(solution)/shard_map/all_to_all | solution.py:393
  52.5 1.0 copy-start.2
  53.5 1.0 copy-start.4
  54.5 14.3 %copy-start.6 = (f32[2,128,256]{2,1,0:T(8,128)}, f32[2,128,256]{2,1,0:T(8,128)S(1)}, u32[]{:S(2)}) copy-start(f32[2,128,256]{2,1,0:T(8,128)S(1)} %get-tuple-element.22) | copy-start | bytes 786436
  55.2 13.6 %collective-permute-start.4 = (f32[2,128,128]{2,1,0:T(8,128)}, f32[2,128,128]{2,1,0:T(8,128)}, u32[]{:S(2)}, u32[]{:S(2)}) collective-permute-start(f32[2,128,128]{2,1,0:T(8,128)} %slice.29), channel_id=1, source_target_pairs={{0,8},{8,16},{16,24},{24,0},{1,9},{9,17},{17,25},{25,1},{2,10},{10... | collective-permute-start | bytes 393224 | tf_op jit(solution)/shard_map/ppermute | solution.py:389
  56.8 30.3 %all-to-all-start.3 = ((bf16[8,512,128]{2,1,0:T(8,128)(2,1)}), bf16[8,512,128]{2,1,0:T(8,128)(2,1)S(1)}, u32[]{:S(2)}, u32[]{:S(2)}) async-start(bf16[8,512,128]{2,1,0:T(8,128)(2,1)} %packz.1), calls=%async_computation.3 | async-start | bytes 2097152 | tf_op jit(solution)/shard_map/all_to_all | solution.py:393
  67.2 0.8 copy-start.8
  68.0 0.8 copy-start.10
  70.0 9.6 %collective-permute-start.5 = (f32[2,128,128]{2,1,0:T(8,128)S(1)}, f32[2,128,128]{2,1,0:T(8,128)S(1)}, u32[]{:S(2)}, u32[]{:S(2)}) collective-permute-start(f32[2,128,128]{2,1,0:T(8,128)S(1)} %convolution_add_fusion.1), channel_id=1, source_target_pairs={{0,8},{8,16},{16,24},{24,0},{1,9},{9,17},{17,25},{25,1},{2,10},{10... | collective-permute-start | bytes 393224 | tf_op jit(solution)/shard_map/ppermute | solution.py:389
  71.6 8.0 %copy-start.7 = (f32[2,128,256]{2,1,0:T(8,128)S(1)}, f32[2,128,256]{2,1,0:T(8,128)}, u32[]{:S(2)}) copy-start(f32[2,128,256]{2,1,0:T(8,128)} %copy-done.6) | copy-start | bytes 786436
  71.6 16.6 %copy-start.16 = (f32[128]{0:T(128)S(1)}, f32[128]{0:T(128)}, u32[]{:S(2)}) copy-start(f32[128]{0:T(128)} %param.15) | copy-start | bytes 1540
  77.9 9.2 %copy-start.12 = (f32[2,512,128]{2,1,0:T(8,128)}, f32[2,512,128]{2,1,0:T(8,128)S(1)}, u32[]{:S(2)}) copy-start(f32[2,512,128]{2,1,0:T(8,128)S(1)} %get-tuple-element.20.refs_2_) | copy-start | bytes 1572868
  77.9 9.2 %copy-start.14 = (bf16[2,512,256]{2,1,0:T(8,128)(2,1)}, bf16[2,512,256]{2,1,0:T(8,128)(2,1)S(1)}, u32[]{:S(2)}) copy-start(bf16[2,512,256]{2,1,0:T(8,128)(2,1)S(1)} %get-tuple-element.21.refs_3_) | copy-start | bytes 1572868
  77.9 10.3 %copy-start.3 = (f32[2,1024,128]{2,1,0:T(8,128)S(1)}, f32[2,1024,128]{2,1,0:T(8,128)}, u32[]{:S(2)}) copy-start(f32[2,1024,128]{2,1,0:T(8,128)} %copy-done.2) | copy-start | bytes 3145732
  78.0 8.2 %collective-permute-start.1 = (f32[2,128,128]{2,1,0:T(8,128)S(1)}, f32[2,128,128]{2,1,0:T(8,128)S(1)}, u32[]{:S(2)}, u32[]{:S(2)}) collective-permute-start(f32[2,128,128]{2,1,0:T(8,128)S(1)} %slice.26), channel_id=1, source_target_pairs={{0,8},{8,16},{16,24},{24,0},{1,9},{9,17},{17,25},{25,1},{2,10},{10... | collective-permute-start | bytes 393224 | tf_op jit(solution)/shard_map/ppermute | solution.py:389
  79.9 8.3 %collective-permute-start.6 = (f32[2,128,128]{2,1,0:T(8,128)S(1)}, f32[2,128,128]{2,1,0:T(8,128)S(1)}, u32[]{:S(2)}, u32[]{:S(2)}) collective-permute-start(f32[2,128,128]{2,1,0:T(8,128)S(1)} %convolution_add_fusion), channel_id=1, source_target_pairs={{0,8},{8,16},{16,24},{24,0},{1,9},{9,17},{17,25},{25,1},{2,10},{10... | collective-permute-start | bytes 393224 | tf_op jit(solution)/shard_map/ppermute | solution.py:389
  87.1 10.0 %collective-permute-start.2 = (f32[2,128,128]{2,1,0:T(8,128)}, f32[2,128,128]{2,1,0:T(8,128)}, u32[]{:S(2)}, u32[]{:S(2)}) collective-permute-start(f32[2,128,128]{2,1,0:T(8,128)} %convolution_add_fusion.3), channel_id=1, source_target_pairs={{0,8},{8,16},{16,24},{24,0},{1,9},{9,17},{17,25},{25,1},{2,10},{10... | collective-permute-start | bytes 393224 | tf_op jit(solution)/shard_map/ppermute | solution.py:389
  88.2 1.2 copy-start.5
  89.5 16.6 %copy-start.13 = (f32[2,512,128]{2,1,0:T(8,128)S(1)}, f32[2,512,128]{2,1,0:T(8,128)}, u32[]{:S(2)}) copy-start(f32[2,512,128]{2,1,0:T(8,128)} %copy-done.12) | copy-start | bytes 1572868
  93.2 12.9 %copy-start.9 = (f32[2,512,128]{2,1,0:T(8,128)S(1)}, f32[2,512,128]{2,1,0:T(8,128)}, u32[]{:S(2)}) copy-start(f32[2,512,128]{2,1,0:T(8,128)} %copy-done.8) | copy-start | bytes 1572868
  93.2 12.9 %copy-start.11 = (bf16[2,512,256]{2,1,0:T(8,128)(2,1)S(1)}, bf16[2,512,256]{2,1,0:T(8,128)(2,1)}, u32[]{:S(2)}) copy-start(bf16[2,512,256]{2,1,0:T(8,128)(2,1)} %copy-done.10) | copy-start | bytes 1572868
  93.2 17.6 %all-to-all-start.5 = ((bf16[8,256,128]{2,1,0:T(8,128)(2,1)}), bf16[8,256,128]{2,1,0:T(8,128)(2,1)S(1)}, u32[]{:S(2)}, u32[]{:S(2)}) async-start(bf16[8,256,128]{2,1,0:T(8,128)(2,1)} %finish0.1), calls=%async_computation.5 | async-start | bytes 1048576 | tf_op jit(solution)/shard_map/all_to_all | solution.py:393
  98.3 7.8 %collective-permute-start.3 = (f32[2,128,128]{2,1,0:T(8,128)S(1)}, f32[2,128,128]{2,1,0:T(8,128)S(1)}, u32[]{:S(2)}, u32[]{:S(2)}) collective-permute-start(f32[2,128,128]{2,1,0:T(8,128)S(1)} %convolution_add_fusion.2), channel_id=1, source_target_pairs={{0,8},{8,16},{16,24},{24,0},{1,9},{9,17},{17,25},{25,1},{2,10},{10... | collective-permute-start | bytes 393224 | tf_op jit(solution)/shard_map/ppermute | solution.py:389
  106.1 1.0 copy-start.15
  110.8 13.5 %all-to-all-start.4 = ((bf16[8,256,128]{2,1,0:T(8,128)(2,1)}), bf16[8,256,128]{2,1,0:T(8,128)(2,1)S(1)}, u32[]{:S(2)}, u32[]{:S(2)}) async-start(bf16[8,256,128]{2,1,0:T(8,128)(2,1)} %finish1.1), calls=%async_computation.4 | async-start | bytes 1048576 | tf_op jit(solution)/shard_map/all_to_all | solution.py:393

commit v2 on v1

v2 whole, which is shorter than its diff:
```python
import functools

import jax
import jax.numpy as jnp
from jax import lax
from jax.experimental import pallas as pl
from jax.experimental.pallas import tpu as pltpu
from jax.sharding import PartitionSpec as P


VALUE_HEADS = 32
KEY_HEADS = 16
HEAD_DIM = 128
CONV = 4
BLOCK = 128
GROUP = VALUE_HEADS // KEY_HEADS
LEVELS = (2, 4, 8, 16, 32, 64)

F32 = jnp.float32
BF16 = jnp.bfloat16


def dot(a, b):
    return jnp.dot(a, b, preferred_element_type=F32)


def split(x):
    high = x.astype(BF16)
    low = (x - high.astype(F32)).astype(BF16)
    return high, low


def beside(*parts):
    return jnp.concatenate(parts, axis=1)


def below(*parts):
    return jnp.concatenate(parts, axis=0)


def narrow_product(a, b):
    row = beside(b[0], b[1])
    both = dot(beside(a[0], a[1]), below(row, row))
    half = row.shape[1] // 2
    return both[:, :half] + both[:, half:]


def wide_product(a, b):
    return dot(beside(a[0], a[1]), below(b[0], b[0])) + dot(a[0], b[1])


def silu(v):
    return v / (1.0 + jnp.exp(-v))


def softplus(v):
    e = jnp.exp(-jnp.abs(v))
    s = e / (2.0 + e)
    t = s * s
    series = 1.0 / 19.0
    for odd in (17, 15, 13, 11, 9, 7, 5, 3, 1):
        series = series * t + 1.0 / odd
    return jnp.maximum(v, 0.0) + 2.0 * s * series


def together(*streams):
    alive = list(streams)
    while alive:
        for stream in list(alive):
            if next(stream, "over") == "over":
                alive.remove(stream)


def shifted_rows(meta_ref, recv_ref, rows_ref, slot, lead, n, first_row):
    piece_rows = BLOCK // 2
    place = meta_ref[jnp.maximum(2 * n - 1, 0)]
    start = first_row + (place % 2) * piece_rows + piece_rows - 16
    old = recv_ref[place // 2, pl.ds(pl.multiple_of(start, 16), 16), :].astype(F32)
    rows_ref[slot, 0:8, :] = jnp.where(n == 0, lead, old)[8:16]
    for half in range(2):
        place = meta_ref[2 * n + half]
        start = pl.multiple_of(first_row + (place % 2) * piece_rows, piece_rows)
        fresh = recv_ref[place // 2, pl.ds(start, piece_rows), :]
        begin = 8 + half * piece_rows
        rows_ref[slot, begin : begin + piece_rows, :] = fresh.astype(F32)


def convolved(rows_ref, slot, weight_ref, tile):
    summed = None
    for offset in range(CONV):
        begin = 8 - CONV + 1 + offset
        term = weight_ref[tile, offset : offset + 1, :] * rows_ref[slot, begin : begin + BLOCK, :]
        summed = term if summed is None else summed + term
    return silu(summed)


def unit_scale(matrix):
    return lax.rsqrt(jnp.sum(matrix * matrix, axis=-1, keepdims=True) + 1e-06)


def inner_kernel(
    dims,
    meta_ref,
    recv_ref,
    tail_ref,
    weight_ref,
    rate_ref,
    solved_out,
    state_out,
    flip_out,
    row_out,
    shift_ref,
    map_ref,
    solved_ref,
    before_ref,
    flip_ref,
    rows_ref,
    mask_ref,
    state_ref,
    sems,
):
    group, share, count, per_step, per_chunk = dims
    tiles = 1 + share
    gate_row = tiles * BLOCK
    piece_rows = BLOCK // 2
    is_first = meta_ref[meta_ref.shape[0] - 1]

    row_index = lax.broadcasted_iota(jnp.int32, (BLOCK, BLOCK), 0)
    col_index = lax.broadcasted_iota(jnp.int32, (BLOCK, BLOCK), 1)
    differ = row_index ^ col_index
    for place, size in enumerate(LEVELS):
        inside = (differ >= size) & (differ < 2 * size)
        mask_ref[place] = jnp.where(inside, 1.0, 0.0).astype(BF16)
    eye = jnp.where(row_index == col_index, 1.0, 0.0).astype(F32)
    strict = row_index > col_index
    upper = jnp.where(row_index <= col_index, 1.0, 0.0).astype(BF16)
    nothing = jnp.zeros((BLOCK, HEAD_DIM), F32)
    for h in range(share):
        state_ref[h] = beside(nothing, eye)

    def leaving(kind, n):
        at = pl.ds(pl.multiple_of(n * BLOCK, BLOCK), BLOCK)
        source, target = ((solved_ref, solved_out), (before_ref, state_out))[kind]
        return pltpu.make_async_copy(source.at[:, at, :], target.at[:, at, :], sems.at[kind, n])

    def leaving_flip(n):
        return pltpu.make_async_copy(flip_ref.at[n], flip_out.at[n], sems.at[2, n])

    def chunk(number, carry):
        steps = []
        for step in range(per_chunk // per_step):
            blocks = [number * per_chunk + step * per_step + b for b in range(per_step)]
            steps.append(dict(blocks=blocks, slot=step * per_step * tiles))

        def prepare(work):
            blocks = work["blocks"]
            lane = lax.broadcasted_iota(jnp.int32, (16, BLOCK), 1)
            work["line"], work["beta"], work["end"], work["keys"], work["values"] = {}, {}, {}, {}, {}
            work["system"], work["inverse"], work["grow"] = {}, {}, {}
            for b, n in enumerate(blocks):
                picked = []
                for half in range(2):
                    place = meta_ref[2 * n + half]
                    found = recv_ref[place // 2, gate_row : gate_row + 16, :].astype(F32)
                    turned = pltpu.roll(found, piece_rows, 1)
                    picked.append(jnp.where(place % 2 == half, found, turned))
                logits = jnp.where(lane < piece_rows, picked[0], picked[1])
                beta = 1.0 / (1.0 + jnp.exp(-logits[0:8]))
                decay = -jnp.exp(rate_ref[0]) * softplus(logits[8:16] + rate_ref[1])
                high = decay.astype(BF16)
                remain = decay - high.astype(F32)
                middle = remain.astype(BF16)
                low = (remain - middle.astype(F32)).astype(BF16)
                stacked = below(high.astype(F32), middle.astype(F32), low.astype(F32))
                stacked = below(stacked, jnp.zeros((8, BLOCK), F32)).astype(BF16)
                sums = dot(stacked, upper)
                cum = sums[0:8] + sums[8:16] + sums[16:24]
                row_out[0, n] = cum
                row_out[1, n] = beta
                work["line"][b], work["beta"][b] = cum, beta
                work["end"][b] = jnp.broadcast_to(cum[:, BLOCK - 1 :], (8, BLOCK))
                yield
            for b, n in enumerate(blocks):
                for tile in range(tiles):
                    slot = work["slot"] + b * tiles + tile
                    lead = jnp.where(is_first == 1, 0.0, tail_ref[tile].astype(F32))
                    shifted_rows(meta_ref, recv_ref, rows_ref, slot, lead, n, tile * BLOCK)
                    active = convolved(rows_ref, slot, weight_ref, tile)
                    if tile == 0:
                        work["keys"][b] = active * unit_scale(active)
                    else:
                        work["values"][b, tile - 1] = active
                    yield
                turned = work["keys"][b].T
                flip_ref[n] = turned
                leaving_flip(n).start()
                gram = narrow_product(split(work["keys"][b]), split(turned))
                yield
                columns = below(work["line"][b], jnp.zeros((BLOCK - 8, BLOCK), F32)).T
                for h in range(share):
                    at = group * share + h
                    column = jnp.broadcast_to(columns[:, at : at + 1], (BLOCK, BLOCK))
                    decay = jnp.exp(jnp.where(strict, column - work["line"][b][at : at + 1], 0.0))
                    work["grow"][b, h] = jnp.exp(column)
                    scaled = decay * work["beta"][b][at : at + 1]
                    lower = jnp.where(strict, gram * scaled, 0.0)
                    work["system"][b, h] = split(lower)
                    work["inverse"][b, h] = eye - jnp.where(differ == 1, lower, 0.0)
                    yield

        def invert(work):
            inverse, system = work["inverse"], work["system"]
            for place, size in enumerate(LEVELS):
                mask = mask_ref[place]
                halves, cross = {}, {}
                for u in inverse:
                    halves[u] = split(inverse[u])
                    parts = (system[u][0] * mask, system[u][1] * mask)
                    cross[u] = split(narrow_product(parts, halves[u]))
                    yield
                for u in inverse:
                    inverse[u] = inverse[u] - narrow_product(halves[u], cross[u])
                    yield

        def advance(work):
            blocks = work["blocks"]
            solved, shift, over, keep = {}, {}, {}, {}
            for b, n in enumerate(blocks):
                at = pl.ds(pl.multiple_of(n * BLOCK, BLOCK), BLOCK)
                for h in range(share):
                    row = group * share + h
                    right = split(beside(work["values"][b, h], work["keys"][b] * work["grow"][b, h]))
                    found = wide_product(split(work["inverse"][b, h]), right)
                    solved_ref[h, at, :] = found
                    solved[b, h] = split(found)
                    yield
                leaving(0, n).start()
            for b, n in enumerate(blocks):
                for h in range(share):
                    row = group * share + h
                    end, line = work["end"][b][row : row + 1], work["line"][b][row : row + 1]
                    weight = jnp.exp(end - line) * work["beta"][b][row : row + 1]
                    moved = wide_product(split(flip_ref[n] * weight), solved[b, h])
                    shift[b, h] = moved[:, :HEAD_DIM]
                    over[b, h] = split(moved[:, HEAD_DIM:])
                    keep[b, h] = beside(jnp.exp(end), jnp.exp(end))
                    yield
            for b, n in enumerate(blocks):
                at = pl.ds(pl.multiple_of(n * BLOCK, BLOCK), BLOCK)
                for h in range(share):
                    state = state_ref[h]
                    before_ref[h, at, :] = state
                    moved = wide_product(over[b, h], split(state))
                    state_ref[h] = state * keep[b, h] + beside(shift[b, h], nothing) - moved
                    yield
                leaving(1, n).start()

        together(prepare(steps[0]))
        for place, work in enumerate(steps):
            streams = [invert(work)]
            if place + 1 < len(steps):
                streams.append(prepare(steps[place + 1]))
            if place:
                streams.append(advance(steps[place - 1]))
            together(*streams)
        together(advance(steps[-1]))
        return carry

    if count == per_chunk:
        chunk(0, 0)
    else:
        lax.fori_loop(0, count // per_chunk, chunk, 0)
    for h in range(share):
        shift_ref[h] = state_ref[h, :, :HEAD_DIM]
        over = jnp.where(is_first == 1, 0.0, state_ref[h, :, HEAD_DIM:])
        map_high, map_low = split(over)
        map_ref[h] = beside(map_high, map_low)

    def drain(n, carry):
        leaving(0, n).wait()
        leaving(1, n).wait()
        leaving_flip(n).wait()
        return carry

    lax.fori_loop(0, count, drain, 0)


def advance_kernel(shift_ref, map_ref, incoming_ref, out_ref):
    for h in range(shift_ref.shape[0]):
        high, low = split(incoming_ref[h])
        row = beside(high, low)
        both = dot(map_ref[h], below(row, row))
        out_ref[h] = shift_ref[h] + both[:, :HEAD_DIM] + both[:, HEAD_DIM:]


def finish_kernel(
    dims,
    meta_ref,
    recv_ref,
    tail_ref,
    weight_ref,
    row_ref,
    incoming_ref,
    gain_ref,
    solved_in,
    state_in,
    flip_in,
    out_ref,
    solved_ref,
    before_ref,
    flip_ref,
    rows_ref,
    sems,
):
    group, share, count, per_step, query_row, gate_row = dims
    piece_rows = BLOCK // 2
    is_first = meta_ref[meta_ref.shape[0] - 1]
    row_index = lax.broadcasted_iota(jnp.int32, (BLOCK, BLOCK), 0)
    col_index = lax.broadcasted_iota(jnp.int32, (BLOCK, BLOCK), 1)
    inclusive = row_index >= col_index

    def arriving(n):
        at = pl.ds(pl.multiple_of(n * BLOCK, BLOCK), BLOCK)
        return (
            pltpu.make_async_copy(flip_in.at[n], flip_ref.at[n], sems.at[0, n]),
            pltpu.make_async_copy(state_in.at[:, at, :], before_ref.at[:, at, :], sems.at[1, n]),
            pltpu.make_async_copy(solved_in.at[:, at, :], solved_ref.at[:, at, :], sems.at[2, n]),
        )

    def fetch(n, carry):
        for copy in arriving(n):
            copy.start()
        return carry

    lax.fori_loop(0, count, fetch, 0)
    entry = [split(jnp.where(is_first == 1, 0.0, incoming_ref[h])) for h in range(share)]

    def step(index, carry):
        blocks = [index * per_step + b for b in range(per_step)]
        queries, grams = {}, {}
        for b, n in enumerate(blocks):
            lead = jnp.where(is_first == 1, 0.0, tail_ref[0].astype(F32))
            shifted_rows(meta_ref, recv_ref, rows_ref, b, lead, n, query_row)
            active = convolved(rows_ref, b, weight_ref, 0)
            queries[b] = active * (unit_scale(active) * HEAD_DIM ** (-0.5))
        for n in blocks:
            for copy in arriving(n):
                copy.wait()
        for b, n in enumerate(blocks):
            grams[b] = narrow_product(split(queries[b]), split(flip_ref[n]))
        units = [(b, h) for b in range(per_step) for h in range(share)]
        lefts, states, fresh = {}, {}, {}
        for b, h in units:
            n = blocks[b]
            at = group * share + h
            cum, beta = row_ref[0, n], row_ref[1, n]
            columns = below(cum, jnp.zeros((BLOCK - 8, BLOCK), F32)).T
            column = jnp.broadcast_to(columns[:, at : at + 1], (BLOCK, BLOCK))
            decay = jnp.exp(jnp.where(inclusive, column - cum[at : at + 1], 0.0))
            attend = jnp.where(inclusive, grams[b] * decay * beta[at : at + 1], 0.0)
            q_high, q_low = split(queries[b] * jnp.exp(column))
            a_high, a_low = split(attend)
            lefts[b, h] = (beside(q_high, a_high), beside(q_low, a_low))
        for b, h in units:
            rows = pl.ds(pl.multiple_of(blocks[b] * BLOCK, BLOCK), BLOCK)
            shift = before_ref[h, rows, :HEAD_DIM]
            over = split(before_ref[h, rows, HEAD_DIM:])
            states[b, h] = split(shift + narrow_product(over, entry[h]))
        for b, h in units:
            rows = pl.ds(pl.multiple_of(blocks[b] * BLOCK, BLOCK), BLOCK)
            px = split(solved_ref[h, rows, HEAD_DIM:])
            ux = solved_ref[h, rows, :HEAD_DIM]
            fresh[b, h] = split(ux - narrow_product(px, states[b, h]))
        for b, h in units:
            n = blocks[b]
            right = below(beside(*states[b, h]), beside(*fresh[b, h]))
            both = dot(lefts[b, h][0], right) + dot(lefts[b, h][1], right)
            core = both[:, :HEAD_DIM] + both[:, HEAD_DIM:]
            scale = lax.rsqrt(jnp.mean(core * core, axis=-1, keepdims=True) + 1e-06)
            gates = []
            for half in range(2):
                place = meta_ref[2 * n + half]
                start = gate_row + h * BLOCK + (place % 2) * piece_rows
                start = pl.multiple_of(start, piece_rows)
                gates.append(recv_ref[place // 2, pl.ds(start, piece_rows), :].astype(F32))
            gate = below(*gates)
            result = core * scale * gain_ref[...] * silu(gate)
            out_ref[n, h * BLOCK : (h + 1) * BLOCK, :] = result.astype(BF16)
        return carry

    lax.fori_loop(0, count // per_step, step, 0)


def gather_kernel(moves, source_count, logit_place, *refs):
    sources, refs = refs[:source_count], refs[source_count:]
    if logit_place:
        logit_ref, out_ref, sems, wide_ref = refs
    else:
        out_ref, sems = refs
    copies = []
    for number, (source, begin, length, column, place, row) in enumerate(moves):
        copies.append(
            pltpu.make_async_copy(
                sources[source].at[pl.ds(begin, length), pl.ds(column, HEAD_DIM)],
                out_ref.at[place, pl.ds(row, length), :],
                sems.at[number],
            )
        )
    for copy in copies:
        copy.start()
    if logit_place:
        first_row, heads = logit_place
        wide_ref[...] = jnp.zeros(wide_ref.shape, F32)
        wide_ref[0 : 2 * VALUE_HEADS, :] = logit_ref[...].astype(F32)
        for place in range(out_ref.shape[0]):
            begin = place * heads
            rates = wide_ref[begin : begin + 8, :]
            steps = wide_ref[VALUE_HEADS + begin : VALUE_HEADS + begin + 8, :]
            out_ref[place, first_row : first_row + 16, :] = below(rates, steps).astype(BF16)
    for copy in copies:
        copy.wait()


def halo_kernel(total, rows, meta_ref, arrived_ref, out_ref, sems):
    last = meta_ref[meta_ref.shape[0] - 2]
    copies = []
    for tile in range(total):
        source = arrived_ref.at[last // 2, pl.ds(tile * rows + rows - 16, 16), :]
        copies.append(pltpu.make_async_copy(source, out_ref.at[tile], sems.at[tile]))
    for copy in copies:
        copy.start()
    for copy in copies:
        copy.wait()


def scatter_kernel(moves, *refs):
    source_ref, out_ref, sems = refs[0], refs[-2], refs[-1]
    copies = []
    for number, (place, row, length, column) in enumerate(moves):
        copies.append(
            pltpu.make_async_copy(
                source_ref.at[place, pl.ds(row, length), :],
                out_ref.at[:, pl.ds(column, HEAD_DIM)],
                sems.at[number],
            )
        )
    for copy in copies:
        copy.start()
    for copy in copies:
        copy.wait()


MIB = 2**20
GATHER_MIB = 6
INNER_MIB = 24
FINISH_MIB = 20


def limits(mib):
    return pltpu.CompilerParams(vmem_limit_bytes=mib * MIB)


def cost(flops):
    return pl.CostEstimate(flops=int(flops), bytes_accessed=2**20, transcendentals=0)


vmem = pl.BlockSpec(memory_space=pltpu.VMEM)
smem = pl.BlockSpec(memory_space=pltpu.SMEM)
anywhere = pl.BlockSpec(memory_space=pl.ANY)
stored = pl.BlockSpec(memory_space=pltpu.HBM)


def gather(sources, moves, places, rows, logits=None, first_row=0, heads=0):
    operands, in_specs = list(sources), [anywhere] * len(sources)
    scratch = [pltpu.SemaphoreType.DMA((len(moves),))]
    logit_place = None
    if logits is not None:
        operands.append(logits)
        in_specs.append(vmem)
        scratch.append(pltpu.VMEM((2 * VALUE_HEADS + 8, logits.shape[1]), F32))
        logit_place = (first_row, heads)
    return pl.pallas_call(
        functools.partial(gather_kernel, tuple(moves), len(sources), logit_place),
        out_shape=jax.ShapeDtypeStruct((places, rows, HEAD_DIM), BF16),
        in_specs=in_specs,
        out_specs=vmem,
        scratch_shapes=scratch,
        compiler_params=limits(GATHER_MIB),
        cost_estimate=cost(8e8),
    )(*operands)


def scatter(source, moves, out_shape, base=None):
    operands, in_specs, aliases = [source], [vmem], {}
    if base is not None:
        operands.append(base)
        in_specs.append(anywhere)
        aliases = {1: 0}
    return pl.pallas_call(
        functools.partial(scatter_kernel, tuple(moves)),
        out_shape=jax.ShapeDtypeStruct(out_shape, BF16),
        in_specs=in_specs,
        out_specs=anywhere,
        scratch_shapes=[pltpu.SemaphoreType.DMA((len(moves),))],
        input_output_aliases=aliases,
        compiler_params=limits(4),
        cost_estimate=cost(8e8),
    )(*operands)


def passed_round(value, axis):
    length = lax.axis_size(axis)
    return lax.ppermute(value, axis, [(i, (i + 1) % length) for i in range(length)])


def exchanged(value):
    return lax.all_to_all(value, "cp", split_axis=0, concat_axis=0, tiled=True)


def per_device(mixed_qkv, gate_z, gate_logits, block_table, conv_weight, a_log, dt_bias, norm_gain):
    cp_count = lax.axis_size("cp")
    seg_count = lax.axis_size("seg")
    cp_place = lax.axis_index("cp")
    rows = mixed_qkv.shape[0]
    heads = VALUE_HEADS // cp_count
    groups = max(1, heads // GROUP)
    share = heads // groups
    tiles = 1 + share
    key_width = KEY_HEADS * HEAD_DIM
    count = cp_count * rows // BLOCK
    gate_row = tiles * BLOCK

    order = jnp.argsort(block_table[0]).astype(jnp.int32)
    is_first = (lax.axis_index("seg") == 0).astype(jnp.int32).reshape(1)
    meta = jnp.concatenate([order, is_first])

    def key_head(place, group):
        return (place * heads + group * share) // GROUP

    def inner_moves(group):
        moves = []
        for place in range(cp_count):
            found = [key_width + key_head(place, group) * HEAD_DIM]
            for h in range(share):
                found.append(2 * key_width + (place * heads + group * share + h) * HEAD_DIM)
            for tile, column in enumerate(found):
                moves.append((0, 0, rows, column, place, tile * rows))
        return moves

    def outer_moves():
        moves = []
        for place in range(cp_count):
            for group in range(groups):
                moves.append((0, 0, rows, key_head(place, group) * HEAD_DIM, place, group * rows))
            for h in range(heads):
                moves.append((1, 0, rows, (place * heads + h) * HEAD_DIM, place, (groups + h) * rows))
        return moves

    def halo(arrived, total):
        found = pl.pallas_call(
            functools.partial(halo_kernel, total, rows),
            out_shape=jax.ShapeDtypeStruct((total, 16, HEAD_DIM), BF16),
            in_specs=[smem, anywhere],
            out_specs=vmem,
            scratch_shapes=[pltpu.SemaphoreType.DMA((total,))],
            compiler_params=limits(2),
            cost_estimate=cost(1e8),
        )(meta, arrived)
        return passed_round(found, "seg")

    received, tails = [], []
    for group in range(groups):
        sent = gather(
            [mixed_qkv],
            inner_moves(group),
            cp_count,
            gate_row + 16,
            logits=gate_logits.T,
            first_row=gate_row,
            heads=heads,
        )
        received.append(exchanged(sent))
        tails.append(halo(received[group], tiles))

    packed = gather([mixed_qkv, gate_z], outer_moves(), cp_count, (groups + heads) * rows)
    outer = exchanged(packed)
    outer_tail = halo(outer, groups)

    shaped = conv_weight.reshape(CONV, -1, HEAD_DIM)

    def taps(first, total):
        return lax.dynamic_slice_in_dim(shaped, first, total, 1).transpose(1, 0, 2)

    weights, query_weights = [], []
    for group in range(groups):
        own_key = key_head(cp_place, group)
        own_value = 2 * KEY_HEADS + cp_place * heads + group * share
        query_weights.append(taps(own_key, 1))
        weights.append(
            jnp.concatenate([taps(KEY_HEADS + own_key, 1), taps(own_value, share)], axis=0)
        )
    head_log = lax.dynamic_slice_in_dim(a_log, cp_place * heads, heads, 0)
    head_bias = lax.dynamic_slice_in_dim(dt_bias, cp_place * heads, heads, 0)
    rates = jnp.pad(jnp.stack([head_log, head_bias]), ((0, 0), (0, 8 - heads)))
    rates = jnp.broadcast_to(rates[:, :, None], (2, 8, BLOCK))

    per_step = min(4, count)
    per_chunk = min(8, count)

    def inner(group):
        dims = (group, share, count, per_step, per_chunk)
        wide = (share, count * BLOCK, 2 * HEAD_DIM)
        return pl.pallas_call(
            functools.partial(inner_kernel, dims),
            out_shape=(
                pltpu.HBM(wide, F32),
                pltpu.HBM(wide, F32),
                pltpu.HBM((count, HEAD_DIM, BLOCK), F32),
                jax.ShapeDtypeStruct((2, count, 8, BLOCK), F32),
                jax.ShapeDtypeStruct((share, HEAD_DIM, HEAD_DIM), F32),
                jax.ShapeDtypeStruct((share, HEAD_DIM, 2 * HEAD_DIM), BF16),
            ),
            in_specs=[smem] + [vmem] * 4,
            out_specs=(stored, stored, stored, vmem, vmem, vmem),
            scratch_shapes=[
                pltpu.VMEM(wide, F32),
                pltpu.VMEM(wide, F32),
                pltpu.VMEM((count, HEAD_DIM, BLOCK), F32),
                pltpu.VMEM((per_chunk * tiles, 8 + BLOCK, HEAD_DIM), F32),
                pltpu.VMEM((len(LEVELS), BLOCK, BLOCK), BF16),
                pltpu.VMEM((share, HEAD_DIM, 2 * HEAD_DIM), F32),
                pltpu.SemaphoreType.DMA((3, count)),
            ],
            compiler_params=limits(INNER_MIB),
            cost_estimate=cost(6e8 * count * share),
        )(meta, received[group], tails[group], weights[group], rates)

    def chain(shift, over):
        incoming = None
        for rounds in range(seg_count - 1):
            advanced = shift
            if rounds:
                advanced = pl.pallas_call(
                    advance_kernel,
                    out_shape=jax.ShapeDtypeStruct(shift.shape, F32),
                    in_specs=[vmem] * 3,
                    out_specs=vmem,
                    compiler_params=limits(3),
                    cost_estimate=cost(2e8),
                )(shift, over, incoming)
            incoming = passed_round(advanced, "seg")
        if incoming is None:
            incoming = jnp.zeros_like(shift)
        return incoming

    def finish(group, incoming, solved, before, flip, lines):
        dims = (group, share, count, per_step, group * rows, (groups + group * share) * rows)
        wide = (share, count * BLOCK, 2 * HEAD_DIM)
        return pl.pallas_call(
            functools.partial(finish_kernel, dims),
            out_shape=jax.ShapeDtypeStruct((count, share * BLOCK, HEAD_DIM), BF16),
            in_specs=[smem] + [vmem] * 6 + [stored] * 3,
            out_specs=vmem,
            scratch_shapes=[
                pltpu.VMEM(wide, F32),
                pltpu.VMEM(wide, F32),
                pltpu.VMEM((count, HEAD_DIM, BLOCK), F32),
                pltpu.VMEM((per_step, 8 + BLOCK, HEAD_DIM), F32),
                pltpu.SemaphoreType.DMA((3, count)),
            ],
            compiler_params=limits(FINISH_MIB),
            cost_estimate=cost(1.5e9),
        )(
            meta,
            outer,
            outer_tail[group : group + 1],
            query_weights[group],
            lines,
            incoming,
            norm_gain.reshape(1, HEAD_DIM),
            *[pltpu.with_memory_space_constraint(x, pltpu.HBM) for x in (solved, before, flip)],
        )

    result = None
    for group in range(groups):
        solved, before, flip, lines, shift, over = inner(group)
        incoming = chain(shift, over)
        done = finish(group, incoming, solved, before, flip, lines)
        swapped = exchanged(done)
        moves = [
            (place, h * rows, rows, (place * heads + group * share + h) * HEAD_DIM)
            for place in range(cp_count)
            for h in range(share)
        ]
        result = scatter(swapped, moves, (rows, VALUE_HEADS * HEAD_DIM), result)
    return result


def solution(mesh):
    return jax.shard_map(
        per_device,
        mesh=mesh,
        in_specs=(
            P(("seg", "cp"), None),
            P(("seg", "cp"), None),
            P(("seg", "cp"), None),
            P("seg", None),
            P(),
            P(),
            P(),
            P(),
        ),
        out_specs=P(("seg", "cp"), None),
        check_vma=False,
    )
```

time: 126 us -> 127 us (level)
  waiting for transfers between devices: 34.8 us -> 45.6 us
  matrix products: 3.56 us -> 0 us
  between operations: 3.08 us -> 0.42 us
  local copies, waits for them, and re-layouts: 10.5 us -> 8.91 us
  Pallas kernels: 40.4 us -> 39.1 us
    ppermute x7 -> x9, waiting for transfers between devices: 14.8 us -> 22.9 us  [passed_round(): lax.ppermute(value, axis, [(i, (i + 1) % length) for i in range(length)])]
    all_to_all x6 -> x5, starting transfers between devices: 25 us -> 19.9 us  [exchanged(): return lax.all_to_all(value, 'cp', split_axis=0, concat_axis=0, tiled=True)]
    ppermute x7 -> x9, starting transfers between devices: 6.79 us -> 10.6 us  [passed_round(): lax.ppermute(value, axis, [(i, (i + 1) % length) for i in range(length)])]
    dot_general x4 -> x0, matrix products: 3.56 us -> none  [chain(): jnp.einsum('hij,hjk->hik', reach_map, incoming, precision=highest)]
    all_to_all x6 -> x5, waiting for transfers between devices: 20 us -> 22.7 us  [exchanged(): return lax.all_to_all(value, 'cp', split_axis=0, concat_axis=0, tiled=True)]
    transpose x0 -> x2, local copies, waits for them, and re-layouts: none -> 1.45 us  [taps(): return lax.dynamic_slice_in_dim(shaped, first, total, 1).transpose(1, 0, 2)]
    dynamic_slice x2 -> x0, local copies, waits for them, and re-layouts: 1.45 us -> none  [the longest x1 0.73 us: group_weights(): lax.dynamic_slice_in_dim(shaped, key_head, 1, 1)]
    slice x4 -> x1, local copies, waits for them, and re-layouts: 1.3 us -> 0.01 us  [finish(): outer_tail[group:group + 1]]
  transfers between devices with their start and end apart: 13 -> 14, of which waited for: 5 -> 8; matrix products, arithmetic and copies ran while one was open for 6% -> 2% of each run, Pallas kernels for 30% -> 29%
where the time goes in v2:
time: 127 us; the launch traced here: 126 us
  waiting for transfers between devices  45.6 us (36%)
  Pallas kernels  39.1 us (31%)
  starting transfers between devices  30.6 us (24%)
  local copies, waits for them, and re-layouts  8.91 us (7%)
  other arithmetic  1.35 us (1%)
    ppermute x9, waiting for transfers between devices, passed_round(): lax.ppermute(value, axis, [(i, (i + 1) % length) for i in range(length)])  22.9 us
    all_to_all x5, waiting for transfers between devices, exchanged(): return lax.all_to_all(value, 'cp', split_axis=0, concat_axis=0, tiled=True)  22.7 us
    all_to_all x5, starting transfers between devices, exchanged(): return lax.all_to_all(value, 'cp', split_axis=0, concat_axis=0, tiled=True)  19.9 us
    pallas_call x2, Pallas kernels, inner(): pl.pallas_call(functools.partial(inner_kernel, dims), out_shape=(pltpu.HB...  19.1 us
    pallas_call x2, Pallas kernels, finish(): pl.pallas_call(functools.partial(finish_kernel, dims), out_shape=jax.Shap...  11.6 us
    ppermute x9, starting transfers between devices, passed_round(): lax.ppermute(value, axis, [(i, (i + 1) % length) for i in range(length)])  10.6 us
    unnamed x30, local copies, waits for them, and re-layouts  7.32 us
    pallas_call x3, Pallas kernels, gather(): pl.pallas_call(functools.partial(gather_kernel, tuple(moves), len(sources...  4 us
  transfers between devices with their start and end apart: 14, of which 8 were waited for; matrix products, arithmetic and copies ran while one was open for 2% of the time, Pallas kernels for 29%

profile of v2, /device:TPU:0, one launch (start us, length us, event | category | flops | bytes accessed | tf_op | source)
XLA Modules:
  0.0 126.0 jit_solution(6357355041353356628)
XLA Ops:
  0.0 1.6 %copy-done = bf16[128,8192]{1,0:T(8,128)(2,1)S(1)} copy-done((bf16[128,8192]{1,0:T(8,128)(2,1)S(1)}, bf16[128,8192]{1,0:T(8,128)(2,1)}, u32[]{:S(2)}) %copy-start) | copy-done | bytes 2097176
  1.6 0.7 copy-done.6
  2.3 1.4 %shard_map.90 = bf16[8,400,128]{2,1,0:T(8,128)(2,1)} custom-call(bf16[128,8192]{1,0:T(8,128)(2,1)S(1)} %copy-done, bf16[64,128]{1,0:T(8,128)(2,1)S(1)} %bitcast.23), custom_call_target="tpu_custom_call" | custom-call | flops 800000000 | bytes 1048576 | tf_op jit(solution)/shard_map/pallas_call | solution.py:482
  3.7 5.2 %all-to-all-start.3 = ((bf16[8,400,128]{2,1,0:T(8,128)(2,1)}), bf16[8,400,128]{2,1,0:T(8,128)(2,1)S(1)}, u32[]{:S(2)}, u32[]{:S(2)}) async-start(bf16[8,400,128]{2,1,0:T(8,128)(2,1)} %shard_map.90), calls=%async_computation.3 | async-start | bytes 1638400 | tf_op jit(solution)/shard_map/all_to_all | solution.py:517
  8.9 0.0 copy-done.14
  8.9 1.2 sort.17
  10.2 0.0 copy-done.7
  10.2 1.6 %copy-done.1 = bf16[128,8192]{1,0:T(8,128)(2,1)S(1)} copy-done((bf16[128,8192]{1,0:T(8,128)(2,1)S(1)}, bf16[128,8192]{1,0:T(8,128)(2,1)}, u32[]{:S(2)}) %copy-start.1) | copy-done | bytes 2097176
  11.8 0.5 shard_map.84
  12.3 0.0 copy-start.4
  12.3 0.9 copy-done.4
  13.2 8.7 %all-to-all-done.3.arrived_ref.recv_ref = bf16[8,400,128]{2,1,0:T(8,128)(2,1)S(1)} async-done(((bf16[8,400,128]{2,1,0:T(8,128)(2,1)}), bf16[8,400,128]{2,1,0:T(8,128)(2,1)S(1)}, u32[]{:S(2)}, u32[]{:S(2)}) %all-to-all-start.3) | async-done | bytes 819232 | tf_op jit(solution)/shard_map/all_to_all | solution.py:517
  21.8 3.5 %all-to-all-start.1 = ((bf16[8,400,128]{2,1,0:T(8,128)(2,1)}), bf16[8,400,128]{2,1,0:T(8,128)(2,1)S(1)}, u32[]{:S(2)}, u32[]{:S(2)}) async-start(bf16[8,400,128]{2,1,0:T(8,128)(2,1)} %copy-done.4), calls=%async_computation.1 | async-start | bytes 1638400 | tf_op jit(solution)/shard_map/all_to_all | solution.py:517
  25.4 0.1 pad_add_fusion.meta_ref
  25.5 0.0 copy-done.12
  25.5 0.0 copy-done.13
  25.5 0.1 dynamic-slice_bitcast_fusion.6
  25.6 0.7 dynamic-slice_bitcast_fusion
  26.3 0.7 dynamic-slice_bitcast_fusion.2
  27.0 0.6 shard_map.91
  27.6 1.6 %collective-permute-start.5 = (bf16[3,16,128]{2,1,0:T(8,128)(2,1)S(1)}, bf16[3,16,128]{2,1,0:T(8,128)(2,1)S(1)}, u32[]{:S(2)}, u32[]{:S(2)}) collective-permute-start(bf16[3,16,128]{2,1,0:T(8,128)(2,1)S(1)} %shard_map.91), channel_id=1, source_target_pairs={{0,8},{8,16},{16,24},{24,0},{1,9},{9,17},{17,25},{25,1},{2,10},{10... | collective-permute-start | bytes 36872 | tf_op jit(solution)/shard_map/ppermute | solution.py:513
  29.3 0.0 copy-done.3
  29.3 1.6 %copy-done.2 = bf16[128,8192]{1,0:T(8,128)(2,1)S(1)} copy-done((bf16[128,8192]{1,0:T(8,128)(2,1)S(1)}, bf16[128,8192]{1,0:T(8,128)(2,1)}, u32[]{:S(2)}) %copy-start.2) | copy-done | bytes 2097176
  30.9 2.1 %shard_map.82 = bf16[8,768,128]{2,1,0:T(8,128)(2,1)} custom-call(bf16[128,8192]{1,0:T(8,128)(2,1)S(1)} %copy-done.2, bf16[128,4096]{1,0:T(8,128)(2,1)S(1)} %copy-done.3), custom_call_target="tpu_custom_call" | custom-call | flops 800000000 | bytes 1048576 | tf_op jit(solution)/shard_map/pallas_call | solution.py:482
  33.0 5.3 %all-to-all-done.1.arrived_ref.recv_ref = bf16[8,400,128]{2,1,0:T(8,128)(2,1)S(1)} async-done(((bf16[8,400,128]{2,1,0:T(8,128)(2,1)}), bf16[8,400,128]{2,1,0:T(8,128)(2,1)S(1)}, u32[]{:S(2)}, u32[]{:S(2)}) %all-to-all-start.1) | async-done | bytes 819232 | tf_op jit(solution)/shard_map/all_to_all | solution.py:517
  38.3 3.6 %all-to-all-start = ((bf16[8,768,128]{2,1,0:T(8,128)(2,1)}), bf16[8,768,128]{2,1,0:T(8,128)(2,1)S(1)}, u32[]{:S(2)}, u32[]{:S(2)}) async-start(bf16[8,768,128]{2,1,0:T(8,128)(2,1)} %shard_map.82), calls=%async_computation | async-start | bytes 3145728 | tf_op jit(solution)/shard_map/all_to_all | solution.py:517
  41.8 0.0 collective-permute-done.5.tail_ref
  41.9 0.1 broadcast_in_dim.2.rate_ref
  41.9 9.6 %shard_map.92 = (f32[2,1024,256]{2,1,0:T(8,128)}, f32[2,1024,256]{2,1,0:T(8,128)}, f32[8,128,128]{2,1,0:T(8,128)}, f32[2,8,8,128]{3,2,1,0:T(8,128)S(1)}, f32[2,1...) custom-call(s32[17]{0:T(128)S(1)} %pad_add_fusion.meta_ref, ...), custom_call_target="tpu_custom_call" | custom-call | flops 9600000000 | bytes 1048576 | tf_op jit(solution)/shard_map/pallas_call | solution.py:613
  51.5 0.0 copy-start.10
  51.5 1.6 %collective-permute-start.6 = (f32[2,128,128]{2,1,0:T(8,128)S(1)}, f32[2,128,128]{2,1,0:T(8,128)S(1)}, u32[]{:S(2)}, u32[]{:S(2)}) collective-permute-start(f32[2,128,128]{2,1,0:T(8,128)S(1)} %get-tuple-element.26.shift_ref), channel_id=1, source_target_pairs={{0,8},{8,16},{16,24},{24,0},{1,9},{9,17},{17,25},{25,1},{2,10},{10... | collective-permute-start | bytes 393224 | tf_op jit(solution)/shard_map/ppermute | solution.py:513
  53.1 0.6 shard_map.85
  53.7 1.6 %collective-permute-start.1 = (bf16[3,16,128]{2,1,0:T(8,128)(2,1)S(1)}, bf16[3,16,128]{2,1,0:T(8,128)(2,1)S(1)}, u32[]{:S(2)}, u32[]{:S(2)}) collective-permute-start(bf16[3,16,128]{2,1,0:T(8,128)(2,1)S(1)} %shard_map.85), channel_id=1, source_target_pairs={{0,8},{8,16},{16,24},{24,0},{1,9},{9,17},{17,25},{25,1},{2,10},{10... | collective-permute-start | bytes 36872 | tf_op jit(solution)/shard_map/ppermute | solution.py:513
  55.4 4.0 %collective-permute-done.6.incoming_ref = f32[2,128,128]{2,1,0:T(8,128)S(1)} collective-permute-done((f32[2,128,128]{2,1,0:T(8,128)S(1)}, f32[2,128,128]{2,1,0:T(8,128)S(1)}, u32[]{:S(2)}, u32[]{:S(2)}) %collective-permute-start.6) | collective-permute-done | bytes 131104 | tf_op jit(solution)/shard_map/ppermute | solution.py:513
  59.4 0.2 shard_map.93
  59.6 0.2 collective-permute-start.7
  59.8 0.0 collective-permute-done.1.tail_ref
  59.8 9.6 %shard_map.86 = (f32[2,1024,256]{2,1,0:T(8,128)}, f32[2,1024,256]{2,1,0:T(8,128)}, f32[8,128,128]{2,1,0:T(8,128)}, f32[2,8,8,128]{3,2,1,0:T(8,128)S(1)}, f32[2,1...) custom-call(s32[17]{0:T(128)S(1)} %pad_add_fusion.meta_ref, ...), custom_call_target="tpu_custom_call" | custom-call | flops 9600000000 | bytes 1048576 | tf_op jit(solution)/shard_map/pallas_call | solution.py:613
  69.4 0.0 copy-start.5
  69.4 1.3 %collective-permute-start.2 = (f32[2,128,128]{2,1,0:T(8,128)S(1)}, f32[2,128,128]{2,1,0:T(8,128)S(1)}, u32[]{:S(2)}, u32[]{:S(2)}) collective-permute-start(f32[2,128,128]{2,1,0:T(8,128)S(1)} %get-tuple-element.20.shift_ref), channel_id=1, source_target_pairs={{0,8},{8,16},{16,24},{24,0},{1,9},{9,17},{17,25},{25,1},{2,10},{10... | collective-permute-start | bytes 393224 | tf_op jit(solution)/shard_map/ppermute | solution.py:513
  70.7 0.0 all-to-all-done.arrived_ref.recv_ref
  70.7 0.6 shard_map.83
  71.3 1.6 %collective-permute-start = (bf16[2,16,128]{2,1,0:T(8,128)(2,1)S(1)}, bf16[2,16,128]{2,1,0:T(8,128)(2,1)S(1)}, u32[]{:S(2)}, u32[]{:S(2)}) collective-permute-start(bf16[2,16,128]{2,1,0:T(8,128)(2,1)S(1)} %shard_map.83), channel_id=1, source_target_pairs={{0,8},{8,16},{16,24},{24,0},{1,9},{9,17},{17,25},{25,1},{2,10},{10... | collective-permute-start | bytes 24584 | tf_op jit(solution)/shard_map/ppermute | solution.py:513
  73.0 0.0 collective-permute-done.7.incoming_ref
  73.0 0.9 copy-done.11
  73.9 0.2 shard_map.94
  74.1 2.1 %collective-permute-start.8 = (f32[2,128,128]{2,1,0:T(8,128)S(1)}, f32[2,128,128]{2,1,0:T(8,128)S(1)}, u32[]{:S(2)}, u32[]{:S(2)}) collective-permute-start(f32[2,128,128]{2,1,0:T(8,128)S(1)} %shard_map.94), channel_id=1, source_target_pairs={{0,8},{8,16},{16,24},{24,0},{1,9},{9,17},{17,25},{25,1},{2,10},{10... | collective-permute-start | bytes 393224 | tf_op jit(solution)/shard_map/ppermute | solution.py:513
  76.2 0.6 collective-permute-done
  76.8 4.1 %collective-permute-done.8.incoming_ref = f32[2,128,128]{2,1,0:T(8,128)S(1)} collective-permute-done((f32[2,128,128]{2,1,0:T(8,128)S(1)}, f32[2,128,128]{2,1,0:T(8,128)S(1)}, u32[]{:S(2)}, u32[]{:S(2)}) %collective-permute-start.8) | collective-permute-done | bytes 131104 | tf_op jit(solution)/shard_map/ppermute | solution.py:513
  80.9 5.8 %shard_map.95 = bf16[8,256,128]{2,1,0:T(8,128)(2,1)} custom-call(s32[17]{0:T(128)S(1)} %pad_add_fusion.meta_ref, bf16[8,768,128]{2,1,0:T(8,128)(2,1)S(1)} %all-to-all-done.arrived_ref.recv_ref, bf16[1,16,128]{2,1,0:T(8,128)(2,1)S(1)} %get-tuple-element.37.tail_ref, f32[1,4,128]{2,1,0:T(4,128)S(1)} %get-tuple-element.32.weight_ref, ...), custom_call_target="tpu_custom_call" | custom-call | flops 1500000000 | bytes 1048576 | tf_op jit(solution)/shard_map/pallas_call | solution.py:659
  86.7 3.9 %all-to-all-start.4 = ((bf16[8,256,128]{2,1,0:T(8,128)(2,1)}), bf16[8,256,128]{2,1,0:T(8,128)(2,1)S(1)}, u32[]{:S(2)}, u32[]{:S(2)}) async-start(bf16[8,256,128]{2,1,0:T(8,128)(2,1)} %shard_map.95), calls=%async_computation.4 | async-start | bytes 1048576 | tf_op jit(solution)/shard_map/all_to_all | solution.py:517
  90.6 0.0 collective-permute-done.2.incoming_ref
  90.6 0.2 shard_map.87
  90.8 0.3 collective-permute-start.3
  91.2 7.4 %collective-permute-done.3.incoming_ref = f32[2,128,128]{2,1,0:T(8,128)S(1)} collective-permute-done((f32[2,128,128]{2,1,0:T(8,128)S(1)}, f32[2,128,128]{2,1,0:T(8,128)S(1)}, u32[]{:S(2)}, u32[]{:S(2)}) %collective-permute-start.3) | collective-permute-done | bytes 131104 | tf_op jit(solution)/shard_map/ppermute | solution.py:513
  98.6 0.2 shard_map.88
  98.8 0.1 collective-permute-start.4
  98.8 6.8 %collective-permute-done.4.incoming_ref = f32[2,128,128]{2,1,0:T(8,128)S(1)} collective-permute-done((f32[2,128,128]{2,1,0:T(8,128)S(1)}, f32[2,128,128]{2,1,0:T(8,128)S(1)}, u32[]{:S(2)}, u32[]{:S(2)}) %collective-permute-start.4) | collective-permute-done | bytes 131104 | tf_op jit(solution)/shard_map/ppermute | solution.py:513
  105.7 5.8 %shard_map.89 = bf16[8,256,128]{2,1,0:T(8,128)(2,1)} custom-call(s32[17]{0:T(128)S(1)} %pad_add_fusion.meta_ref, bf16[8,768,128]{2,1,0:T(8,128)(2,1)S(1)} %all-to-all-done.arrived_ref.recv_ref, bf16[1,16,128]{2,1,0:T(8,128)(2,1)S(1)} %get-tuple-element.38.tail_ref, f32[1,4,128]{2,1,0:T(4,128)S(1)} %get-tuple-element.34.weight_ref, ...), custom_call_target="tpu_custom_call" | custom-call | flops 1500000000 | bytes 1048576 | tf_op jit(solution)/shard_map/pallas_call | solution.py:659
  111.5 0.0 all-to-all-done.4.refs_0_
  111.5 3.7 %all-to-all-start.2 = ((bf16[8,256,128]{2,1,0:T(8,128)(2,1)}), bf16[8,256,128]{2,1,0:T(8,128)(2,1)S(1)}, u32[]{:S(2)}, u32[]{:S(2)}) async-start(bf16[8,256,128]{2,1,0:T(8,128)(2,1)} %shard_map.89), calls=%async_computation.2 | async-start | bytes 1048576 | tf_op jit(solution)/shard_map/all_to_all | solution.py:517
  115.2 0.9 shard_map.96.refs_1_
  116.1 8.8 %all-to-all-done.2.refs_0_ = bf16[8,256,128]{2,1,0:T(8,128)(2,1)S(1)} async-done(((bf16[8,256,128]{2,1,0:T(8,128)(2,1)}), bf16[8,256,128]{2,1,0:T(8,128)(2,1)S(1)}, u32[]{:S(2)}, u32[]{:S(2)}) %all-to-all-start.2) | async-done | bytes 524320 | tf_op jit(solution)/shard_map/all_to_all | solution.py:517
  124.9 0.9 shard_map.97
  (21 shorter events, 0.1 us)
Async XLA Ops:
  0.0 1.6 %copy-start = (bf16[128,8192]{1,0:T(8,128)(2,1)S(1)}, bf16[128,8192]{1,0:T(8,128)(2,1)}, u32[]{:S(2)}) copy-start(bf16[128,8192]{1,0:T(8,128)(2,1)} %refs_0_.5) | copy-start | bytes 6291460
  1.6 0.7 copy-start.6
  2.3 6.6 %copy-start.14 = (s32[1,16]{1,0:T(1,128)S(1)}, s32[1,16]{1,0:T(1,128)}, u32[]{:S(2)}) copy-start(s32[1,16]{1,0:T(1,128)} %param.11) | copy-start | bytes 196
  2.3 7.9 %copy-start.7 = (bf16[128,64]{0,1:T(8,128)(2,1)S(1)}, bf16[128,64]{0,1:T(8,128)(2,1)}, u32[]{:S(2)}) copy-start(bf16[128,64]{0,1:T(8,128)(2,1)} %param.10) | copy-start | bytes 49156
  3.7 18.1 %all-to-all-start.3 = ((bf16[8,400,128]{2,1,0:T(8,128)(2,1)}), bf16[8,400,128]{2,1,0:T(8,128)(2,1)S(1)}, u32[]{:S(2)}, u32[]{:S(2)}) async-start(bf16[8,400,128]{2,1,0:T(8,128)(2,1)} %shard_map.90), calls=%async_computation.3 | async-start | bytes 1638400 | tf_op jit(solution)/shard_map/all_to_all | solution.py:517
  10.2 1.6 %copy-start.1 = (bf16[128,8192]{1,0:T(8,128)(2,1)S(1)}, bf16[128,8192]{1,0:T(8,128)(2,1)}, u32[]{:S(2)}) copy-start(bf16[128,8192]{1,0:T(8,128)(2,1)} %refs_0_.5) | copy-start | bytes 6291460
  11.8 13.7 %copy-start.12 = (f32[32]{0:T(128)S(1)}, f32[32]{0:T(128)}, u32[]{:S(2)}) copy-start(f32[32]{0:T(128)} %param.14) | copy-start | bytes 388
  11.8 13.7 %copy-start.13 = (f32[32]{0:T(128)S(1)}, f32[32]{0:T(128)}, u32[]{:S(2)}) copy-start(f32[32]{0:T(128)} %param.13) | copy-start | bytes 388
  11.8 17.5 %copy-start.3 = (bf16[128,4096]{1,0:T(8,128)(2,1)S(1)}, bf16[128,4096]{1,0:T(8,128)(2,1)}, u32[]{:S(2)}) copy-start(bf16[128,4096]{1,0:T(8,128)(2,1)} %refs_1_.1) | copy-start | bytes 3145732
  12.3 0.9 copy-start.4
  21.8 16.4 %all-to-all-start.1 = ((bf16[8,400,128]{2,1,0:T(8,128)(2,1)}), bf16[8,400,128]{2,1,0:T(8,128)(2,1)S(1)}, u32[]{:S(2)}, u32[]{:S(2)}) async-start(bf16[8,400,128]{2,1,0:T(8,128)(2,1)} %copy-done.4), calls=%async_computation.1 | async-start | bytes 1638400 | tf_op jit(solution)/shard_map/all_to_all | solution.py:517
  27.6 14.2 %collective-permute-start.5 = (bf16[3,16,128]{2,1,0:T(8,128)(2,1)S(1)}, bf16[3,16,128]{2,1,0:T(8,128)(2,1)S(1)}, u32[]{:S(2)}, u32[]{:S(2)}) collective-permute-start(bf16[3,16,128]{2,1,0:T(8,128)(2,1)S(1)} %shard_map.91), channel_id=1, source_target_pairs={{0,8},{8,16},{16,24},{24,0},{1,9},{9,17},{17,25},{25,1},{2,10},{10... | collective-permute-start | bytes 36872 | tf_op jit(solution)/shard_map/ppermute | solution.py:513
  29.3 1.6 %copy-start.2 = (bf16[128,8192]{1,0:T(8,128)(2,1)S(1)}, bf16[128,8192]{1,0:T(8,128)(2,1)}, u32[]{:S(2)}) copy-start(bf16[128,8192]{1,0:T(8,128)(2,1)} %refs_0_.5) | copy-start | bytes 6291460
  38.3 32.5 %all-to-all-start = ((bf16[8,768,128]{2,1,0:T(8,128)(2,1)}), bf16[8,768,128]{2,1,0:T(8,128)(2,1)S(1)}, u32[]{:S(2)}, u32[]{:S(2)}) async-start(bf16[8,768,128]{2,1,0:T(8,128)(2,1)} %shard_map.82), calls=%async_computation | async-start | bytes 3145728 | tf_op jit(solution)/shard_map/all_to_all | solution.py:517
  51.5 17.9 %copy-start.10 = (bf16[2,128,256]{2,1,0:T(8,128)(2,1)}, bf16[2,128,256]{2,1,0:T(8,128)(2,1)S(1)}, u32[]{:S(2)}) copy-start(bf16[2,128,256]{2,1,0:T(8,128)(2,1)S(1)} %get-tuple-element.27.map_ref) | copy-start | bytes 393220
  51.5 7.9 %collective-permute-start.6 = (f32[2,128,128]{2,1,0:T(8,128)S(1)}, f32[2,128,128]{2,1,0:T(8,128)S(1)}, u32[]{:S(2)}, u32[]{:S(2)}) collective-permute-start(f32[2,128,128]{2,1,0:T(8,128)S(1)} %get-tuple-element.26.shift_ref), channel_id=1, source_target_pairs={{0,8},{8,16},{16,24},{24,0},{1,9},{9,17},{17,25},{25,1},{2,10},{10... | collective-permute-start | bytes 393224 | tf_op jit(solution)/shard_map/ppermute | solution.py:513
  53.7 6.1 %collective-permute-start.1 = (bf16[3,16,128]{2,1,0:T(8,128)(2,1)S(1)}, bf16[3,16,128]{2,1,0:T(8,128)(2,1)S(1)}, u32[]{:S(2)}, u32[]{:S(2)}) collective-permute-start(bf16[3,16,128]{2,1,0:T(8,128)(2,1)S(1)} %shard_map.85), channel_id=1, source_target_pairs={{0,8},{8,16},{16,24},{24,0},{1,9},{9,17},{17,25},{25,1},{2,10},{10... | collective-permute-start | bytes 36872 | tf_op jit(solution)/shard_map/ppermute | solution.py:513
  59.6 13.4 %collective-permute-start.7 = (f32[2,128,128]{2,1,0:T(8,128)S(1)}, f32[2,128,128]{2,1,0:T(8,128)S(1)}, u32[]{:S(2)}, u32[]{:S(2)}) collective-permute-start(f32[2,128,128]{2,1,0:T(8,128)S(1)} %shard_map.93), channel_id=1, source_target_pairs={{0,8},{8,16},{16,24},{24,0},{1,9},{9,17},{17,25},{25,1},{2,10},{10... | collective-permute-start | bytes 393224 | tf_op jit(solution)/shard_map/ppermute | solution.py:513
  69.4 3.6 %copy-start.8 = (bf16[2,128,256]{2,1,0:T(8,128)(2,1)}, bf16[2,128,256]{2,1,0:T(8,128)(2,1)S(1)}, u32[]{:S(2)}) copy-start(bf16[2,128,256]{2,1,0:T(8,128)(2,1)S(1)} %get-tuple-element.21.map_ref) | copy-start | bytes 393220
  69.4 11.5 %copy-start.5 = (f32[128]{0:T(128)S(1)}, f32[128]{0:T(128)}, u32[]{:S(2)}) copy-start(f32[128]{0:T(128)} %param.15) | copy-start | bytes 1540
  69.4 21.2 %collective-permute-start.2 = (f32[2,128,128]{2,1,0:T(8,128)S(1)}, f32[2,128,128]{2,1,0:T(8,128)S(1)}, u32[]{:S(2)}, u32[]{:S(2)}) collective-permute-start(f32[2,128,128]{2,1,0:T(8,128)S(1)} %get-tuple-element.20.shift_ref), channel_id=1, source_target_pairs={{0,8},{8,16},{16,24},{24,0},{1,9},{9,17},{17,25},{25,1},{2,10},{10... | collective-permute-start | bytes 393224 | tf_op jit(solution)/shard_map/ppermute | solution.py:513
  71.3 5.5 %collective-permute-start = (bf16[2,16,128]{2,1,0:T(8,128)(2,1)S(1)}, bf16[2,16,128]{2,1,0:T(8,128)(2,1)S(1)}, u32[]{:S(2)}, u32[]{:S(2)}) collective-permute-start(bf16[2,16,128]{2,1,0:T(8,128)(2,1)S(1)} %shard_map.83), channel_id=1, source_target_pairs={{0,8},{8,16},{16,24},{24,0},{1,9},{9,17},{17,25},{25,1},{2,10},{10... | collective-permute-start | bytes 24584 | tf_op jit(solution)/shard_map/ppermute | solution.py:513
  73.0 0.9 copy-start.11
  74.1 6.8 %collective-permute-start.8 = (f32[2,128,128]{2,1,0:T(8,128)S(1)}, f32[2,128,128]{2,1,0:T(8,128)S(1)}, u32[]{:S(2)}, u32[]{:S(2)}) collective-permute-start(f32[2,128,128]{2,1,0:T(8,128)S(1)} %shard_map.94), channel_id=1, source_target_pairs={{0,8},{8,16},{16,24},{24,0},{1,9},{9,17},{17,25},{25,1},{2,10},{10... | collective-permute-start | bytes 393224 | tf_op jit(solution)/shard_map/ppermute | solution.py:513
  80.9 9.7 %copy-start.9 = (bf16[2,128,256]{2,1,0:T(8,128)(2,1)S(1)}, bf16[2,128,256]{2,1,0:T(8,128)(2,1)}, u32[]{:S(2)}) copy-start(bf16[2,128,256]{2,1,0:T(8,128)(2,1)} %copy-done.8) | copy-start | bytes 393220
  86.7 24.7 %all-to-all-start.4 = ((bf16[8,256,128]{2,1,0:T(8,128)(2,1)}), bf16[8,256,128]{2,1,0:T(8,128)(2,1)S(1)}, u32[]{:S(2)}, u32[]{:S(2)}) async-start(bf16[8,256,128]{2,1,0:T(8,128)(2,1)} %shard_map.95), calls=%async_computation.4 | async-start | bytes 1048576 | tf_op jit(solution)/shard_map/all_to_all | solution.py:517
  90.8 7.8 %collective-permute-start.3 = (f32[2,128,128]{2,1,0:T(8,128)S(1)}, f32[2,128,128]{2,1,0:T(8,128)S(1)}, u32[]{:S(2)}, u32[]{:S(2)}) collective-permute-start(f32[2,128,128]{2,1,0:T(8,128)S(1)} %shard_map.87), channel_id=1, source_target_pairs={{0,8},{8,16},{16,24},{24,0},{1,9},{9,17},{17,25},{25,1},{2,10},{10... | collective-permute-start | bytes 393224 | tf_op jit(solution)/shard_map/ppermute | solution.py:513
  98.8 6.9 %collective-permute-start.4 = (f32[2,128,128]{2,1,0:T(8,128)S(1)}, f32[2,128,128]{2,1,0:T(8,128)S(1)}, u32[]{:S(2)}, u32[]{:S(2)}) collective-permute-start(f32[2,128,128]{2,1,0:T(8,128)S(1)} %shard_map.88), channel_id=1, source_target_pairs={{0,8},{8,16},{16,24},{24,0},{1,9},{9,17},{17,25},{25,1},{2,10},{10... | collective-permute-start | bytes 393224 | tf_op jit(solution)/shard_map/ppermute | solution.py:513
  111.5 13.5 %all-to-all-start.2 = ((bf16[8,256,128]{2,1,0:T(8,128)(2,1)}), bf16[8,256,128]{2,1,0:T(8,128)(2,1)S(1)}, u32[]{:S(2)}, u32[]{:S(2)}) async-start(bf16[8,256,128]{2,1,0:T(8,128)(2,1)} %shard_map.89), calls=%async_computation.2 | async-start | bytes 1048576 | tf_op jit(solution)/shard_map/all_to_all | solution.py:517

commit v3 on v2

--- a/solution.py
+++ b/solution.py
@@ -98,28 +98,19 @@
     return lax.rsqrt(jnp.sum(matrix * matrix, axis=-1, keepdims=True) + 1e-06)
 
 
-def inner_kernel(
-    dims,
-    meta_ref,
-    recv_ref,
-    tail_ref,
-    weight_ref,
-    rate_ref,
-    solved_out,
-    state_out,
-    flip_out,
-    row_out,
-    shift_ref,
-    map_ref,
-    solved_ref,
-    before_ref,
-    flip_ref,
-    rows_ref,
-    mask_ref,
-    state_ref,
-    sems,
-):
-    group, share, count, per_step, per_chunk = dims
+def inner_kernel(dims, meta_ref, recv_ref, tail_ref, weight_ref, rate_ref, *refs):
+    group, share, first_block, count, per_step, per_chunk, last_part = dims
+    if first_block:
+        given_ref = refs[0]
+        refs = refs[4:]
+    else:
+        given_ref = None
+    solved_out, state_out, flip_out, row_out, refs = *refs[:4], refs[4:]
+    if last_part:
+        shift_ref, map_ref, refs = *refs[:2], refs[2:]
+    else:
+        final_ref, refs = refs[0], refs[1:]
+    solved_ref, before_ref, flip_ref, rows_ref, mask_ref, state_ref, sems = refs
     tiles = 1 + share
     gate_row = tiles * BLOCK
     piece_rows = BLOCK // 2
@@ -136,15 +127,16 @@
     upper = jnp.where(row_index <= col_index, 1.0, 0.0).astype(BF16)
     nothing = jnp.zeros((BLOCK, HEAD_DIM), F32)
     for h in range(share):
-        state_ref[h] = beside(nothing, eye)
+        state_ref[h] = beside(nothing, eye) if given_ref is None else given_ref[h]
 
     def leaving(kind, n):
-        at = pl.ds(pl.multiple_of(n * BLOCK, BLOCK), BLOCK)
+        here = pl.ds(pl.multiple_of(n * BLOCK, BLOCK), BLOCK)
+        there = pl.ds(pl.multiple_of((first_block + n) * BLOCK, BLOCK), BLOCK)
         source, target = ((solved_ref, solved_out), (before_ref, state_out))[kind]
-        return pltpu.make_async_copy(source.at[:, at, :], target.at[:, at, :], sems.at[kind, n])
+        return pltpu.make_async_copy(source.at[:, here, :], target.at[:, there, :], sems.at[kind, n])
 
     def leaving_flip(n):
-        return pltpu.make_async_copy(flip_ref.at[n], flip_out.at[n], sems.at[2, n])
+        return pltpu.make_async_copy(flip_ref.at[n], flip_out.at[first_block + n], sems.at[2, n])
 
     def chunk(number, carry):
         steps = []
@@ -160,7 +152,7 @@
             for b, n in enumerate(blocks):
                 picked = []
                 for half in range(2):
-                    place = meta_ref[2 * n + half]
+                    place = meta_ref[2 * (first_block + n) + half]
                     found = recv_ref[place // 2, gate_row : gate_row + 16, :].astype(F32)
                     turned = pltpu.roll(found, piece_rows, 1)
                     picked.append(jnp.where(place % 2 == half, found, turned))
@@ -184,7 +176,7 @@
                 for tile in range(tiles):
                     slot = work["slot"] + b * tiles + tile
                     lead = jnp.where(is_first == 1, 0.0, tail_ref[tile].astype(F32))
-                    shifted_rows(meta_ref, recv_ref, rows_ref, slot, lead, n, tile * BLOCK)
+                    shifted_rows(meta_ref, recv_ref, rows_ref, slot, lead, first_block + n, tile * BLOCK)
                     active = convolved(rows_ref, slot, weight_ref, tile)
                     if tile == 0:
                         work["keys"][b] = active * unit_scale(active)
@@ -271,10 +263,13 @@
     else:
         lax.fori_loop(0, count // per_chunk, chunk, 0)
     for h in range(share):
-        shift_ref[h] = state_ref[h, :, :HEAD_DIM]
-        over = jnp.where(is_first == 1, 0.0, state_ref[h, :, HEAD_DIM:])
-        map_high, map_low = split(over)
-        map_ref[h] = beside(map_high, map_low)
+        if last_part:
+            shift_ref[h] = state_ref[h, :, :HEAD_DIM]
+            over = jnp.where(is_first == 1, 0.0, state_ref[h, :, HEAD_DIM:])
+            map_high, map_low = split(over)
+            map_ref[h] = beside(map_high, map_low)
+        else:
+            final_ref[h] = state_ref[h]
 
     def drain(n, carry):
         leaving(0, n).wait()
@@ -296,23 +291,20 @@
 def finish_kernel(
     dims,
     meta_ref,
-    recv_ref,
+    outer_ref,
     tail_ref,
     weight_ref,
-    row_ref,
     incoming_ref,
     gain_ref,
     solved_in,
     state_in,
     flip_in,
-    out_ref,
-    solved_ref,
-    before_ref,
-    flip_ref,
-    rows_ref,
-    sems,
+    *refs,
 ):
-    group, share, count, per_step, query_row, gate_row = dims
+    group, share, counts, query_row, gate_row, tail_place = dims
+    count = sum(counts)
+    line_refs = refs[: len(counts)]
+    out_ref, solved_ref, before_ref, flip_ref, rows_ref, sems = refs[len(counts) :]
     piece_rows = BLOCK // 2
     is_first = meta_ref[meta_ref.shape[0] - 1]
     row_index = lax.broadcasted_iota(jnp.int32, (BLOCK, BLOCK), 0)
@@ -335,12 +327,13 @@
     lax.fori_loop(0, count, fetch, 0)
     entry = [split(jnp.where(is_first == 1, 0.0, incoming_ref[h])) for h in range(share)]
 
-    def step(index, carry):
-        blocks = [index * per_step + b for b in range(per_step)]
+    def step(index, carry, first_block, per_step, row_ref):
+        spots = [index * per_step + b for b in range(per_step)]
+        blocks = [first_block + spot for spot in spots]
         queries, grams = {}, {}
         for b, n in enumerate(blocks):
-            lead = jnp.where(is_first == 1, 0.0, tail_ref[0].astype(F32))
-            shifted_rows(meta_ref, recv_ref, rows_ref, b, lead, n, query_row)
+            lead = jnp.where(is_first == 1, 0.0, tail_ref[tail_place].astype(F32))
+            shifted_rows(meta_ref, outer_ref, rows_ref, b, lead, n, query_row)
             active = convolved(rows_ref, b, weight_ref, 0)
             queries[b] = active * (unit_scale(active) * HEAD_DIM ** (-0.5))
         for n in blocks:
@@ -353,7 +346,7 @@
         for b, h in units:
             n = blocks[b]
             at = group * share + h
-            cum, beta = row_ref[0, n], row_ref[1, n]
+            cum, beta = row_ref[0, spots[b]], row_ref[1, spots[b]]
             columns = below(cum, jnp.zeros((BLOCK - 8, BLOCK), F32)).T
             column = jnp.broadcast_to(columns[:, at : at + 1], (BLOCK, BLOCK))
             decay = jnp.exp(jnp.where(inclusive, column - cum[at : at + 1], 0.0))
@@ -382,13 +375,21 @@
                 place = meta_ref[2 * n + half]
                 start = gate_row + h * BLOCK + (place % 2) * piece_rows
                 start = pl.multiple_of(start, piece_rows)
-                gates.append(recv_ref[place // 2, pl.ds(start, piece_rows), :].astype(F32))
+                gates.append(outer_ref[place // 2, pl.ds(start, piece_rows), :].astype(F32))
             gate = below(*gates)
             result = core * scale * gain_ref[...] * silu(gate)
             out_ref[n, h * BLOCK : (h + 1) * BLOCK, :] = result.astype(BF16)
         return carry
 
-    lax.fori_loop(0, count // per_step, step, 0)
+    first_block = 0
+    for blocks, row_ref in zip(counts, line_refs):
+        per_step = min(4, blocks)
+        part = functools.partial(step, first_block=first_block, per_step=per_step, row_ref=row_ref)
+        if blocks == per_step:
+            part(0, 0)
+        else:
+            lax.fori_loop(0, blocks // per_step, part, 0)
+        first_block += blocks
 
 
 def gather_kernel(moves, source_count, logit_place, *refs):
@@ -421,11 +422,11 @@
         copy.wait()
 
 
-def halo_kernel(total, rows, meta_ref, arrived_ref, out_ref, sems):
+def halo_kernel(places, meta_ref, arrived_ref, out_ref, sems):
     last = meta_ref[meta_ref.shape[0] - 2]
     copies = []
-    for tile in range(total):
-        source = arrived_ref.at[last // 2, pl.ds(tile * rows + rows - 16, 16), :]
+    for tile, row in enumerate(places):
+        source = arrived_ref.at[last // 2, pl.ds(row, 16), :]
         copies.append(pltpu.make_async_copy(source, out_ref.at[tile], sems.at[tile]))
     for copy in copies:
         copy.start()
@@ -537,7 +538,16 @@
     def key_head(place, group):
         return (place * heads + group * share) // GROUP
 
+    def query_column(place, group):
+        return key_head(place, group) * HEAD_DIM
+
+    def inner_layout(group):
+        rows_total = gate_row + 16
+        tail_row = rows_total if group == groups - 1 else None
+        return tail_row, rows_total + (16 * groups if group == groups - 1 else 0)
+
     def inner_moves(group):
+        tail_row, _ = inner_layout(group)
         moves = []
         for place in range(cp_count):
             found = [key_width + key_head(place, group) * HEAD_DIM]
@@ -545,46 +555,59 @@
                 found.append(2 * key_width + (place * heads + group * share + h) * HEAD_DIM)
             for tile, column in enumerate(found):
                 moves.append((0, 0, rows, column, place, tile * rows))
+            if tail_row is not None:
+                for other in range(groups):
+                    column = query_column(place, other)
+                    moves.append((0, rows - 16, 16, column, place, tail_row + 16 * other))
         return moves
 
     def outer_moves():
         moves = []
         for place in range(cp_count):
             for group in range(groups):
-                moves.append((0, 0, rows, key_head(place, group) * HEAD_DIM, place, group * rows))
+                moves.append((0, 0, rows, query_column(place, group), place, group * rows))
             for h in range(heads):
-                moves.append((1, 0, rows, (place * heads + h) * HEAD_DIM, place, (groups + h) * rows))
+                column = (place * heads + h) * HEAD_DIM
+                moves.append((1, 0, rows, column, place, (groups + h) * rows))
         return moves
 
-    def halo(arrived, total):
+    def halo(arrived, places):
         found = pl.pallas_call(
-            functools.partial(halo_kernel, total, rows),
-            out_shape=jax.ShapeDtypeStruct((total, 16, HEAD_DIM), BF16),
+            functools.partial(halo_kernel, tuple(places)),
+            out_shape=jax.ShapeDtypeStruct((len(places), 16, HEAD_DIM), BF16),
             in_specs=[smem, anywhere],
             out_specs=vmem,
-            scratch_shapes=[pltpu.SemaphoreType.DMA((total,))],
+            scratch_shapes=[pltpu.SemaphoreType.DMA((len(places),))],
             compiler_params=limits(2),
             cost_estimate=cost(1e8),
         )(meta, arrived)
         return passed_round(found, "seg")
 
+    def in_hbm(array):
+        return pltpu.with_memory_space_constraint(array, pltpu.HBM)
+
     received, tails = [], []
     for group in range(groups):
+        tail_row, rows_total = inner_layout(group)
         sent = gather(
-            [mixed_qkv],
+            [in_hbm(mixed_qkv)],
             inner_moves(group),
             cp_count,
-            gate_row + 16,
+            rows_total,
             logits=gate_logits.T,
             first_row=gate_row,
             heads=heads,
         )
         received.append(exchanged(sent))
-        tails.append(halo(received[group], tiles))
-
-    packed = gather([mixed_qkv, gate_z], outer_moves(), cp_count, (groups + heads) * rows)
+        places = [tile * rows + rows - 16 for tile in range(tiles)]
+        if tail_row is not None:
+            places += [tail_row + 16 * other for other in range(groups)]
+        tails.append(halo(received[group], places))
+
+    packed = gather(
+        [in_hbm(mixed_qkv), in_hbm(gate_z)], outer_moves(), cp_count, (groups + heads) * rows
+    )
     outer = exchanged(packed)
-    outer_tail = halo(outer, groups)
 
     shaped = conv_weight.reshape(CONV, -1, HEAD_DIM)
 
@@ -604,36 +627,48 @@
     rates = jnp.pad(jnp.stack([head_log, head_bias]), ((0, 0), (0, 8 - heads)))
     rates = jnp.broadcast_to(rates[:, :, None], (2, 8, BLOCK))
 
-    per_step = min(4, count)
-    per_chunk = min(8, count)
-
-    def inner(group):
-        dims = (group, share, count, per_step, per_chunk)
+    def inner(group, first_block, blocks, last_part, earlier):
+        per_step, per_chunk = min(4, blocks), min(8, blocks)
+        dims = (group, share, first_block, blocks, per_step, per_chunk, last_part)
         wide = (share, count * BLOCK, 2 * HEAD_DIM)
+        kept = (share, blocks * BLOCK, 2 * HEAD_DIM)
+        out_shape = [
+            pltpu.HBM(wide, F32),
+            pltpu.HBM(wide, F32),
+            pltpu.HBM((count, HEAD_DIM, BLOCK), F32),
+            jax.ShapeDtypeStruct((2, blocks, 8, BLOCK), F32),
+        ]
+        if last_part:
+            out_shape.append(jax.ShapeDtypeStruct((share, HEAD_DIM, HEAD_DIM), F32))
+            out_shape.append(jax.ShapeDtypeStruct((share, HEAD_DIM, 2 * HEAD_DIM), BF16))
+        else:
+            out_shape.append(jax.ShapeDtypeStruct((share, HEAD_DIM, 2 * HEAD_DIM), F32))
+        operands = [meta, received[group], tails[group], weights[group], rates]
+        in_specs = [smem] + [vmem] * 4
+        aliases = {}
+        if earlier is not None:
+            state, buffers = earlier
+            operands += [state] + list(buffers)
+            in_specs += [vmem] + [stored] * 3
+            aliases = {6: 0, 7: 1, 8: 2}
         return pl.pallas_call(
             functools.partial(inner_kernel, dims),
-            out_shape=(
-                pltpu.HBM(wide, F32),
-                pltpu.HBM(wide, F32),
-                pltpu.HBM((count, HEAD_DIM, BLOCK), F32),
-                jax.ShapeDtypeStruct((2, count, 8, BLOCK), F32),
-                jax.ShapeDtypeStruct((share, HEAD_DIM, HEAD_DIM), F32),
-                jax.ShapeDtypeStruct((share, HEAD_DIM, 2 * HEAD_DIM), BF16),
-            ),
-            in_specs=[smem] + [vmem] * 4,
-            out_specs=(stored, stored, stored, vmem, vmem, vmem),
+            out_shape=out_shape,
+            in_specs=in_specs,
+            out_specs=[stored] * 3 + [vmem] * (len(out_shape) - 3),
             scratch_shapes=[
-                pltpu.VMEM(wide, F32),
-                pltpu.VMEM(wide, F32),
-                pltpu.VMEM((count, HEAD_DIM, BLOCK), F32),
+                pltpu.VMEM(kept, F32),
+                pltpu.VMEM(kept, F32),
+                pltpu.VMEM((blocks, HEAD_DIM, BLOCK), F32),
                 pltpu.VMEM((per_chunk * tiles, 8 + BLOCK, HEAD_DIM), F32),
                 pltpu.VMEM((len(LEVELS), BLOCK, BLOCK), BF16),
                 pltpu.VMEM((share, HEAD_DIM, 2 * HEAD_DIM), F32),
-                pltpu.SemaphoreType.DMA((3, count)),
+                pltpu.SemaphoreType.DMA((3, blocks)),
             ],
+            input_output_aliases=aliases,
             compiler_params=limits(INNER_MIB),
-            cost_estimate=cost(6e8 * count * share),
-        )(meta, received[group], tails[group], weights[group], rates)
+            cost_estimate=cost(6e8 * blocks * share),
+        )(*operands)
 
     def chain(shift, over):
         incoming = None
@@ -653,39 +688,44 @@
             incoming = jnp.zeros_like(shift)
         return incoming
 
-    def finish(group, incoming, solved, before, flip, lines):
-        dims = (group, share, count, per_step, group * rows, (groups + group * share) * rows)
+    def finish(group, counts, incoming, buffers, lines):
+        gate_start = (groups + group * share) * rows
+        dims = (group, share, tuple(counts), group * rows, gate_start, tiles + group)
         wide = (share, count * BLOCK, 2 * HEAD_DIM)
+        operands = [meta, outer, tails[-1], query_weights[group], incoming]
+        operands.append(norm_gain.reshape(1, HEAD_DIM))
+        operands += [in_hbm(array) for array in buffers]
+        operands += lines
         return pl.pallas_call(
             functools.partial(finish_kernel, dims),
             out_shape=jax.ShapeDtypeStruct((count, share * BLOCK, HEAD_DIM), BF16),
-            in_specs=[smem] + [vmem] * 6 + [stored] * 3,
+            in_specs=[smem] + [vmem] * 5 + [stored] * 3 + [vmem] * len(lines),
             out_specs=vmem,
             scratch_shapes=[
                 pltpu.VMEM(wide, F32),
                 pltpu.VMEM(wide, F32),
                 pltpu.VMEM((count, HEAD_DIM, BLOCK), F32),
-                pltpu.VMEM((per_step, 8 + BLOCK, HEAD_DIM), F32),
+                pltpu.VMEM((4, 8 + BLOCK, HEAD_DIM), F32),
                 pltpu.SemaphoreType.DMA((3, count)),
             ],
             compiler_params=limits(FINISH_MIB),
             cost_estimate=cost(1.5e9),
-        )(
-            meta,
-            outer,
-            outer_tail[group : group + 1],
-            query_weights[group],
-            lines,
-            incoming,
-            norm_gain.reshape(1, HEAD_DIM),
-            *[pltpu.with_memory_space_constraint(x, pltpu.HBM) for x in (solved, before, flip)],
-        )
+        )(*operands)
 
     result = None
     for group in range(groups):
-        solved, before, flip, lines, shift, over = inner(group)
-        incoming = chain(shift, over)
-        done = finish(group, incoming, solved, before, flip, lines)
+        parts = 2 if group and count % 8 == 0 else 1
+        blocks = count // parts
+        earlier, lines = None, []
+        for part in range(parts):
+            *buffers, line, state, over = (
+                *inner(group, part * blocks, blocks, part == parts - 1, earlier),
+                *([None] if part < parts - 1 else []),
+            )
+            lines.append(line)
+            earlier = (state, buffers)
+        incoming = chain(state, over)
+        done = finish(group, [blocks] * parts, incoming, buffers, lines)
         swapped = exchanged(done)
         moves = [
             (place, h * rows, rows, (place * heads + group * share + h) * HEAD_DIM)

time: 127 us -> 121 us (0.953)
  local copies, waits for them, and re-layouts: 8.91 us -> 2.34 us
  Pallas kernels: 39.1 us -> 44.2 us
  waiting for transfers between devices: 45.6 us -> 41.7 us
    unnamed x30 -> x12, local copies, waits for them, and re-layouts: 7.32 us -> 0.74 us
    ppermute x9 -> x8, waiting for transfers between devices: 22.9 us -> 17.1 us  [passed_round(): lax.ppermute(value, axis, [(i, (i + 1) % length) for i in range(length)])]
    pallas_call x3, Pallas kernels: 4 us -> 7.66 us  [gather(): pl.pallas_call(functools.partial(gather_kernel, tuple(moves), len(sources...]
    all_to_all x5, waiting for transfers between devices: 22.7 us -> 24.5 us  [exchanged(): return lax.all_to_all(value, 'cp', split_axis=0, concat_axis=0, tiled=True)]
    pallas_call x5, Pallas kernels: 20.9 us -> 22.4 us  [the longest x3 21.2 us: inner(): pl.pallas_call(functools.partial(inner_kernel, dims), out_shape=out_shape...]
    ppermute x9 -> x8, starting transfers between devices: 10.6 us -> 9.86 us  [passed_round(): lax.ppermute(value, axis, [(i, (i + 1) % length) for i in range(length)])]
  transfers between devices with their start and end apart: 14 -> 13, of which waited for: 8 -> 7; matrix products, arithmetic and copies ran while one was open for 2% -> 3% of each run, Pallas kernels for 29% -> 34%
where the time goes in v3:
time: 121 us; the launch traced here: 120 us
  Pallas kernels  44.2 us (37%)
  waiting for transfers between devices  41.7 us (34%)
  starting transfers between devices  29.8 us (25%)
  local copies, waits for them, and re-layouts  2.34 us (2%)
  other arithmetic  1.41 us (1%)
    all_to_all x5, waiting for transfers between devices, exchanged(): return lax.all_to_all(value, 'cp', split_axis=0, concat_axis=0, tiled=True)  24.5 us
    pallas_call x3, Pallas kernels, inner(): pl.pallas_call(functools.partial(inner_kernel, dims), out_shape=out_shape...  21.2 us
    all_to_all x5, starting transfers between devices, exchanged(): return lax.all_to_all(value, 'cp', split_axis=0, concat_axis=0, tiled=True)  19.9 us
    ppermute x8, waiting for transfers between devices, passed_round(): lax.ppermute(value, axis, [(i, (i + 1) % length) for i in range(length)])  17.1 us
    pallas_call x2, Pallas kernels, finish(): pl.pallas_call(functools.partial(finish_kernel, dims), out_shape=jax.Shap...  11.6 us
    ppermute x8, starting transfers between devices, passed_round(): lax.ppermute(value, axis, [(i, (i + 1) % length) for i in range(length)])  9.86 us
    pallas_call x3, Pallas kernels, gather(): pl.pallas_call(functools.partial(gather_kernel, tuple(moves), len(sources...  7.66 us
  transfers between devices with their start and end apart: 13, of which 7 were waited for; matrix products, arithmetic and copies ran while one was open for 3% of the time, Pallas kernels for 34%

profile of v3, /device:TPU:0, one launch (start us, length us, event | category | flops | bytes accessed | tf_op | source)
XLA Modules:
  0.0 119.9 jit_solution(14947534623220823595)
XLA Ops:
  0.0 0.0 copy-start
  0.0 0.7 copy-done
  0.7 0.0 copy-start.1
  0.7 2.2 %shard_map.90 = bf16[8,400,128]{2,1,0:T(8,128)(2,1)} custom-call(bf16[128,8192]{1,0:T(8,128)(2,1)} %refs_0_.5, bf16[64,128]{1,0:T(8,128)(2,1)S(1)} %bitcast.21), custom_call_target="tpu_custom_call" | custom-call | flops 800000000 | bytes 1048576 | tf_op jit(solution)/shard_map/pallas_call | solution.py:483
  2.9 5.2 %all-to-all-start.3 = ((bf16[8,400,128]{2,1,0:T(8,128)(2,1)}), bf16[8,400,128]{2,1,0:T(8,128)(2,1)S(1)}, u32[]{:S(2)}, u32[]{:S(2)}) async-start(bf16[8,400,128]{2,1,0:T(8,128)(2,1)} %shard_map.90), calls=%async_computation.3 | async-start | bytes 1638400 | tf_op jit(solution)/shard_map/all_to_all | solution.py:518
  8.2 0.0 copy-done.1
  8.2 0.0 copy-start.5
  8.2 0.0 copy-start.3
  8.2 0.0 copy-start.4
  8.2 2.5 %shard_map.83 = bf16[8,432,128]{2,1,0:T(8,128)(2,1)} custom-call(bf16[128,8192]{1,0:T(8,128)(2,1)} %refs_0_.5, bf16[64,128]{1,0:T(8,128)(2,1)S(1)} %bitcast.22), custom_call_target="tpu_custom_call" | custom-call | flops 800000000 | bytes 1048576 | tf_op jit(solution)/shard_map/pallas_call | solution.py:483
  10.7 10.4 %all-to-all-done.3.arrived_ref.recv_ref = bf16[8,400,128]{2,1,0:T(8,128)(2,1)S(1)} async-done(((bf16[8,400,128]{2,1,0:T(8,128)(2,1)}), bf16[8,400,128]{2,1,0:T(8,128)(2,1)S(1)}, u32[]{:S(2)}, u32[]{:S(2)}) %all-to-all-start.3) | async-done | bytes 819232 | tf_op jit(solution)/shard_map/all_to_all | solution.py:518
  21.1 3.6 %all-to-all-start.1 = ((bf16[8,432,128]{2,1,0:T(8,128)(2,1)}), bf16[8,432,128]{2,1,0:T(8,128)(2,1)S(1)}, u32[]{:S(2)}, u32[]{:S(2)}) async-start(bf16[8,432,128]{2,1,0:T(8,128)(2,1)} %shard_map.83), calls=%async_computation.1 | async-start | bytes 1769472 | tf_op jit(solution)/shard_map/all_to_all | solution.py:518
  24.7 0.0 copy-done.5
  24.7 1.3 %sort.17 = (s32[16]{0:T(128)}, s32[16]{0:T(128)S(1)}) sort(s32[16]{0:T(128)S(1)} %bitcast.27, s32[16]{0:T(128)S(1)} %iota.4), dimensions={0}, to_apply=%region_0.0 | sort | flops 64 | bytes 256 | tf_op jit(solution)/shard_map/jit(argsort)/sort | solution.py:534
  26.0 0.1 pad_add_fusion.meta_ref
  26.1 0.0 copy-done.3
  26.1 0.0 copy-done.4
  26.1 0.1 dynamic-slice_bitcast_fusion.6
  26.2 0.7 dynamic-slice_bitcast_fusion
  26.9 0.7 dynamic-slice_bitcast_fusion.2
  27.6 0.6 shard_map.91
  28.2 1.6 %collective-permute-start.4 = (bf16[3,16,128]{2,1,0:T(8,128)(2,1)S(1)}, bf16[3,16,128]{2,1,0:T(8,128)(2,1)S(1)}, u32[]{:S(2)}, u32[]{:S(2)}) collective-permute-start(bf16[3,16,128]{2,1,0:T(8,128)(2,1)S(1)} %shard_map.91), channel_id=1, source_target_pairs={{0,8},{8,16},{16,24},{24,0},{1,9},{9,17},{17,25},{25,1},{2,10},{10... | collective-permute-start | bytes 36872 | tf_op jit(solution)/shard_map/ppermute | solution.py:514
  29.9 3.0 %shard_map.82 = bf16[8,768,128]{2,1,0:T(8,128)(2,1)} custom-call(bf16[128,8192]{1,0:T(8,128)(2,1)} %refs_0_.5, bf16[128,4096]{1,0:T(8,128)(2,1)} %refs_1_.1), custom_call_target="tpu_custom_call" | custom-call | flops 800000000 | bytes 1048576 | tf_op jit(solution)/shard_map/pallas_call | solution.py:483
  32.8 5.3 %all-to-all-done.1.arrived_ref.recv_ref = bf16[8,432,128]{2,1,0:T(8,128)(2,1)S(1)} async-done(((bf16[8,432,128]{2,1,0:T(8,128)(2,1)}), bf16[8,432,128]{2,1,0:T(8,128)(2,1)S(1)}, u32[]{:S(2)}, u32[]{:S(2)}) %all-to-all-start.1) | async-done | bytes 884768 | tf_op jit(solution)/shard_map/all_to_all | solution.py:518
  38.2 3.6 %all-to-all-start = ((bf16[8,768,128]{2,1,0:T(8,128)(2,1)}), bf16[8,768,128]{2,1,0:T(8,128)(2,1)S(1)}, u32[]{:S(2)}, u32[]{:S(2)}) async-start(bf16[8,768,128]{2,1,0:T(8,128)(2,1)} %shard_map.82), calls=%async_computation | async-start | bytes 3145728 | tf_op jit(solution)/shard_map/all_to_all | solution.py:518
  41.8 0.0 collective-permute-done.4.tail_ref
  41.8 0.1 broadcast_in_dim.2.rate_ref
  41.9 9.6 %shard_map.92 = (f32[2,1024,256]{2,1,0:T(8,128)}, f32[2,1024,256]{2,1,0:T(8,128)}, f32[8,128,128]{2,1,0:T(8,128)}, f32[2,8,8,128]{3,2,1,0:T(8,128)S(1)}, f32[2,1...) custom-call(s32[17]{0:T(128)S(1)} %pad_add_fusion.meta_ref, ...), custom_call_target="tpu_custom_call" | custom-call | flops 9600000000 | bytes 1048576 | tf_op jit(solution)/shard_map/pallas_call | solution.py:654
  51.4 1.6 %collective-permute-start.5 = (f32[2,128,128]{2,1,0:T(8,128)S(1)}, f32[2,128,128]{2,1,0:T(8,128)S(1)}, u32[]{:S(2)}, u32[]{:S(2)}) collective-permute-start(f32[2,128,128]{2,1,0:T(8,128)S(1)} %get-tuple-element.35.shift_ref), channel_id=1, source_target_pairs={{0,8},{8,16},{16,24},{24,0},{1,9},{9,17},{17,25},{25,1},{2,10},{10... | collective-permute-start | bytes 393224 | tf_op jit(solution)/shard_map/ppermute | solution.py:514
  53.1 0.6 shard_map.84
  53.7 1.6 %collective-permute-start = (bf16[5,16,128]{2,1,0:T(8,128)(2,1)S(1)}, bf16[5,16,128]{2,1,0:T(8,128)(2,1)S(1)}, u32[]{:S(2)}, u32[]{:S(2)}) collective-permute-start(bf16[5,16,128]{2,1,0:T(8,128)(2,1)S(1)} %shard_map.84), channel_id=1, source_target_pairs={{0,8},{8,16},{16,24},{24,0},{1,9},{9,17},{17,25},{25,1},{2,10},{10... | collective-permute-start | bytes 61448 | tf_op jit(solution)/shard_map/ppermute | solution.py:514
  55.3 4.0 %collective-permute-done.5.incoming_ref = f32[2,128,128]{2,1,0:T(8,128)S(1)} collective-permute-done((f32[2,128,128]{2,1,0:T(8,128)S(1)}, f32[2,128,128]{2,1,0:T(8,128)S(1)}, u32[]{:S(2)}, u32[]{:S(2)}) %collective-permute-start.5) | collective-permute-done | bytes 131104 | tf_op jit(solution)/shard_map/ppermute | solution.py:514
  59.4 0.2 shard_map.93
  59.6 0.2 collective-permute-start.6
  59.8 0.0 collective-permute-done.tail_ref
  59.8 5.8 %shard_map.85 = (f32[2,1024,256]{2,1,0:T(8,128)}, f32[2,1024,256]{2,1,0:T(8,128)}, f32[8,128,128]{2,1,0:T(8,128)}, f32[2,4,8,128]{3,2,1,0:T(8,128)S(1)}, f32[2,128,256]{2,1,0:T(8,128)S(1)}) custom-call(s32[17]{0:T(128)S(1)} %pad_add_fusion.meta_ref, bf16[8,432,128]{2,1,0:T(8,128)(2,1)S(1)} %all-to-all-done.1.arrived_ref.recv_ref, ...), custom_call_target="tpu_custom_call" | custom-call | flops 4800000000 | bytes 1048576 | tf_op jit(solution)/shard_map/pallas_call | solution.py:654
  65.6 0.9 collective-permute-done.6.incoming_ref
  66.6 0.2 shard_map.94
  66.8 0.4 collective-permute-start.7
  67.2 0.0 copy-start.2
  67.2 5.8 %shard_map.86 = (f32[2,1024,256]{2,1,0:T(8,128)}, f32[2,1024,256]{2,1,0:T(8,128)}, f32[8,128,128]{2,1,0:T(8,128)}, f32[2,4,8,128]{3,2,1,0:T(8,128)S(1)}, f32[2,1...) custom-call(s32[17]{0:T(128)S(1)} %pad_add_fusion.meta_ref, ...), custom_call_target="tpu_custom_call", output_to_operand_aliasing={{0}: (6, {}), {1}: (7, {}), {2}: (8, {})} | custom-call | flops 4800000000 | bytes 1048576 | tf_op jit(solution)/shard_map/pallas_call | solution.py:654
  73.0 1.6 %collective-permute-start.1 = (f32[2,128,128]{2,1,0:T(8,128)S(1)}, f32[2,128,128]{2,1,0:T(8,128)S(1)}, u32[]{:S(2)}, u32[]{:S(2)}) collective-permute-start(f32[2,128,128]{2,1,0:T(8,128)S(1)} %get-tuple-element.28.shift_ref), channel_id=1, source_target_pairs={{0,8},{8,16},{16,24},{24,0},{1,9},{9,17},{17,25},{25,1},{2,10},{10... | collective-permute-start | bytes 393224 | tf_op jit(solution)/shard_map/ppermute | solution.py:514
  74.6 0.0 collective-permute-done.7.incoming_ref
  74.6 0.0 all-to-all-done.outer_ref
  74.6 0.0 copy-done.2
  74.6 5.8 %shard_map.95 = bf16[8,256,128]{2,1,0:T(8,128)(2,1)} custom-call(s32[17]{0:T(128)S(1)} %pad_add_fusion.meta_ref, bf16[8,768,128]{2,1,0:T(8,128)(2,1)S(1)} %all-to-all-done.outer_ref, bf16[5,16,128]{2,1,0:T(8,128)(2,1)S(1)} %collective-permute-done.tail_ref, f32[1,4,128]{2,1,0:T(4,128)S(1)} %get-tuple-element.42.weight_ref, ...), custom_call_target="tpu_custom_call" | custom-call | flops 1500000000 | bytes 1048576 | tf_op jit(solution)/shard_map/pallas_call | solution.py:699
  80.5 3.9 %all-to-all-start.4 = ((bf16[8,256,128]{2,1,0:T(8,128)(2,1)}), bf16[8,256,128]{2,1,0:T(8,128)(2,1)S(1)}, u32[]{:S(2)}, u32[]{:S(2)}) async-start(bf16[8,256,128]{2,1,0:T(8,128)(2,1)} %shard_map.95), calls=%async_computation.4 | async-start | bytes 1048576 | tf_op jit(solution)/shard_map/all_to_all | solution.py:518
  84.3 0.0 collective-permute-done.1.incoming_ref
  84.3 0.2 shard_map.87
  84.5 2.1 %collective-permute-start.2 = (f32[2,128,128]{2,1,0:T(8,128)S(1)}, f32[2,128,128]{2,1,0:T(8,128)S(1)}, u32[]{:S(2)}, u32[]{:S(2)}) collective-permute-start(f32[2,128,128]{2,1,0:T(8,128)S(1)} %shard_map.87), channel_id=1, source_target_pairs={{0,8},{8,16},{16,24},{24,0},{1,9},{9,17},{17,25},{25,1},{2,10},{10... | collective-permute-start | bytes 393224 | tf_op jit(solution)/shard_map/ppermute | solution.py:514
  86.7 5.6 %collective-permute-done.2.incoming_ref = f32[2,128,128]{2,1,0:T(8,128)S(1)} collective-permute-done((f32[2,128,128]{2,1,0:T(8,128)S(1)}, f32[2,128,128]{2,1,0:T(8,128)S(1)}, u32[]{:S(2)}, u32[]{:S(2)}) %collective-permute-start.2) | collective-permute-done | bytes 131104 | tf_op jit(solution)/shard_map/ppermute | solution.py:514
  92.3 0.2 shard_map.88
  92.5 0.6 collective-permute-start.3
  93.0 6.5 %collective-permute-done.3.incoming_ref = f32[2,128,128]{2,1,0:T(8,128)S(1)} collective-permute-done((f32[2,128,128]{2,1,0:T(8,128)S(1)}, f32[2,128,128]{2,1,0:T(8,128)S(1)}, u32[]{:S(2)}, u32[]{:S(2)}) %collective-permute-start.3) | collective-permute-done | bytes 131104 | tf_op jit(solution)/shard_map/ppermute | solution.py:514
  99.6 5.7 %shard_map.89 = bf16[8,256,128]{2,1,0:T(8,128)(2,1)} custom-call(s32[17]{0:T(128)S(1)} %pad_add_fusion.meta_ref, bf16[8,768,128]{2,1,0:T(8,128)(2,1)S(1)} %all-to-all-done.outer_ref, bf16[5,16,128]{2,1,0:T(8,128)(2,1)S(1)} %collective-permute-done.tail_ref, f32[1,4,128]{2,1,0:T(4,128)S(1)} %get-tuple-element.44.weight_ref, ...), custom_call_target="tpu_custom_call" | custom-call | flops 1500000000 | bytes 1048576 | tf_op jit(solution)/shard_map/pallas_call | solution.py:699
  105.3 0.0 all-to-all-done.4.refs_0_
  105.4 3.7 %all-to-all-start.2 = ((bf16[8,256,128]{2,1,0:T(8,128)(2,1)}), bf16[8,256,128]{2,1,0:T(8,128)(2,1)S(1)}, u32[]{:S(2)}, u32[]{:S(2)}) async-start(bf16[8,256,128]{2,1,0:T(8,128)(2,1)} %shard_map.89), calls=%async_computation.2 | async-start | bytes 1048576 | tf_op jit(solution)/shard_map/all_to_all | solution.py:518
  109.1 0.9 shard_map.96.refs_1_
  110.0 8.8 %all-to-all-done.2.refs_0_ = bf16[8,256,128]{2,1,0:T(8,128)(2,1)S(1)} async-done(((bf16[8,256,128]{2,1,0:T(8,128)(2,1)}), bf16[8,256,128]{2,1,0:T(8,128)(2,1)S(1)}, u32[]{:S(2)}, u32[]{:S(2)}) %all-to-all-start.2) | async-done | bytes 524320 | tf_op jit(solution)/shard_map/all_to_all | solution.py:518
  118.8 0.9 shard_map.97
  (4 shorter events, 0.0 us)
Async XLA Ops:
  0.0 0.7 copy-start
  0.7 7.4 %copy-start.1 = (bf16[128,64]{0,1:T(8,128)(2,1)S(1)}, bf16[128,64]{0,1:T(8,128)(2,1)}, u32[]{:S(2)}) copy-start(bf16[128,64]{0,1:T(8,128)(2,1)} %param.10) | copy-start | bytes 49156
  2.9 18.1 %all-to-all-start.3 = ((bf16[8,400,128]{2,1,0:T(8,128)(2,1)}), bf16[8,400,128]{2,1,0:T(8,128)(2,1)S(1)}, u32[]{:S(2)}, u32[]{:S(2)}) async-start(bf16[8,400,128]{2,1,0:T(8,128)(2,1)} %shard_map.90), calls=%async_computation.3 | async-start | bytes 1638400 | tf_op jit(solution)/shard_map/all_to_all | solution.py:518
  8.2 16.5 %copy-start.5 = (s32[1,16]{1,0:T(1,128)S(1)}, s32[1,16]{1,0:T(1,128)}, u32[]{:S(2)}) copy-start(s32[1,16]{1,0:T(1,128)} %param.11) | copy-start | bytes 196
  8.2 17.9 %copy-start.3 = (f32[32]{0:T(128)S(1)}, f32[32]{0:T(128)}, u32[]{:S(2)}) copy-start(f32[32]{0:T(128)} %param.14) | copy-start | bytes 388
  8.2 17.9 %copy-start.4 = (f32[32]{0:T(128)S(1)}, f32[32]{0:T(128)}, u32[]{:S(2)}) copy-start(f32[32]{0:T(128)} %param.13) | copy-start | bytes 388
  21.1 17.1 %all-to-all-start.1 = ((bf16[8,432,128]{2,1,0:T(8,128)(2,1)}), bf16[8,432,128]{2,1,0:T(8,128)(2,1)S(1)}, u32[]{:S(2)}, u32[]{:S(2)}) async-start(bf16[8,432,128]{2,1,0:T(8,128)(2,1)} %shard_map.83), calls=%async_computation.1 | async-start | bytes 1769472 | tf_op jit(solution)/shard_map/all_to_all | solution.py:518
  28.2 13.6 %collective-permute-start.4 = (bf16[3,16,128]{2,1,0:T(8,128)(2,1)S(1)}, bf16[3,16,128]{2,1,0:T(8,128)(2,1)S(1)}, u32[]{:S(2)}, u32[]{:S(2)}) collective-permute-start(bf16[3,16,128]{2,1,0:T(8,128)(2,1)S(1)} %shard_map.91), channel_id=1, source_target_pairs={{0,8},{8,16},{16,24},{24,0},{1,9},{9,17},{17,25},{25,1},{2,10},{10... | collective-permute-start | bytes 36872 | tf_op jit(solution)/shard_map/ppermute | solution.py:514
  38.2 36.4 %all-to-all-start = ((bf16[8,768,128]{2,1,0:T(8,128)(2,1)}), bf16[8,768,128]{2,1,0:T(8,128)(2,1)S(1)}, u32[]{:S(2)}, u32[]{:S(2)}) async-start(bf16[8,768,128]{2,1,0:T(8,128)(2,1)} %shard_map.82), calls=%async_computation | async-start | bytes 3145728 | tf_op jit(solution)/shard_map/all_to_all | solution.py:518
  51.4 7.9 %collective-permute-start.5 = (f32[2,128,128]{2,1,0:T(8,128)S(1)}, f32[2,128,128]{2,1,0:T(8,128)S(1)}, u32[]{:S(2)}, u32[]{:S(2)}) collective-permute-start(f32[2,128,128]{2,1,0:T(8,128)S(1)} %get-tuple-element.35.shift_ref), channel_id=1, source_target_pairs={{0,8},{8,16},{16,24},{24,0},{1,9},{9,17},{17,25},{25,1},{2,10},{10... | collective-permute-start | bytes 393224 | tf_op jit(solution)/shard_map/ppermute | solution.py:514
  53.7 6.1 %collective-permute-start = (bf16[5,16,128]{2,1,0:T(8,128)(2,1)S(1)}, bf16[5,16,128]{2,1,0:T(8,128)(2,1)S(1)}, u32[]{:S(2)}, u32[]{:S(2)}) collective-permute-start(bf16[5,16,128]{2,1,0:T(8,128)(2,1)S(1)} %shard_map.84), channel_id=1, source_target_pairs={{0,8},{8,16},{16,24},{24,0},{1,9},{9,17},{17,25},{25,1},{2,10},{10... | collective-permute-start | bytes 61448 | tf_op jit(solution)/shard_map/ppermute | solution.py:514
  59.6 7.0 %collective-permute-start.6 = (f32[2,128,128]{2,1,0:T(8,128)S(1)}, f32[2,128,128]{2,1,0:T(8,128)S(1)}, u32[]{:S(2)}, u32[]{:S(2)}) collective-permute-start(f32[2,128,128]{2,1,0:T(8,128)S(1)} %shard_map.93), channel_id=1, source_target_pairs={{0,8},{8,16},{16,24},{24,0},{1,9},{9,17},{17,25},{25,1},{2,10},{10... | collective-permute-start | bytes 393224 | tf_op jit(solution)/shard_map/ppermute | solution.py:514
  66.8 7.8 %collective-permute-start.7 = (f32[2,128,128]{2,1,0:T(8,128)S(1)}, f32[2,128,128]{2,1,0:T(8,128)S(1)}, u32[]{:S(2)}, u32[]{:S(2)}) collective-permute-start(f32[2,128,128]{2,1,0:T(8,128)S(1)} %shard_map.94), channel_id=1, source_target_pairs={{0,8},{8,16},{16,24},{24,0},{1,9},{9,17},{17,25},{25,1},{2,10},{10... | collective-permute-start | bytes 393224 | tf_op jit(solution)/shard_map/ppermute | solution.py:514
  67.2 7.4 %copy-start.2 = (f32[128]{0:T(128)S(1)}, f32[128]{0:T(128)}, u32[]{:S(2)}) copy-start(f32[128]{0:T(128)} %param.15) | copy-start | bytes 1540
  73.0 11.3 %collective-permute-start.1 = (f32[2,128,128]{2,1,0:T(8,128)S(1)}, f32[2,128,128]{2,1,0:T(8,128)S(1)}, u32[]{:S(2)}, u32[]{:S(2)}) collective-permute-start(f32[2,128,128]{2,1,0:T(8,128)S(1)} %get-tuple-element.28.shift_ref), channel_id=1, source_target_pairs={{0,8},{8,16},{16,24},{24,0},{1,9},{9,17},{17,25},{25,1},{2,10},{10... | collective-permute-start | bytes 393224 | tf_op jit(solution)/shard_map/ppermute | solution.py:514
  80.5 24.9 %all-to-all-start.4 = ((bf16[8,256,128]{2,1,0:T(8,128)(2,1)}), bf16[8,256,128]{2,1,0:T(8,128)(2,1)S(1)}, u32[]{:S(2)}, u32[]{:S(2)}) async-start(bf16[8,256,128]{2,1,0:T(8,128)(2,1)} %shard_map.95), calls=%async_computation.4 | async-start | bytes 1048576 | tf_op jit(solution)/shard_map/all_to_all | solution.py:518
  84.5 7.8 %collective-permute-start.2 = (f32[2,128,128]{2,1,0:T(8,128)S(1)}, f32[2,128,128]{2,1,0:T(8,128)S(1)}, u32[]{:S(2)}, u32[]{:S(2)}) collective-permute-start(f32[2,128,128]{2,1,0:T(8,128)S(1)} %shard_map.87), channel_id=1, source_target_pairs={{0,8},{8,16},{16,24},{24,0},{1,9},{9,17},{17,25},{25,1},{2,10},{10... | collective-permute-start | bytes 393224 | tf_op jit(solution)/shard_map/ppermute | solution.py:514
  92.5 7.1 %collective-permute-start.3 = (f32[2,128,128]{2,1,0:T(8,128)S(1)}, f32[2,128,128]{2,1,0:T(8,128)S(1)}, u32[]{:S(2)}, u32[]{:S(2)}) collective-permute-start(f32[2,128,128]{2,1,0:T(8,128)S(1)} %shard_map.88), channel_id=1, source_target_pairs={{0,8},{8,16},{16,24},{24,0},{1,9},{9,17},{17,25},{25,1},{2,10},{10... | collective-permute-start | bytes 393224 | tf_op jit(solution)/shard_map/ppermute | solution.py:514
  105.4 13.5 %all-to-all-start.2 = ((bf16[8,256,128]{2,1,0:T(8,128)(2,1)}), bf16[8,256,128]{2,1,0:T(8,128)(2,1)S(1)}, u32[]{:S(2)}, u32[]{:S(2)}) async-start(bf16[8,256,128]{2,1,0:T(8,128)(2,1)} %shard_map.89), calls=%async_computation.2 | async-start | bytes 1048576 | tf_op jit(solution)/shard_map/all_to_all | solution.py:518

commit v4 on v3

--- a/solution.py
+++ b/solution.py
@@ -395,7 +395,9 @@
 def gather_kernel(moves, source_count, logit_place, *refs):
     sources, refs = refs[:source_count], refs[source_count:]
     if logit_place:
-        logit_ref, out_ref, sems, wide_ref = refs
+        logit_ref, out_ref, sems, wide_ref, plain_ref, logit_sem = refs
+        fetch = pltpu.make_async_copy(logit_ref, plain_ref, logit_sem.at[0])
+        fetch.start()
     else:
         out_ref, sems = refs
     copies = []
@@ -412,7 +414,8 @@
     if logit_place:
         first_row, heads = logit_place
         wide_ref[...] = jnp.zeros(wide_ref.shape, F32)
-        wide_ref[0 : 2 * VALUE_HEADS, :] = logit_ref[...].astype(F32)
+        fetch.wait()
+        wide_ref[0 : 2 * VALUE_HEADS, :] = plain_ref[...].astype(F32)
         for place in range(out_ref.shape[0]):
             begin = place * heads
             rates = wide_ref[begin : begin + 8, :]
@@ -477,8 +480,10 @@
     logit_place = None
     if logits is not None:
         operands.append(logits)
-        in_specs.append(vmem)
+        in_specs.append(anywhere)
         scratch.append(pltpu.VMEM((2 * VALUE_HEADS + 8, logits.shape[1]), F32))
+        scratch.append(pltpu.VMEM(logits.shape, BF16))
+        scratch.append(pltpu.SemaphoreType.DMA((1,)))
         logit_place = (first_row, heads)
     return pl.pallas_call(
         functools.partial(gather_kernel, tuple(moves), len(sources), logit_place),
@@ -542,23 +547,27 @@
         return key_head(place, group) * HEAD_DIM
 
     def inner_layout(group):
-        rows_total = gate_row + 16
-        tail_row = rows_total if group == groups - 1 else None
-        return tail_row, rows_total + (16 * groups if group == groups - 1 else 0)
+        later = [other for other in range(1, groups)] if group == 0 else []
+        asked = groups if group == groups - 1 else 0
+        tail_row = gate_row + 16
+        return later, asked, tail_row, tail_row + 16 * (len(later) * tiles + asked)
+
+    def inner_columns(place, group):
+        found = [key_width + key_head(place, group) * HEAD_DIM]
+        for h in range(share):
+            found.append(2 * key_width + (place * heads + group * share + h) * HEAD_DIM)
+        return found
 
     def inner_moves(group):
-        tail_row, _ = inner_layout(group)
+        later, asked, tail_row, _ = inner_layout(group)
         moves = []
         for place in range(cp_count):
-            found = [key_width + key_head(place, group) * HEAD_DIM]
-            for h in range(share):
-                found.append(2 * key_width + (place * heads + group * share + h) * HEAD_DIM)
-            for tile, column in enumerate(found):
+            for tile, column in enumerate(inner_columns(place, group)):
                 moves.append((0, 0, rows, column, place, tile * rows))
-            if tail_row is not None:
-                for other in range(groups):
-                    column = query_column(place, other)
-                    moves.append((0, rows - 16, 16, column, place, tail_row + 16 * other))
+            extra = [column for other in later for column in inner_columns(place, other)]
+            extra += [query_column(place, other) for other in range(asked)]
+            for spot, column in enumerate(extra):
+                moves.append((0, rows - 16, 16, column, place, tail_row + 16 * spot))
         return moves
 
     def outer_moves():
@@ -586,23 +595,26 @@
     def in_hbm(array):
         return pltpu.with_memory_space_constraint(array, pltpu.HBM)
 
-    received, tails = [], []
+    received = []
     for group in range(groups):
-        tail_row, rows_total = inner_layout(group)
+        later, asked, tail_row, rows_total = inner_layout(group)
         sent = gather(
             [in_hbm(mixed_qkv)],
             inner_moves(group),
             cp_count,
             rows_total,
-            logits=gate_logits.T,
+            logits=in_hbm(gate_logits.T),
             first_row=gate_row,
             heads=heads,
         )
         received.append(exchanged(sent))
-        places = [tile * rows + rows - 16 for tile in range(tiles)]
-        if tail_row is not None:
-            places += [tail_row + 16 * other for other in range(groups)]
-        tails.append(halo(received[group], places))
+        places = [tile * rows + rows - 16 for tile in range(tiles)] if group == 0 else []
+        places += [tail_row + 16 * spot for spot in range(len(later) * tiles + asked)]
+        if places:
+            arrived = halo(received[group], places)
+            if group == 0:
+                tails = [arrived[other * tiles : (other + 1) * tiles] for other in range(groups)]
+            query_tails = arrived[len(places) - asked :]
 
     packed = gather(
         [in_hbm(mixed_qkv), in_hbm(gate_z)], outer_moves(), cp_count, (groups + heads) * rows
@@ -690,9 +702,9 @@
 
     def finish(group, counts, incoming, buffers, lines):
         gate_start = (groups + group * share) * rows
-        dims = (group, share, tuple(counts), group * rows, gate_start, tiles + group)
+        dims = (group, share, tuple(counts), group * rows, gate_start, group)
         wide = (share, count * BLOCK, 2 * HEAD_DIM)
-        operands = [meta, outer, tails[-1], query_weights[group], incoming]
+        operands = [meta, outer, query_tails, query_weights[group], incoming]
         operands.append(norm_gain.reshape(1, HEAD_DIM))
         operands += [in_hbm(array) for array in buffers]
         operands += lines

time: 121 us -> 122 us (level)
  transfers between devices with their start and end apart: 13 -> 13, of which waited for: 7 -> 8; matrix products, arithmetic and copies ran while one was open for 3% -> 2% of each run, Pallas kernels for 34% -> 34%
where the time goes in v4:
time: 122 us; the launch traced here: 121 us
  Pallas kernels  44.7 us (37%)
  waiting for transfers between devices  42.6 us (35%)
  starting transfers between devices  29.7 us (24%)
  local copies, waits for them, and re-layouts  2.27 us (2%)
  other arithmetic  1.41 us (1%)
    all_to_all x5, waiting for transfers between devices, exchanged(): return lax.all_to_all(value, 'cp', split_axis=0, concat_axis=0, tiled=True)  24.5 us
    pallas_call x3, Pallas kernels, inner(): pl.pallas_call(functools.partial(inner_kernel, dims), out_shape=out_shape...  21.1 us
    all_to_all x5, starting transfers between devices, exchanged(): return lax.all_to_all(value, 'cp', split_axis=0, concat_axis=0, tiled=True)  19.9 us
    ppermute x8, waiting for transfers between devices, passed_round(): lax.ppermute(value, axis, [(i, (i + 1) % length) for i in range(length)])  18.1 us
    pallas_call x2, Pallas kernels, finish(): pl.pallas_call(functools.partial(finish_kernel, dims), out_shape=jax.Shap...  11.5 us
    ppermute x8, starting transfers between devices, passed_round(): lax.ppermute(value, axis, [(i, (i + 1) % length) for i in range(length)])  9.79 us
    pallas_call x3, Pallas kernels, gather(): pl.pallas_call(functools.partial(gather_kernel, tuple(moves), len(sources...  8.14 us
  transfers between devices with their start and end apart: 13, of which 8 were waited for; matrix products, arithmetic and copies ran while one was open for 2% of the time, Pallas kernels for 34%

profile of v4, /device:TPU:0, one launch (start us, length us, event | category | flops | bytes accessed | tf_op | source)
XLA Modules:
  0.0 121.1 jit_solution(2934556046474102963)
XLA Ops:
  0.0 0.0 copy-start.5
  0.0 2.6 %shard_map.85 = bf16[8,448,128]{2,1,0:T(8,128)(2,1)} custom-call(bf16[128,8192]{1,0:T(8,128)(2,1)} %refs_0_.5, bf16[64,128]{1,0:T(8,128)(2,1)} %bitcast.23), custom_call_target="tpu_custom_call" | custom-call | flops 800000000 | bytes 1048576 | tf_op jit(solution)/shard_map/pallas_call | solution.py:488
  2.7 0.0 copy-start.3
  2.7 0.0 copy-start.4
  2.7 5.2 %all-to-all-start.2 = ((bf16[8,448,128]{2,1,0:T(8,128)(2,1)}), bf16[8,448,128]{2,1,0:T(8,128)(2,1)S(1)}, u32[]{:S(2)}, u32[]{:S(2)}) async-start(bf16[8,448,128]{2,1,0:T(8,128)(2,1)} %shard_map.85), calls=%async_computation.2 | async-start | bytes 1835008 | tf_op jit(solution)/shard_map/all_to_all | solution.py:523
  7.9 0.0 copy-done.5
  7.9 1.3 %sort.17 = (s32[16]{0:T(128)}, s32[16]{0:T(128)S(1)}) sort(s32[16]{0:T(128)S(1)} %bitcast.27, s32[16]{0:T(128)S(1)} %iota.4), dimensions={0}, to_apply=%region_0.0 | sort | flops 64 | bytes 256 | tf_op jit(solution)/shard_map/jit(argsort)/sort | solution.py:539
  9.2 2.5 %shard_map.83 = bf16[8,432,128]{2,1,0:T(8,128)(2,1)} custom-call(bf16[128,8192]{1,0:T(8,128)(2,1)} %refs_0_.5, bf16[64,128]{1,0:T(8,128)(2,1)} %bitcast.24), custom_call_target="tpu_custom_call" | custom-call | flops 800000000 | bytes 1048576 | tf_op jit(solution)/shard_map/pallas_call | solution.py:488
  11.7 0.0 copy-done.3
  11.7 0.0 copy-done.4
  11.8 0.1 dynamic-slice_bitcast_fusion.6
  11.8 10.0 %all-to-all-done.2.arrived_ref.recv_ref = bf16[8,448,128]{2,1,0:T(8,128)(2,1)S(1)} async-done(((bf16[8,448,128]{2,1,0:T(8,128)(2,1)}), bf16[8,448,128]{2,1,0:T(8,128)(2,1)S(1)}, u32[]{:S(2)}, u32[]{:S(2)}) %all-to-all-start.2) | async-done | bytes 917536 | tf_op jit(solution)/shard_map/all_to_all | solution.py:523
  21.9 3.6 %all-to-all-start.1 = ((bf16[8,432,128]{2,1,0:T(8,128)(2,1)}), bf16[8,432,128]{2,1,0:T(8,128)(2,1)S(1)}, u32[]{:S(2)}, u32[]{:S(2)}) async-start(bf16[8,432,128]{2,1,0:T(8,128)(2,1)} %shard_map.83), calls=%async_computation.1 | async-start | bytes 1769472 | tf_op jit(solution)/shard_map/all_to_all | solution.py:523
  25.4 0.1 pad_add_fusion.meta_ref
  25.5 0.7 dynamic-slice_bitcast_fusion
  26.2 0.7 dynamic-slice_bitcast_fusion.2
  27.0 0.6 shard_map.86
  27.6 1.6 %collective-permute-start.1 = (bf16[6,16,128]{2,1,0:T(8,128)(2,1)S(1)}, bf16[6,16,128]{2,1,0:T(8,128)(2,1)S(1)}, u32[]{:S(2)}, u32[]{:S(2)}) collective-permute-start(bf16[6,16,128]{2,1,0:T(8,128)(2,1)S(1)} %shard_map.86), channel_id=1, source_target_pairs={{0,8},{8,16},{16,24},{24,0},{1,9},{9,17},{17,25},{25,1},{2,10},{10... | collective-permute-start | bytes 73736 | tf_op jit(solution)/shard_map/ppermute | solution.py:519
  29.2 3.0 %shard_map.82 = bf16[8,768,128]{2,1,0:T(8,128)(2,1)} custom-call(bf16[128,8192]{1,0:T(8,128)(2,1)} %refs_0_.5, bf16[128,4096]{1,0:T(8,128)(2,1)} %refs_1_.1), custom_call_target="tpu_custom_call" | custom-call | flops 800000000 | bytes 1048576 | tf_op jit(solution)/shard_map/pallas_call | solution.py:488
  32.2 1.1 collective-permute-done.1
  33.3 5.7 %all-to-all-done.1.arrived_ref.recv_ref = bf16[8,432,128]{2,1,0:T(8,128)(2,1)S(1)} async-done(((bf16[8,432,128]{2,1,0:T(8,128)(2,1)}), bf16[8,432,128]{2,1,0:T(8,128)(2,1)S(1)}, u32[]{:S(2)}, u32[]{:S(2)}) %all-to-all-start.1) | async-done | bytes 884768 | tf_op jit(solution)/shard_map/all_to_all | solution.py:523
  39.0 3.6 %all-to-all-start = ((bf16[8,768,128]{2,1,0:T(8,128)(2,1)}), bf16[8,768,128]{2,1,0:T(8,128)(2,1)S(1)}, u32[]{:S(2)}, u32[]{:S(2)}) async-start(bf16[8,768,128]{2,1,0:T(8,128)(2,1)} %shard_map.82), calls=%async_computation | async-start | bytes 3145728 | tf_op jit(solution)/shard_map/all_to_all | solution.py:523
  42.6 0.1 broadcast_in_dim.2.rate_ref
  42.6 9.6 %shard_map.92 = (f32[2,1024,256]{2,1,0:T(8,128)}, f32[2,1024,256]{2,1,0:T(8,128)}, f32[8,128,128]{2,1,0:T(8,128)}, f32[2,8,8,128]{3,2,1,0:T(8,128)S(1)}, f32[2,1...) custom-call(s32[17]{0:T(128)S(1)} %pad_add_fusion.meta_ref, ...), custom_call_target="tpu_custom_call" | custom-call | flops 9600000000 | bytes 1048576 | tf_op jit(solution)/shard_map/pallas_call | solution.py:666
  52.2 1.6 %collective-permute-start.5 = (f32[2,128,128]{2,1,0:T(8,128)S(1)}, f32[2,128,128]{2,1,0:T(8,128)S(1)}, u32[]{:S(2)}, u32[]{:S(2)}) collective-permute-start(f32[2,128,128]{2,1,0:T(8,128)S(1)} %get-tuple-element.35.shift_ref), channel_id=1, source_target_pairs={{0,8},{8,16},{16,24},{24,0},{1,9},{9,17},{17,25},{25,1},{2,10},{10... | collective-permute-start | bytes 393224 | tf_op jit(solution)/shard_map/ppermute | solution.py:519
  53.8 0.6 shard_map.84
  54.4 1.6 %collective-permute-start = (bf16[2,16,128]{2,1,0:T(8,128)(2,1)S(1)}, bf16[2,16,128]{2,1,0:T(8,128)(2,1)S(1)}, u32[]{:S(2)}, u32[]{:S(2)}) collective-permute-start(bf16[2,16,128]{2,1,0:T(8,128)(2,1)S(1)} %shard_map.84), channel_id=1, source_target_pairs={{0,8},{8,16},{16,24},{24,0},{1,9},{9,17},{17,25},{25,1},{2,10},{10... | collective-permute-start | bytes 24584 | tf_op jit(solution)/shard_map/ppermute | solution.py:519
  56.1 4.0 %collective-permute-done.5.incoming_ref = f32[2,128,128]{2,1,0:T(8,128)S(1)} collective-permute-done((f32[2,128,128]{2,1,0:T(8,128)S(1)}, f32[2,128,128]{2,1,0:T(8,128)S(1)}, u32[]{:S(2)}, u32[]{:S(2)}) %collective-permute-start.5) | collective-permute-done | bytes 131104 | tf_op jit(solution)/shard_map/ppermute | solution.py:519
  60.0 0.2 shard_map.93
  60.2 0.2 collective-permute-start.6
  60.5 5.8 %shard_map.87 = (f32[2,1024,256]{2,1,0:T(8,128)}, f32[2,1024,256]{2,1,0:T(8,128)}, f32[8,128,128]{2,1,0:T(8,128)}, f32[2,4,8,128]{3,2,1,0:T(8,128)S(1)}, f32[2,128,256]{2,1,0:T(8,128)S(1)}) custom-call(s32[17]{0:T(128)S(1)} %pad_add_fusion.meta_ref, bf16[8,432,128]{2,1,0:T(8,128)(2,1)S(1)} %all-to-all-done.1.arrived_ref.recv_ref, ...), custom_call_target="tpu_custom_call" | custom-call | flops 4800000000 | bytes 1048576 | tf_op jit(solution)/shard_map/pallas_call | solution.py:666
  66.3 0.9 collective-permute-done.6.incoming_ref
  67.2 0.2 shard_map.94
  67.4 0.4 collective-permute-start.7
  67.8 0.0 copy-start
  67.8 5.8 %shard_map.88 = (f32[2,1024,256]{2,1,0:T(8,128)}, f32[2,1024,256]{2,1,0:T(8,128)}, f32[8,128,128]{2,1,0:T(8,128)}, f32[2,4,8,128]{3,2,1,0:T(8,128)S(1)}, f32[2,1...) custom-call(s32[17]{0:T(128)S(1)} %pad_add_fusion.meta_ref, ...), custom_call_target="tpu_custom_call", output_to_operand_aliasing={{0}: (6, {}), {1}: (7, {}), {2}: (8, {})} | custom-call | flops 4800000000 | bytes 1048576 | tf_op jit(solution)/shard_map/pallas_call | solution.py:666
  73.6 0.0 copy-start.1
  73.6 0.6 copy-done.1
  74.3 1.6 %collective-permute-start.2 = (f32[2,128,128]{2,1,0:T(8,128)S(1)}, f32[2,128,128]{2,1,0:T(8,128)S(1)}, u32[]{:S(2)}, u32[]{:S(2)}) collective-permute-start(f32[2,128,128]{2,1,0:T(8,128)S(1)} %get-tuple-element.28.shift_ref), channel_id=1, source_target_pairs={{0,8},{8,16},{16,24},{24,0},{1,9},{9,17},{17,25},{25,1},{2,10},{10... | collective-permute-start | bytes 393224 | tf_op jit(solution)/shard_map/ppermute | solution.py:519
  75.8 0.0 collective-permute-done.tail_ref
  75.9 0.0 collective-permute-done.7.incoming_ref
  75.9 0.0 all-to-all-done.outer_ref
  75.9 0.0 copy-done
  75.9 0.0 copy-start.2
  75.9 5.8 %shard_map.95 = bf16[8,256,128]{2,1,0:T(8,128)(2,1)} custom-call(s32[17]{0:T(128)S(1)} %pad_add_fusion.meta_ref, bf16[8,768,128]{2,1,0:T(8,128)(2,1)S(1)} %all-to-all-done.outer_ref, bf16[2,16,128]{2,1,0:T(8,128)(2,1)S(1)} %collective-permute-done.tail_ref, f32[1,4,128]{2,1,0:T(4,128)S(1)} %get-tuple-element.42.weight_ref, ...), custom_call_target="tpu_custom_call" | custom-call | flops 1500000000 | bytes 1048576 | tf_op jit(solution)/shard_map/pallas_call | solution.py:711
  81.7 3.9 %all-to-all-start.4 = ((bf16[8,256,128]{2,1,0:T(8,128)(2,1)}), bf16[8,256,128]{2,1,0:T(8,128)(2,1)S(1)}, u32[]{:S(2)}, u32[]{:S(2)}) async-start(bf16[8,256,128]{2,1,0:T(8,128)(2,1)} %shard_map.95), calls=%async_computation.4 | async-start | bytes 1048576 | tf_op jit(solution)/shard_map/all_to_all | solution.py:523
  85.6 0.0 collective-permute-done.2.incoming_ref
  85.6 0.0 copy-done.2
  85.6 0.2 shard_map.89
  85.8 2.1 %collective-permute-start.3 = (f32[2,128,128]{2,1,0:T(8,128)S(1)}, f32[2,128,128]{2,1,0:T(8,128)S(1)}, u32[]{:S(2)}, u32[]{:S(2)}) collective-permute-start(f32[2,128,128]{2,1,0:T(8,128)S(1)} %shard_map.89), channel_id=1, source_target_pairs={{0,8},{8,16},{16,24},{24,0},{1,9},{9,17},{17,25},{25,1},{2,10},{10... | collective-permute-start | bytes 393224 | tf_op jit(solution)/shard_map/ppermute | solution.py:519
  87.9 5.6 %collective-permute-done.3.incoming_ref = f32[2,128,128]{2,1,0:T(8,128)S(1)} collective-permute-done((f32[2,128,128]{2,1,0:T(8,128)S(1)}, f32[2,128,128]{2,1,0:T(8,128)S(1)}, u32[]{:S(2)}, u32[]{:S(2)}) %collective-permute-start.3) | collective-permute-done | bytes 131104 | tf_op jit(solution)/shard_map/ppermute | solution.py:519
  93.5 0.2 shard_map.90
  93.7 0.6 collective-permute-start.4
  94.3 6.6 %collective-permute-done.4.incoming_ref = f32[2,128,128]{2,1,0:T(8,128)S(1)} collective-permute-done((f32[2,128,128]{2,1,0:T(8,128)S(1)}, f32[2,128,128]{2,1,0:T(8,128)S(1)}, u32[]{:S(2)}, u32[]{:S(2)}) %collective-permute-start.4) | collective-permute-done | bytes 131104 | tf_op jit(solution)/shard_map/ppermute | solution.py:519
  100.9 5.7 %shard_map.91 = bf16[8,256,128]{2,1,0:T(8,128)(2,1)} custom-call(s32[17]{0:T(128)S(1)} %pad_add_fusion.meta_ref, bf16[8,768,128]{2,1,0:T(8,128)(2,1)S(1)} %all-to-all-done.outer_ref, bf16[2,16,128]{2,1,0:T(8,128)(2,1)S(1)} %collective-permute-done.tail_ref, f32[1,4,128]{2,1,0:T(4,128)S(1)} %get-tuple-element.44.weight_ref, ...), custom_call_target="tpu_custom_call" | custom-call | flops 1500000000 | bytes 1048576 | tf_op jit(solution)/shard_map/pallas_call | solution.py:711
  106.6 0.0 all-to-all-done.4.refs_0_
  106.6 3.7 %all-to-all-start.3 = ((bf16[8,256,128]{2,1,0:T(8,128)(2,1)}), bf16[8,256,128]{2,1,0:T(8,128)(2,1)S(1)}, u32[]{:S(2)}, u32[]{:S(2)}) async-start(bf16[8,256,128]{2,1,0:T(8,128)(2,1)} %shard_map.91), calls=%async_computation.3 | async-start | bytes 1048576 | tf_op jit(solution)/shard_map/all_to_all | solution.py:523
  110.3 0.9 shard_map.96.refs_1_
  111.3 8.8 %all-to-all-done.3.refs_0_ = bf16[8,256,128]{2,1,0:T(8,128)(2,1)S(1)} async-done(((bf16[8,256,128]{2,1,0:T(8,128)(2,1)}), bf16[8,256,128]{2,1,0:T(8,128)(2,1)S(1)}, u32[]{:S(2)}, u32[]{:S(2)}) %all-to-all-start.3) | async-done | bytes 524320 | tf_op jit(solution)/shard_map/all_to_all | solution.py:523
  120.1 0.9 shard_map.97
  (5 shorter events, 0.0 us)
Async XLA Ops:
  0.0 7.9 %copy-start.5 = (s32[1,16]{1,0:T(1,128)S(1)}, s32[1,16]{1,0:T(1,128)}, u32[]{:S(2)}) copy-start(s32[1,16]{1,0:T(1,128)} %param.11) | copy-start | bytes 196
  2.7 9.1 %copy-start.3 = (f32[32]{0:T(128)S(1)}, f32[32]{0:T(128)}, u32[]{:S(2)}) copy-start(f32[32]{0:T(128)} %param.14) | copy-start | bytes 388
  2.7 9.1 %copy-start.4 = (f32[32]{0:T(128)S(1)}, f32[32]{0:T(128)}, u32[]{:S(2)}) copy-start(f32[32]{0:T(128)} %param.13) | copy-start | bytes 388
  2.7 19.2 %all-to-all-start.2 = ((bf16[8,448,128]{2,1,0:T(8,128)(2,1)}), bf16[8,448,128]{2,1,0:T(8,128)(2,1)S(1)}, u32[]{:S(2)}, u32[]{:S(2)}) async-start(bf16[8,448,128]{2,1,0:T(8,128)(2,1)} %shard_map.85), calls=%async_computation.2 | async-start | bytes 1835008 | tf_op jit(solution)/shard_map/all_to_all | solution.py:523
  21.9 17.1 %all-to-all-start.1 = ((bf16[8,432,128]{2,1,0:T(8,128)(2,1)}), bf16[8,432,128]{2,1,0:T(8,128)(2,1)S(1)}, u32[]{:S(2)}, u32[]{:S(2)}) async-start(bf16[8,432,128]{2,1,0:T(8,128)(2,1)} %shard_map.83), calls=%async_computation.1 | async-start | bytes 1769472 | tf_op jit(solution)/shard_map/all_to_all | solution.py:523
  27.6 5.7 %collective-permute-start.1 = (bf16[6,16,128]{2,1,0:T(8,128)(2,1)S(1)}, bf16[6,16,128]{2,1,0:T(8,128)(2,1)S(1)}, u32[]{:S(2)}, u32[]{:S(2)}) collective-permute-start(bf16[6,16,128]{2,1,0:T(8,128)(2,1)S(1)} %shard_map.86), channel_id=1, source_target_pairs={{0,8},{8,16},{16,24},{24,0},{1,9},{9,17},{17,25},{25,1},{2,10},{10... | collective-permute-start | bytes 73736 | tf_op jit(solution)/shard_map/ppermute | solution.py:519
  39.0 36.9 %all-to-all-start = ((bf16[8,768,128]{2,1,0:T(8,128)(2,1)}), bf16[8,768,128]{2,1,0:T(8,128)(2,1)S(1)}, u32[]{:S(2)}, u32[]{:S(2)}) async-start(bf16[8,768,128]{2,1,0:T(8,128)(2,1)} %shard_map.82), calls=%async_computation | async-start | bytes 3145728 | tf_op jit(solution)/shard_map/all_to_all | solution.py:523
  52.2 7.8 %collective-permute-start.5 = (f32[2,128,128]{2,1,0:T(8,128)S(1)}, f32[2,128,128]{2,1,0:T(8,128)S(1)}, u32[]{:S(2)}, u32[]{:S(2)}) collective-permute-start(f32[2,128,128]{2,1,0:T(8,128)S(1)} %get-tuple-element.35.shift_ref), channel_id=1, source_target_pairs={{0,8},{8,16},{16,24},{24,0},{1,9},{9,17},{17,25},{25,1},{2,10},{10... | collective-permute-start | bytes 393224 | tf_op jit(solution)/shard_map/ppermute | solution.py:519
  54.4 21.4 %collective-permute-start = (bf16[2,16,128]{2,1,0:T(8,128)(2,1)S(1)}, bf16[2,16,128]{2,1,0:T(8,128)(2,1)S(1)}, u32[]{:S(2)}, u32[]{:S(2)}) collective-permute-start(bf16[2,16,128]{2,1,0:T(8,128)(2,1)S(1)} %shard_map.84), channel_id=1, source_target_pairs={{0,8},{8,16},{16,24},{24,0},{1,9},{9,17},{17,25},{25,1},{2,10},{10... | collective-permute-start | bytes 24584 | tf_op jit(solution)/shard_map/ppermute | solution.py:519
  60.2 7.0 %collective-permute-start.6 = (f32[2,128,128]{2,1,0:T(8,128)S(1)}, f32[2,128,128]{2,1,0:T(8,128)S(1)}, u32[]{:S(2)}, u32[]{:S(2)}) collective-permute-start(f32[2,128,128]{2,1,0:T(8,128)S(1)} %shard_map.93), channel_id=1, source_target_pairs={{0,8},{8,16},{16,24},{24,0},{1,9},{9,17},{17,25},{25,1},{2,10},{10... | collective-permute-start | bytes 393224 | tf_op jit(solution)/shard_map/ppermute | solution.py:519
  67.4 8.4 %collective-permute-start.7 = (f32[2,128,128]{2,1,0:T(8,128)S(1)}, f32[2,128,128]{2,1,0:T(8,128)S(1)}, u32[]{:S(2)}, u32[]{:S(2)}) collective-permute-start(f32[2,128,128]{2,1,0:T(8,128)S(1)} %shard_map.94), channel_id=1, source_target_pairs={{0,8},{8,16},{16,24},{24,0},{1,9},{9,17},{17,25},{25,1},{2,10},{10... | collective-permute-start | bytes 393224 | tf_op jit(solution)/shard_map/ppermute | solution.py:519
  67.8 8.1 %copy-start = (f32[128]{0:T(128)S(1)}, f32[128]{0:T(128)}, u32[]{:S(2)}) copy-start(f32[128]{0:T(128)} %param.15) | copy-start | bytes 1540
  73.6 0.7 copy-start.1
  74.3 11.3 %collective-permute-start.2 = (f32[2,128,128]{2,1,0:T(8,128)S(1)}, f32[2,128,128]{2,1,0:T(8,128)S(1)}, u32[]{:S(2)}, u32[]{:S(2)}) collective-permute-start(f32[2,128,128]{2,1,0:T(8,128)S(1)} %get-tuple-element.28.shift_ref), channel_id=1, source_target_pairs={{0,8},{8,16},{16,24},{24,0},{1,9},{9,17},{17,25},{25,1},{2,10},{10... | collective-permute-start | bytes 393224 | tf_op jit(solution)/shard_map/ppermute | solution.py:519
  75.9 9.7 %copy-start.2 = (bf16[2,128,256]{2,1,0:T(8,128)(2,1)S(1)}, bf16[2,128,256]{2,1,0:T(8,128)(2,1)}, u32[]{:S(2)}) copy-start(bf16[2,128,256]{2,1,0:T(8,128)(2,1)} %copy-done.1) | copy-start | bytes 393220
  81.7 24.9 %all-to-all-start.4 = ((bf16[8,256,128]{2,1,0:T(8,128)(2,1)}), bf16[8,256,128]{2,1,0:T(8,128)(2,1)S(1)}, u32[]{:S(2)}, u32[]{:S(2)}) async-start(bf16[8,256,128]{2,1,0:T(8,128)(2,1)} %shard_map.95), calls=%async_computation.4 | async-start | bytes 1048576 | tf_op jit(solution)/shard_map/all_to_all | solution.py:523
  85.8 7.8 %collective-permute-start.3 = (f32[2,128,128]{2,1,0:T(8,128)S(1)}, f32[2,128,128]{2,1,0:T(8,128)S(1)}, u32[]{:S(2)}, u32[]{:S(2)}) collective-permute-start(f32[2,128,128]{2,1,0:T(8,128)S(1)} %shard_map.89), channel_id=1, source_target_pairs={{0,8},{8,16},{16,24},{24,0},{1,9},{9,17},{17,25},{25,1},{2,10},{10... | collective-permute-start | bytes 393224 | tf_op jit(solution)/shard_map/ppermute | solution.py:519
  93.7 7.1 %collective-permute-start.4 = (f32[2,128,128]{2,1,0:T(8,128)S(1)}, f32[2,128,128]{2,1,0:T(8,128)S(1)}, u32[]{:S(2)}, u32[]{:S(2)}) collective-permute-start(f32[2,128,128]{2,1,0:T(8,128)S(1)} %shard_map.90), channel_id=1, source_target_pairs={{0,8},{8,16},{16,24},{24,0},{1,9},{9,17},{17,25},{25,1},{2,10},{10... | collective-permute-start | bytes 393224 | tf_op jit(solution)/shard_map/ppermute | solution.py:519
  106.6 13.5 %all-to-all-start.3 = ((bf16[8,256,128]{2,1,0:T(8,128)(2,1)}), bf16[8,256,128]{2,1,0:T(8,128)(2,1)S(1)}, u32[]{:S(2)}, u32[]{:S(2)}) async-start(bf16[8,256,128]{2,1,0:T(8,128)(2,1)} %shard_map.91), calls=%async_computation.3 | async-start | bytes 1048576 | tf_op jit(solution)/shard_map/all_to_all | solution.py:523

commit v5 on v4

--- a/solution.py
+++ b/solution.py
@@ -304,7 +304,7 @@
     group, share, counts, query_row, gate_row, tail_place = dims
     count = sum(counts)
     line_refs = refs[: len(counts)]
-    out_ref, solved_ref, before_ref, flip_ref, rows_ref, sems = refs[len(counts) :]
+    out_hbm, out_ref, solved_ref, before_ref, flip_ref, rows_ref, sems = refs[len(counts) :]
     piece_rows = BLOCK // 2
     is_first = meta_ref[meta_ref.shape[0] - 1]
     row_index = lax.broadcasted_iota(jnp.int32, (BLOCK, BLOCK), 0)
@@ -318,6 +318,13 @@
             pltpu.make_async_copy(state_in.at[:, at, :], before_ref.at[:, at, :], sems.at[1, n]),
             pltpu.make_async_copy(solved_in.at[:, at, :], solved_ref.at[:, at, :], sems.at[2, n]),
         )
+
+    def leaving(n):
+        return pltpu.make_async_copy(out_ref.at[n], out_hbm.at[n], sems.at[3, n])
+
+    def drain(n, carry):
+        leaving(n).wait()
+        return carry
 
     def fetch(n, carry):
         for copy in arriving(n):
@@ -379,6 +386,8 @@
             gate = below(*gates)
             result = core * scale * gain_ref[...] * silu(gate)
             out_ref[n, h * BLOCK : (h + 1) * BLOCK, :] = result.astype(BF16)
+            if h == share - 1:
+                leaving(n).start()
         return carry
 
     first_block = 0
@@ -390,38 +399,60 @@
         else:
             lax.fori_loop(0, blocks // per_step, part, 0)
         first_block += blocks
-
-
-def gather_kernel(moves, source_count, logit_place, *refs):
-    sources, refs = refs[:source_count], refs[source_count:]
+    lax.fori_loop(0, count, drain, 0)
+
+
+def gather_kernel(moves, ends, source_count, logit_place, *refs):
+    sources, refs = refs[:source_count], list(refs[source_count:])
+    logit_ref = refs.pop(0) if logit_place else None
+    out_hbm, out_ref, sems, out_sems = refs[:4]
+    refs = refs[4:]
+    if ends:
+        end_sem, end_ref = refs.pop(), refs.pop()
+        rows = sources[0].shape[0]
+        end_copy = pltpu.make_async_copy(
+            sources[0].at[pl.ds(rows - 16, 16), :], end_ref, end_sem.at[0]
+        )
+        end_copy.start()
     if logit_place:
-        logit_ref, out_ref, sems, wide_ref, plain_ref, logit_sem = refs
+        wide_ref, plain_ref, logit_sem = refs
         fetch = pltpu.make_async_copy(logit_ref, plain_ref, logit_sem.at[0])
         fetch.start()
-    else:
-        out_ref, sems = refs
-    copies = []
+    places = out_ref.shape[0]
+    copies = [[] for _ in range(places)]
     for number, (source, begin, length, column, place, row) in enumerate(moves):
-        copies.append(
+        copies[place].append(
             pltpu.make_async_copy(
                 sources[source].at[pl.ds(begin, length), pl.ds(column, HEAD_DIM)],
                 out_ref.at[place, pl.ds(row, length), :],
                 sems.at[number],
             )
         )
-    for copy in copies:
+    for copy in [copy for group in copies for copy in group]:
         copy.start()
     if logit_place:
         first_row, heads = logit_place
         wide_ref[...] = jnp.zeros(wide_ref.shape, F32)
         fetch.wait()
         wide_ref[0 : 2 * VALUE_HEADS, :] = plain_ref[...].astype(F32)
-        for place in range(out_ref.shape[0]):
+        for place in range(places):
             begin = place * heads
             rates = wide_ref[begin : begin + 8, :]
             steps = wide_ref[VALUE_HEADS + begin : VALUE_HEADS + begin + 8, :]
             out_ref[place, first_row : first_row + 16, :] = below(rates, steps).astype(BF16)
-    for copy in copies:
+    if ends:
+        end_copy.wait()
+        for column, place, row in ends:
+            out_ref[place, row : row + 16, :] = end_ref[:, column : column + HEAD_DIM]
+    leaving = [
+        pltpu.make_async_copy(out_ref.at[place], out_hbm.at[place], out_sems.at[place])
+        for place in range(places)
+    ]
+    for place in range(places):
+        for copy in copies[place]:
+            copy.wait()
+        leaving[place].start()
+    for copy in leaving:
         copy.wait()
 
 
@@ -476,7 +507,7 @@
 
 def gather(sources, moves, places, rows, logits=None, first_row=0, heads=0):
     operands, in_specs = list(sources), [anywhere] * len(sources)
-    scratch = [pltpu.SemaphoreType.DMA((len(moves),))]
+    scratch = []
     logit_place = None
     if logits is not None:
         operands.append(logits)
@@ -485,11 +516,21 @@
         scratch.append(pltpu.VMEM(logits.shape, BF16))
         scratch.append(pltpu.SemaphoreType.DMA((1,)))
         logit_place = (first_row, heads)
+    ends = [(move[3], move[4], move[5]) for move in moves if move[2] == 16]
+    moves = [move for move in moves if move[2] != 16]
+    scratch = [
+        pltpu.VMEM((places, rows, HEAD_DIM), BF16),
+        pltpu.SemaphoreType.DMA((len(moves),)),
+        pltpu.SemaphoreType.DMA((places,)),
+    ] + scratch
+    if ends:
+        scratch.append(pltpu.VMEM((16, sources[0].shape[1]), BF16))
+        scratch.append(pltpu.SemaphoreType.DMA((1,)))
     return pl.pallas_call(
-        functools.partial(gather_kernel, tuple(moves), len(sources), logit_place),
-        out_shape=jax.ShapeDtypeStruct((places, rows, HEAD_DIM), BF16),
+        functools.partial(gather_kernel, tuple(moves), tuple(ends), len(sources), logit_place),
+        out_shape=pltpu.HBM((places, rows, HEAD_DIM), BF16),
         in_specs=in_specs,
-        out_specs=vmem,
+        out_specs=stored,
         scratch_shapes=scratch,
         compiler_params=limits(GATHER_MIB),
         cost_estimate=cost(8e8),
@@ -548,7 +589,7 @@
 
     def inner_layout(group):
         later = [other for other in range(1, groups)] if group == 0 else []
-        asked = groups if group == groups - 1 else 0
+        asked = groups if group == 0 else 0
         tail_row = gate_row + 16
         return later, asked, tail_row, tail_row + 16 * (len(later) * tiles + asked)
 
@@ -710,15 +751,16 @@
         operands += lines
         return pl.pallas_call(
             functools.partial(finish_kernel, dims),
-            out_shape=jax.ShapeDtypeStruct((count, share * BLOCK, HEAD_DIM), BF16),
+            out_shape=pltpu.HBM((count, share * BLOCK, HEAD_DIM), BF16),
             in_specs=[smem] + [vmem] * 5 + [stored] * 3 + [vmem] * len(lines),
-            out_specs=vmem,
+            out_specs=stored,
             scratch_shapes=[
+                pltpu.VMEM((count, share * BLOCK, HEAD_DIM), BF16),
                 pltpu.VMEM(wide, F32),
                 pltpu.VMEM(wide, F32),
                 pltpu.VMEM((count, HEAD_DIM, BLOCK), F32),
                 pltpu.VMEM((4, 8 + BLOCK, HEAD_DIM), F32),
-                pltpu.SemaphoreType.DMA((3, count)),
+                pltpu.SemaphoreType.DMA((4, count)),
             ],
             compiler_params=limits(FINISH_MIB),
             cost_estimate=cost(1.5e9),
@@ -726,7 +768,7 @@
 
     result = None
     for group in range(groups):
-        parts = 2 if group and count % 8 == 0 else 1
+        parts = 1
         blocks = count // parts
         earlier, lines = None, []
         for part in range(parts):

time: 122 us -> 124 us (1.016)
  waiting for transfers between devices: 42.6 us -> 52.8 us
  starting transfers between devices: 29.7 us -> 24.7 us
  Pallas kernels: 44.7 us -> 41.2 us
    ppermute x8 -> x7, waiting for transfers between devices: 18.1 us -> 28.2 us  [passed_round(): lax.ppermute(value, axis, [(i, (i + 1) % length) for i in range(length)])]
    ppermute x8 -> x7, starting transfers between devices: 9.79 us -> 5.04 us  [passed_round(): lax.ppermute(value, axis, [(i, (i + 1) % length) for i in range(length)])]
    pallas_call x3 -> x2, Pallas kernels: 21.1 us -> 19.2 us  [inner(): pl.pallas_call(functools.partial(inner_kernel, dims), out_shape=out_shape...]
  transfers between devices with their start and end apart: 13 -> 12, of which waited for: 8 -> 8; matrix products, arithmetic and copies ran while one was open for 2% -> 2% of each run, Pallas kernels for 34% -> 31%
where the time goes in v5:
time: 124 us; the launch traced here: 123 us
  waiting for transfers between devices  52.8 us (43%)
  Pallas kernels  41.2 us (33%)
  starting transfers between devices  24.7 us (20%)
  local copies, waits for them, and re-layouts  2.26 us (2%)
  other arithmetic  1.36 us (1%)
    ppermute x7, waiting for transfers between devices, passed_round(): lax.ppermute(value, axis, [(i, (i + 1) % length) for i in range(length)])  28.2 us
    all_to_all x5, waiting for transfers between devices, exchanged(): return lax.all_to_all(value, 'cp', split_axis=0, concat_axis=0, tiled=True)  24.6 us
    all_to_all x5, starting transfers between devices, exchanged(): return lax.all_to_all(value, 'cp', split_axis=0, concat_axis=0, tiled=True)  19.6 us
    pallas_call x2, Pallas kernels, inner(): pl.pallas_call(functools.partial(inner_kernel, dims), out_shape=out_shape...  19.2 us
    pallas_call x2, Pallas kernels, finish(): pl.pallas_call(functools.partial(finish_kernel, dims), out_shape=pltpu.HB...  11.3 us
    pallas_call x3, Pallas kernels, gather(): pl.pallas_call(functools.partial(gather_kernel, tuple(moves), tuple(ends)...  7.41 us
    ppermute x7, starting transfers between devices, passed_round(): lax.ppermute(value, axis, [(i, (i + 1) % length) for i in range(length)])  5.04 us
  transfers between devices with their start and end apart: 12, of which 8 were waited for; matrix products, arithmetic and copies ran while one was open for 2% of the time, Pallas kernels for 31%

profile of v5, /device:TPU:0, one launch (start us, length us, event | category | flops | bytes accessed | tf_op | source)
XLA Modules:
  0.0 122.8 jit_solution(17880657498259938700)
XLA Ops:
  0.0 0.0 copy-start.5
  0.0 2.6 %shard_map.83 = bf16[8,480,128]{2,1,0:T(8,128)(2,1)} custom-call(bf16[128,8192]{1,0:T(8,128)(2,1)} %refs_0_.5, bf16[64,128]{1,0:T(8,128)(2,1)} %bitcast.23), custom_call_target="tpu_custom_call" | custom-call | flops 800000000 | bytes 1048576 | tf_op jit(solution)/shard_map/pallas_call | solution.py:529
  2.6 0.0 copy-start.3
  2.6 0.0 copy-start.4
  2.6 5.2 %all-to-all-start.1 = ((bf16[8,480,128]{2,1,0:T(8,128)(2,1)}), bf16[8,480,128]{2,1,0:T(8,128)(2,1)S(1)}, u32[]{:S(2)}, u32[]{:S(2)}) async-start(bf16[8,480,128]{2,1,0:T(8,128)(2,1)} %shard_map.83), calls=%async_computation.1 | async-start | bytes 1966080 | tf_op jit(solution)/shard_map/all_to_all | solution.py:564
  7.8 0.0 copy-done.5
  7.9 1.3 %sort.17 = (s32[16]{0:T(128)}, s32[16]{0:T(128)S(1)}) sort(s32[16]{0:T(128)S(1)} %bitcast.27, s32[16]{0:T(128)S(1)} %iota.4), dimensions={0}, to_apply=%region_0.0 | sort | flops 64 | bytes 256 | tf_op jit(solution)/shard_map/jit(argsort)/sort | solution.py:580
  9.1 2.3 %shard_map.85 = bf16[8,400,128]{2,1,0:T(8,128)(2,1)} custom-call(bf16[128,8192]{1,0:T(8,128)(2,1)} %refs_0_.5, bf16[64,128]{1,0:T(8,128)(2,1)} %bitcast.24), custom_call_target="tpu_custom_call" | custom-call | flops 800000000 | bytes 1048576 | tf_op jit(solution)/shard_map/pallas_call | solution.py:529
  11.4 0.0 copy-done.3
  11.4 0.0 copy-done.4
  11.4 0.1 dynamic-slice_bitcast_fusion.6
  11.5 11.0 %all-to-all-done.1.arrived_ref.recv_ref = bf16[8,480,128]{2,1,0:T(8,128)(2,1)S(1)} async-done(((bf16[8,480,128]{2,1,0:T(8,128)(2,1)}), bf16[8,480,128]{2,1,0:T(8,128)(2,1)S(1)}, u32[]{:S(2)}, u32[]{:S(2)}) %all-to-all-start.1) | async-done | bytes 983072 | tf_op jit(solution)/shard_map/all_to_all | solution.py:564
  22.5 3.5 %all-to-all-start.2 = ((bf16[8,400,128]{2,1,0:T(8,128)(2,1)}), bf16[8,400,128]{2,1,0:T(8,128)(2,1)S(1)}, u32[]{:S(2)}, u32[]{:S(2)}) async-start(bf16[8,400,128]{2,1,0:T(8,128)(2,1)} %shard_map.85), calls=%async_computation.2 | async-start | bytes 1638400 | tf_op jit(solution)/shard_map/all_to_all | solution.py:564
  26.1 0.1 pad_add_fusion.meta_ref
  26.1 0.7 dynamic-slice_bitcast_fusion
  26.9 0.7 dynamic-slice_bitcast_fusion.2
  27.6 0.7 shard_map.84
  28.3 1.6 %collective-permute-start = (bf16[8,16,128]{2,1,0:T(8,128)(2,1)S(1)}, bf16[8,16,128]{2,1,0:T(8,128)(2,1)S(1)}, u32[]{:S(2)}, u32[]{:S(2)}) collective-permute-start(bf16[8,16,128]{2,1,0:T(8,128)(2,1)S(1)} %shard_map.84), channel_id=1, source_target_pairs={{0,8},{8,16},{16,24},{24,0},{1,9},{9,17},{17,25},{25,1},{2,10},{10... | collective-permute-start | bytes 98312 | tf_op jit(solution)/shard_map/ppermute | solution.py:560
  29.9 2.6 %shard_map.82 = bf16[8,768,128]{2,1,0:T(8,128)(2,1)} custom-call(bf16[128,8192]{1,0:T(8,128)(2,1)} %refs_0_.5, bf16[128,4096]{1,0:T(8,128)(2,1)} %refs_1_.1), custom_call_target="tpu_custom_call" | custom-call | flops 800000000 | bytes 1048576 | tf_op jit(solution)/shard_map/pallas_call | solution.py:529
  32.5 1.6 %collective-permute-done = bf16[8,16,128]{2,1,0:T(8,128)(2,1)S(1)} collective-permute-done((bf16[8,16,128]{2,1,0:T(8,128)(2,1)S(1)}, bf16[8,16,128]{2,1,0:T(8,128)(2,1)S(1)}, u32[]{:S(2)}, u32[]{:S(2)}) %collective-permute-start) | collective-permute-done | bytes 32800 | tf_op jit(solution)/shard_map/ppermute | solution.py:560
  34.1 4.9 %all-to-all-done.2.recv_ref = bf16[8,400,128]{2,1,0:T(8,128)(2,1)S(1)} async-done(((bf16[8,400,128]{2,1,0:T(8,128)(2,1)}), bf16[8,400,128]{2,1,0:T(8,128)(2,1)S(1)}, u32[]{:S(2)}, u32[]{:S(2)}) %all-to-all-start.2) | async-done | bytes 819232 | tf_op jit(solution)/shard_map/all_to_all | solution.py:564
  38.9 3.6 %all-to-all-start = ((bf16[8,768,128]{2,1,0:T(8,128)(2,1)}), bf16[8,768,128]{2,1,0:T(8,128)(2,1)S(1)}, u32[]{:S(2)}, u32[]{:S(2)}) async-start(bf16[8,768,128]{2,1,0:T(8,128)(2,1)} %shard_map.82), calls=%async_computation | async-start | bytes 3145728 | tf_op jit(solution)/shard_map/all_to_all | solution.py:564
  42.5 0.1 broadcast_in_dim.2.rate_ref
  42.6 9.6 %shard_map.90 = (f32[2,1024,256]{2,1,0:T(8,128)}, f32[2,1024,256]{2,1,0:T(8,128)}, f32[8,128,128]{2,1,0:T(8,128)}, f32[2,8,8,128]{3,2,1,0:T(8,128)S(1)}, f32[2,1...) custom-call(s32[17]{0:T(128)S(1)} %pad_add_fusion.meta_ref, ...), custom_call_target="tpu_custom_call" | custom-call | flops 9600000000 | bytes 1048576 | tf_op jit(solution)/shard_map/pallas_call | solution.py:707
  52.2 1.6 %collective-permute-start.4 = (f32[2,128,128]{2,1,0:T(8,128)S(1)}, f32[2,128,128]{2,1,0:T(8,128)S(1)}, u32[]{:S(2)}, u32[]{:S(2)}) collective-permute-start(f32[2,128,128]{2,1,0:T(8,128)S(1)} %get-tuple-element.25.shift_ref), channel_id=1, source_target_pairs={{0,8},{8,16},{16,24},{24,0},{1,9},{9,17},{17,25},{25,1},{2,10},{10... | collective-permute-start | bytes 393224 | tf_op jit(solution)/shard_map/ppermute | solution.py:560
  53.8 6.1 %collective-permute-done.4.incoming_ref = f32[2,128,128]{2,1,0:T(8,128)S(1)} collective-permute-done((f32[2,128,128]{2,1,0:T(8,128)S(1)}, f32[2,128,128]{2,1,0:T(8,128)S(1)}, u32[]{:S(2)}, u32[]{:S(2)}) %collective-permute-start.4) | collective-permute-done | bytes 131104 | tf_op jit(solution)/shard_map/ppermute | solution.py:560
  59.9 0.2 shard_map.91
  60.1 0.1 collective-permute-start.5
  60.2 6.8 %collective-permute-done.5.incoming_ref = f32[2,128,128]{2,1,0:T(8,128)S(1)} collective-permute-done((f32[2,128,128]{2,1,0:T(8,128)S(1)}, f32[2,128,128]{2,1,0:T(8,128)S(1)}, u32[]{:S(2)}, u32[]{:S(2)}) %collective-permute-start.5) | collective-permute-done | bytes 131104 | tf_op jit(solution)/shard_map/ppermute | solution.py:560
  67.0 0.2 shard_map.92
  67.2 0.2 collective-permute-start.6
  67.4 0.0 copy-start
  67.4 9.6 %shard_map.86 = (f32[2,1024,256]{2,1,0:T(8,128)}, f32[2,1024,256]{2,1,0:T(8,128)}, f32[8,128,128]{2,1,0:T(8,128)}, f32[2,8,8,128]{3,2,1,0:T(8,128)S(1)}, f32[2,1...) custom-call(s32[17]{0:T(128)S(1)} %pad_add_fusion.meta_ref, bf16[8,400,128]{2,1,0:T(8,128)(2,1)S(1)} %all-to-all-done.2.recv_ref, ...), custom_call_target="tpu_custom_call" | custom-call | flops 9600000000 | bytes 1048576 | tf_op jit(solution)/shard_map/pallas_call | solution.py:707
  77.0 0.0 copy-start.1
  77.0 0.6 copy-done.1
  77.7 0.0 collective-permute-start.1
  77.7 0.0 collective-permute-done.6.incoming_ref
  77.7 0.0 all-to-all-done.outer_ref
  77.7 0.0 copy-done
  77.7 0.0 copy-start.2
  77.7 5.7 %shard_map.93 = bf16[8,256,128]{2,1,0:T(8,128)(2,1)} custom-call(s32[17]{0:T(128)S(1)} %pad_add_fusion.meta_ref, bf16[8,768,128]{2,1,0:T(8,128)(2,1)S(1)} %all-to-all-done.outer_ref, bf16[2,16,128]{2,1,0:T(8,128)(2,1)S(1)} %slice.12.tail_ref, f32[1,4,128]{2,1,0:T(4,128)S(1)} %get-tuple-element.32.weight_ref, ...), custom_call_target="tpu_custom_call" | custom-call | flops 1500000000 | bytes 1048576 | tf_op jit(solution)/shard_map/pallas_call | solution.py:752
  83.4 3.8 %all-to-all-start.4 = ((bf16[8,256,128]{2,1,0:T(8,128)(2,1)}), bf16[8,256,128]{2,1,0:T(8,128)(2,1)S(1)}, u32[]{:S(2)}, u32[]{:S(2)}) async-start(bf16[8,256,128]{2,1,0:T(8,128)(2,1)} %shard_map.93), calls=%async_computation.4 | async-start | bytes 1048576 | tf_op jit(solution)/shard_map/all_to_all | solution.py:564
  87.2 0.0 collective-permute-done.1.incoming_ref
  87.2 0.0 copy-done.2
  87.2 0.2 shard_map.87
  87.4 1.1 collective-permute-start.2
  88.5 6.9 %collective-permute-done.2.incoming_ref = f32[2,128,128]{2,1,0:T(8,128)S(1)} collective-permute-done((f32[2,128,128]{2,1,0:T(8,128)S(1)}, f32[2,128,128]{2,1,0:T(8,128)S(1)}, u32[]{:S(2)}, u32[]{:S(2)}) %collective-permute-start.2) | collective-permute-done | bytes 131104 | tf_op jit(solution)/shard_map/ppermute | solution.py:560
  95.4 0.2 shard_map.88
  95.6 0.4 collective-permute-start.3
  96.1 6.8 %collective-permute-done.3.incoming_ref = f32[2,128,128]{2,1,0:T(8,128)S(1)} collective-permute-done((f32[2,128,128]{2,1,0:T(8,128)S(1)}, f32[2,128,128]{2,1,0:T(8,128)S(1)}, u32[]{:S(2)}, u32[]{:S(2)}) %collective-permute-start.3) | collective-permute-done | bytes 131104 | tf_op jit(solution)/shard_map/ppermute | solution.py:560
  102.8 5.7 %shard_map.89 = bf16[8,256,128]{2,1,0:T(8,128)(2,1)} custom-call(s32[17]{0:T(128)S(1)} %pad_add_fusion.meta_ref, bf16[8,768,128]{2,1,0:T(8,128)(2,1)S(1)} %all-to-all-done.outer_ref, bf16[2,16,128]{2,1,0:T(8,128)(2,1)S(1)} %slice.12.tail_ref, f32[1,4,128]{2,1,0:T(4,128)S(1)} %get-tuple-element.34.weight_ref, ...), custom_call_target="tpu_custom_call" | custom-call | flops 1500000000 | bytes 1048576 | tf_op jit(solution)/shard_map/pallas_call | solution.py:752
  108.5 0.0 all-to-all-done.4.refs_0_
  108.5 3.5 %all-to-all-start.3 = ((bf16[8,256,128]{2,1,0:T(8,128)(2,1)}), bf16[8,256,128]{2,1,0:T(8,128)(2,1)S(1)}, u32[]{:S(2)}, u32[]{:S(2)}) async-start(bf16[8,256,128]{2,1,0:T(8,128)(2,1)} %shard_map.89), calls=%async_computation.3 | async-start | bytes 1048576 | tf_op jit(solution)/shard_map/all_to_all | solution.py:564
  112.0 0.9 shard_map.94.refs_1_
  112.9 8.7 %all-to-all-done.3.refs_0_ = bf16[8,256,128]{2,1,0:T(8,128)(2,1)S(1)} async-done(((bf16[8,256,128]{2,1,0:T(8,128)(2,1)}), bf16[8,256,128]{2,1,0:T(8,128)(2,1)S(1)}, u32[]{:S(2)}, u32[]{:S(2)}) %all-to-all-start.3) | async-done | bytes 524320 | tf_op jit(solution)/shard_map/all_to_all | solution.py:564
  121.7 0.9 shard_map.95
  (6 shorter events, 0.0 us)
Async XLA Ops:
  0.0 7.8 %copy-start.5 = (s32[1,16]{1,0:T(1,128)S(1)}, s32[1,16]{1,0:T(1,128)}, u32[]{:S(2)}) copy-start(s32[1,16]{1,0:T(1,128)} %param.11) | copy-start | bytes 196
  2.6 8.8 %copy-start.3 = (f32[32]{0:T(128)S(1)}, f32[32]{0:T(128)}, u32[]{:S(2)}) copy-start(f32[32]{0:T(128)} %param.14) | copy-start | bytes 388
  2.6 8.8 %copy-start.4 = (f32[32]{0:T(128)S(1)}, f32[32]{0:T(128)}, u32[]{:S(2)}) copy-start(f32[32]{0:T(128)} %param.13) | copy-start | bytes 388
  2.6 19.9 %all-to-all-start.1 = ((bf16[8,480,128]{2,1,0:T(8,128)(2,1)}), bf16[8,480,128]{2,1,0:T(8,128)(2,1)S(1)}, u32[]{:S(2)}, u32[]{:S(2)}) async-start(bf16[8,480,128]{2,1,0:T(8,128)(2,1)} %shard_map.83), calls=%async_computation.1 | async-start | bytes 1966080 | tf_op jit(solution)/shard_map/all_to_all | solution.py:564
  22.5 16.4 %all-to-all-start.2 = ((bf16[8,400,128]{2,1,0:T(8,128)(2,1)}), bf16[8,400,128]{2,1,0:T(8,128)(2,1)S(1)}, u32[]{:S(2)}, u32[]{:S(2)}) async-start(bf16[8,400,128]{2,1,0:T(8,128)(2,1)} %shard_map.85), calls=%async_computation.2 | async-start | bytes 1638400 | tf_op jit(solution)/shard_map/all_to_all | solution.py:564
  28.3 5.8 %collective-permute-start = (bf16[8,16,128]{2,1,0:T(8,128)(2,1)S(1)}, bf16[8,16,128]{2,1,0:T(8,128)(2,1)S(1)}, u32[]{:S(2)}, u32[]{:S(2)}) collective-permute-start(bf16[8,16,128]{2,1,0:T(8,128)(2,1)S(1)} %shard_map.84), channel_id=1, source_target_pairs={{0,8},{8,16},{16,24},{24,0},{1,9},{9,17},{17,25},{25,1},{2,10},{10... | collective-permute-start | bytes 98312 | tf_op jit(solution)/shard_map/ppermute | solution.py:560
  38.9 38.8 %all-to-all-start = ((bf16[8,768,128]{2,1,0:T(8,128)(2,1)}), bf16[8,768,128]{2,1,0:T(8,128)(2,1)S(1)}, u32[]{:S(2)}, u32[]{:S(2)}) async-start(bf16[8,768,128]{2,1,0:T(8,128)(2,1)} %shard_map.82), calls=%async_computation | async-start | bytes 3145728 | tf_op jit(solution)/shard_map/all_to_all | solution.py:564
  52.2 7.7 %collective-permute-start.4 = (f32[2,128,128]{2,1,0:T(8,128)S(1)}, f32[2,128,128]{2,1,0:T(8,128)S(1)}, u32[]{:S(2)}, u32[]{:S(2)}) collective-permute-start(f32[2,128,128]{2,1,0:T(8,128)S(1)} %get-tuple-element.25.shift_ref), channel_id=1, source_target_pairs={{0,8},{8,16},{16,24},{24,0},{1,9},{9,17},{17,25},{25,1},{2,10},{10... | collective-permute-start | bytes 393224 | tf_op jit(solution)/shard_map/ppermute | solution.py:560
  60.1 6.9 %collective-permute-start.5 = (f32[2,128,128]{2,1,0:T(8,128)S(1)}, f32[2,128,128]{2,1,0:T(8,128)S(1)}, u32[]{:S(2)}, u32[]{:S(2)}) collective-permute-start(f32[2,128,128]{2,1,0:T(8,128)S(1)} %shard_map.91), channel_id=1, source_target_pairs={{0,8},{8,16},{16,24},{24,0},{1,9},{9,17},{17,25},{25,1},{2,10},{10... | collective-permute-start | bytes 393224 | tf_op jit(solution)/shard_map/ppermute | solution.py:560
  67.2 10.5 %collective-permute-start.6 = (f32[2,128,128]{2,1,0:T(8,128)S(1)}, f32[2,128,128]{2,1,0:T(8,128)S(1)}, u32[]{:S(2)}, u32[]{:S(2)}) collective-permute-start(f32[2,128,128]{2,1,0:T(8,128)S(1)} %shard_map.92), channel_id=1, source_target_pairs={{0,8},{8,16},{16,24},{24,0},{1,9},{9,17},{17,25},{25,1},{2,10},{10... | collective-permute-start | bytes 393224 | tf_op jit(solution)/shard_map/ppermute | solution.py:560
  67.4 10.3 %copy-start = (f32[128]{0:T(128)S(1)}, f32[128]{0:T(128)}, u32[]{:S(2)}) copy-start(f32[128]{0:T(128)} %param.15) | copy-start | bytes 1540
  77.0 0.7 copy-start.1
  77.7 9.5 %collective-permute-start.1 = (f32[2,128,128]{2,1,0:T(8,128)S(1)}, f32[2,128,128]{2,1,0:T(8,128)S(1)}, u32[]{:S(2)}, u32[]{:S(2)}) collective-permute-start(f32[2,128,128]{2,1,0:T(8,128)S(1)} %get-tuple-element.19.shift_ref), channel_id=1, source_target_pairs={{0,8},{8,16},{16,24},{24,0},{1,9},{9,17},{17,25},{25,1},{2,10},{10... | collective-permute-start | bytes 393224 | tf_op jit(solution)/shard_map/ppermute | solution.py:560
  77.7 9.5 %copy-start.2 = (bf16[2,128,256]{2,1,0:T(8,128)(2,1)S(1)}, bf16[2,128,256]{2,1,0:T(8,128)(2,1)}, u32[]{:S(2)}) copy-start(bf16[2,128,256]{2,1,0:T(8,128)(2,1)} %copy-done.1) | copy-start | bytes 393220
  83.4 25.1 %all-to-all-start.4 = ((bf16[8,256,128]{2,1,0:T(8,128)(2,1)}), bf16[8,256,128]{2,1,0:T(8,128)(2,1)S(1)}, u32[]{:S(2)}, u32[]{:S(2)}) async-start(bf16[8,256,128]{2,1,0:T(8,128)(2,1)} %shard_map.93), calls=%async_computation.4 | async-start | bytes 1048576 | tf_op jit(solution)/shard_map/all_to_all | solution.py:564
  87.4 8.0 %collective-permute-start.2 = (f32[2,128,128]{2,1,0:T(8,128)S(1)}, f32[2,128,128]{2,1,0:T(8,128)S(1)}, u32[]{:S(2)}, u32[]{:S(2)}) collective-permute-start(f32[2,128,128]{2,1,0:T(8,128)S(1)} %shard_map.87), channel_id=1, source_target_pairs={{0,8},{8,16},{16,24},{24,0},{1,9},{9,17},{17,25},{25,1},{2,10},{10... | collective-permute-start | bytes 393224 | tf_op jit(solution)/shard_map/ppermute | solution.py:560
  95.6 7.2 %collective-permute-start.3 = (f32[2,128,128]{2,1,0:T(8,128)S(1)}, f32[2,128,128]{2,1,0:T(8,128)S(1)}, u32[]{:S(2)}, u32[]{:S(2)}) collective-permute-start(f32[2,128,128]{2,1,0:T(8,128)S(1)} %shard_map.88), channel_id=1, source_target_pairs={{0,8},{8,16},{16,24},{24,0},{1,9},{9,17},{17,25},{25,1},{2,10},{10... | collective-permute-start | bytes 393224 | tf_op jit(solution)/shard_map/ppermute | solution.py:560
  108.5 13.2 %all-to-all-start.3 = ((bf16[8,256,128]{2,1,0:T(8,128)(2,1)}), bf16[8,256,128]{2,1,0:T(8,128)(2,1)S(1)}, u32[]{:S(2)}, u32[]{:S(2)}) async-start(bf16[8,256,128]{2,1,0:T(8,128)(2,1)} %shard_map.89), calls=%async_computation.3 | async-start | bytes 1048576 | tf_op jit(solution)/shard_map/all_to_all | solution.py:564
